TPU v7x, 256 devices: a whole 4x4x8 slice. The times are simulated.
256 devices in a mesh: sp: 64 (over z, y, core), tp: 4 (over x).
Axes of the slice: x: 4, y: 4, z: 8, core: 2. Of those that a mesh axis runs over, the one named last changes fastest.
Arguments:
- decay_rate: float32 [4, 65536, 1024], P(None, 'sp', 'tp'), may hold values from 0.2 to 2
- drive_in: bfloat16 [4, 65536, 1024], P(None, 'sp', 'tp'), may hold values from -6 to 6
- gate_in: bfloat16 [4, 65536, 1024], P(None, 'sp', 'tp'), may hold values from -6 to 6
- norm_gain: float32 [1024], P('tp'), may hold values from 0.25 to 1.75
Outputs:
- filtered: bfloat16 [4, 65536, 1024], P(None, 'sp', 'tp')
All inputs are finite; a program needn't handle non-finite values.
Results may differ from a plain program's by a relative error of at most 0.0015.
Values sent between devices are 32-bit elements.
No kernel may reach another device: no remote copies, remote signals or barrier semaphores. Data moves between devices by JAX's collectives and lax.ppermute only.
A program may use at most 128 MiB of HBM per device.

v0:
```python
import jax
import jax.numpy as jnp
from jax import lax
from jax.sharding import Mesh
from jax.sharding import PartitionSpec as P

SP = ("sp_0", "sp_1", "sp_2")


def neutral_like(array, identity):
    return jax.tree.map(
        lambda a, e: jnp.broadcast_to(jnp.asarray(e, a.dtype), a.shape), array, identity
    )


def carried_in(array, axes, combine, identity):
    before = start = neutral_like(array, identity)
    so_far = array
    for axis in reversed(axes):
        peers, place = (lax.axis_size(axis), lax.axis_index(axis))
        pieces = jax.tree.map(lambda part: lax.all_gather(part, axis), so_far)
        inside, so_far = (start, start)
        for k in range(peers):
            passed = k < place
            so_far = combine(so_far, jax.tree.map(lambda part: part[k], pieces))
            inside = jax.tree.map(lambda new, old: jnp.where(passed, new, old), so_far, inside)
        before = combine(inside, before)
    return before


def over_pieces(array, axis):
    return lax.all_gather(array, axis).sum(0)


def join_pair(earlier, later):
    return (earlier[0] * later[0], later[0] * earlier[1] + later[1])


def shards(decay_rate, drive_in, gate_in, norm_gain):
    total_length = decay_rate.shape[1] * lax.axis_size(SP)
    keep = jnp.exp(-decay_rate / total_length)
    push = drive_in.astype(jnp.float32) * total_length ** (-0.5)
    steps = -decay_rate / total_length
    logs = jnp.sum(steps, axis=1, keepdims=True) - jnp.cumsum(steps, axis=1)
    summary = (jnp.exp(jnp.sum(steps, axis=1)), jnp.sum(jnp.exp(logs) * push, axis=1))
    entering_forward = carried_in(
        summary, SP, join_pair, (jnp.ones_like(keep[:, 0]), jnp.zeros_like(push[:, 0]))
    )
    started = push.at[:, 0].add(keep[:, 0] * entering_forward[1])
    forward = lax.associative_scan(join_pair, (keep, started), axis=1)[1]
    gated = forward * jax.nn.sigmoid(gate_in.astype(jnp.float32))
    power = over_pieces(jnp.sum(gated * gated, axis=-1, keepdims=True), "tp") / (
        gated.shape[-1] * lax.axis_size("tp")
    )
    filtered = (gated * lax.rsqrt(power + 1e-06) * norm_gain).astype(jnp.bfloat16)
    return filtered


def solution(mesh):
    torus = Mesh(mesh.devices.reshape(8, 4, 2, mesh.shape["tp"]), ("sp_0", "sp_1", "sp_2", "tp"))
    in_specs = (P(None, SP, "tp"), P(None, SP, "tp"), P(None, SP, "tp"), P("tp"))
    out_specs = P(None, SP, "tp")
    return jax.shard_map(
        shards, mesh=torus, in_specs=in_specs, out_specs=out_specs, check_vma=False
    )
```

profile of v0, /device:TPU:2, one launch (start us, length us, event | category | flops | bytes accessed | tf_op | source)
XLA Modules:
  0.0 278.8 jit_solution(14980261275409801767)
XLA Ops:
  0.0 4.9 %fusion.22 = (f32[4,256]{1,0:T(4,128)S(1)}, f32[4,1024,256]{2,1,0:T(8,128)}, f32[4,1024,256]{2,1,0:T(8,128)S(1)}) fusion(f32[4,1024,256]{2,1,0:T(8,128)} %param.6), kind=kLoop, calls=%fused_computation.120 | loop fusion | flops 3144704 | bytes 12587008 | tf_op jit(solution)/shard_map/reduce_sum | solution.py:45
  4.9 2.6 fusion.2
  7.5 1.8 all-gather.3
  9.3 0.1 copy-done.2
  9.5 2.6 broadcast_add_fusion
  12.1 1.3 copy.25
  13.4 0.3 copy-done.5
  13.7 1.3 fusion
  15.0 1.8 all-gather.4
  16.9 12.5 %all_gather.34 = f32[4,4,256]{2,1,0:T(4,128)S(1)} all-gather(f32[1,4,256]{2,1,0:T(4,128)S(1)} %copy.28), channel_id=1, replica_groups=mesh['sp_0'=8,'sp_1'=4,'sp_2'=2,'tp'=4] {'sp_1'}, dimensions={0}, use_global_device_ids=true | all-gather | bytes 20480 | tf_op jit(solution)/shard_map/all_gather | solution.py:21
  29.4 12.0 %all_gather.30 = f32[4,4,256]{2,1,0:T(4,128)S(1)} all-gather(f32[1,4,256]{2,1,0:T(4,128)S(1)} %copy.10), channel_id=1, replica_groups=mesh['sp_0'=8,'sp_1'=4,'sp_2'=2,'tp'=4] {'sp_1'}, dimensions={0}, use_global_device_ids=true | all-gather | bytes 20480 | tf_op jit(solution)/shard_map/all_gather | solution.py:21
  41.5 28.3 %all_gather.35 = f32[8,4,256]{2,1,0:T(4,128)S(1)} all-gather(f32[1,4,256]{2,1,0:T(4,128)S(1)} %copy.33), channel_id=1, replica_groups=mesh['sp_0'=8,'sp_1'=4,'sp_2'=2,'tp'=4] {'sp_0'}, dimensions={0}, use_global_device_ids=true | all-gather | bytes 36864 | tf_op jit(solution)/shard_map/all_gather | solution.py:21
  69.8 24.8 %all_gather.31 = f32[8,4,256]{2,1,0:T(4,128)S(1)} all-gather(f32[1,4,256]{2,1,0:T(4,128)S(1)} %copy.15), channel_id=1, replica_groups=mesh['sp_0'=8,'sp_1'=4,'sp_2'=2,'tp'=4] {'sp_0'}, dimensions={0}, use_global_device_ids=true | all-gather | bytes 36864 | tf_op jit(solution)/shard_map/all_gather | solution.py:21
  94.6 0.9 fusion.20
  95.5 1.4 scatter-add.4
  96.9 11.9 %slice.449 = f32[4,511,256]{2,1,0:T(8,128)} slice(f32[4,1024,256]{2,1,0:T(8,128)} %scatter-add.4), slice={[0:4:1], [2:1024:2], [0:256:1]} | slice | bytes 4186112 | tf_op jit(solution)/shard_map/slice | solution.py:50
  108.8 11.8 %slice.379 = f32[4,512,256]{2,1,0:T(8,128)} slice(f32[4,1024,256]{2,1,0:T(8,128)} %scatter-add.4), slice={[0:4:1], [1:1024:2], [0:256:1]} | slice | bytes 4194304 | tf_op jit(solution)/shard_map/slice | solution.py:50
  120.6 11.8 %slice.378 = f32[4,512,256]{2,1,0:T(8,128)} slice(f32[4,1024,256]{2,1,0:T(8,128)} %scatter-add.4), slice={[0:4:1], [0:1023:2], [0:256:1]} | slice | bytes 4194304 | tf_op jit(solution)/shard_map/slice | solution.py:50
  132.4 11.8 %slice.381 = f32[4,512,256]{2,1,0:T(8,128)} slice(f32[4,1024,256]{2,1,0:T(8,128)} %get-tuple-element.20), slice={[0:4:1], [0:1023:2], [0:256:1]} | slice | bytes 4194304 | tf_op jit(solution)/shard_map/slice | solution.py:50
  144.1 11.8 %slice.377 = f32[4,512,256]{2,1,0:T(8,128)} slice(f32[4,1024,256]{2,1,0:T(8,128)} %get-tuple-element.20), slice={[0:4:1], [1:1024:2], [0:256:1]} | slice | bytes 4194304 | tf_op jit(solution)/shard_map/slice | solution.py:50
  155.9 5.4 %fusion.24 = (f32[4,512,256]{2,1,0:T(8,128)}, f32[4,512,256]{2,1,0:T(8,128)S(1)}) fusion(f32[4,512,256]{2,1,0:T(8,128)} %slice.381, f32[4,512,256]{2,1,0:T(8,128)} %slice.377, f32[4,512,256]{2,1,0:T(8,128)} %slice.379, f32[4,512,256]{2,1,0:T(8,128)} %slice.378), kind=kLoop, calls=%fused_computation.122 | loop fusion | flops 1572864 | bytes 12582912 | tf_op jit(solution)/shard_map/mul | solution.py:36
  161.4 11.9 %slice.376 = f32[4,511,256]{2,1,0:T(8,128)} slice(f32[4,1024,256]{2,1,0:T(8,128)} %get-tuple-element.20), slice={[0:4:1], [2:1024:2], [0:256:1]} | slice | bytes 4186112 | tf_op jit(solution)/shard_map/slice | solution.py:50
  173.3 7.3 %slice.387 = f32[4,256,256]{2,1,0:T(8,128)} slice(f32[4,512,256]{2,1,0:T(8,128)} %get-tuple-element.22), slice={[0:4:1], [0:511:2], [0:256:1]} | slice | bytes 2097152 | tf_op jit(solution)/shard_map/slice | solution.py:50
  180.6 7.3 %slice.383 = f32[4,256,256]{2,1,0:T(8,128)} slice(f32[4,512,256]{2,1,0:T(8,128)} %get-tuple-element.22), slice={[0:4:1], [1:512:2], [0:256:1]} | slice | bytes 2097152 | tf_op jit(solution)/shard_map/slice | solution.py:50
  187.9 6.0 %slice.382 = f32[4,255,256]{2,1,0:T(8,128)S(1)} slice(f32[4,512,256]{2,1,0:T(8,128)} %get-tuple-element.22), slice={[0:4:1], [2:512:2], [0:256:1]} | slice | bytes 2088960 | tf_op jit(solution)/shard_map/slice | solution.py:50
  194.0 4.3 %slice.447 = f32[4,255,256]{2,1,0:T(8,128)} slice(f32[4,512,256]{2,1,0:T(8,128)S(1)} %get-tuple-element.23), slice={[0:4:1], [2:512:2], [0:256:1]} | slice | bytes 2088960 | tf_op jit(solution)/shard_map/slice | solution.py:50
  198.3 4.2 %slice.385 = f32[4,256,256]{2,1,0:T(8,128)} slice(f32[4,512,256]{2,1,0:T(8,128)S(1)} %get-tuple-element.23), slice={[0:4:1], [1:512:2], [0:256:1]} | slice | bytes 2097152 | tf_op jit(solution)/shard_map/slice | solution.py:50
  202.4 4.2 %slice.384 = f32[4,256,256]{2,1,0:T(8,128)} slice(f32[4,512,256]{2,1,0:T(8,128)S(1)} %get-tuple-element.23), slice={[0:4:1], [0:511:2], [0:256:1]} | slice | bytes 2097152 | tf_op jit(solution)/shard_map/slice | solution.py:50
  206.6 2.5 fusion.25
  209.1 1.5 slice.393
  210.6 1.5 slice.389
  212.1 1.6 slice.388
  213.7 0.4 slice.445
  214.0 0.3 slice.391
  214.3 1.5 slice.390
  215.8 1.5 fusion.26
  217.3 0.1 slice.399
  217.5 0.1 slice.395
  217.6 0.2 slice.394
  217.8 0.2 slice.443
  218.0 0.1 slice.397
  218.1 0.8 slice.396
  218.9 1.0 fusion.27
  221.8 0.1 pad.73
  221.8 0.1 pad.74
  222.1 0.1 pad.75
  222.2 0.1 pad.76
  222.4 0.1 fusion.6
  222.5 0.9 add.344
  223.5 0.2 pad.77
  223.7 2.0 pad.78
  225.7 1.5 fusion.5
  227.2 0.1 add.346
  227.4 1.1 pad_maximum_fusion.1
  228.5 2.3 pad.79
  230.8 3.3 %pad.80 = f32[4,512,256]{2,1,0:T(8,128)} pad(f32[4,256,256]{2,1,0:T(8,128)S(1)} %add.346, f32[]{:T(128)} %constant.61.clone.1), padding=0_0_0x1_0_1x0_0_0 | pad | bytes 3145732 | tf_op jit(solution)/shard_map/pad | solution.py:50
  234.1 3.5 %fusion.4 = f32[4,511,256]{2,1,0:T(8,128)S(1)} fusion(f32[4,511,256]{2,1,0:T(8,128)} %slice.449, f32[4,511,256]{2,1,0:T(8,128)} %slice.376, f32[4,512,256]{2,1,0:T(8,128)} %pad.80, f32[4,512,256]{2,1,0:T(8,128)S(1)} %pad.79), kind=kLoop, calls=%fused_computation.12 | loop fusion | flops 1569792 | bytes 10465280 | tf_op jit(solution)/shard_map/add | solution.py:36
  237.6 1.6 add.348
  239.2 1.5 pad_maximum_fusion
  240.7 9.4 %pad.81 = f32[4,1024,256]{2,1,0:T(8,128)} pad(f32[4,512,256]{2,1,0:T(8,128)} %pad_maximum_fusion, f32[]{:T(128)} %constant.61.clone.1), padding=0_0_0x0_1_1x0_0_0 | pad | bytes 6291460 | tf_op jit(solution)/shard_map/pad | solution.py:50
  250.1 5.9 %pad.82 = f32[4,1024,256]{2,1,0:T(8,128)} pad(f32[4,512,256]{2,1,0:T(8,128)S(1)} %copy-done.3, f32[]{:T(128)} %constant.61.clone.1), padding=0_0_0x1_0_1x0_0_0 | pad | bytes 6291460 | tf_op jit(solution)/shard_map/pad | solution.py:50
  256.0 7.3 %multiply_reduce_fusion = (f32[4,1024]{1,0:T(4,128)S(1)}, f32[4,1024,256]{2,1,0:T(8,128)}) fusion(bf16[4,1024,256]{2,1,0:T(8,128)(2,1)} %param.8, f32[4,1024,256]{2,1,0:T(8,128)} %pad.81, f32[4,1024,256]{2,1,0:T(8,128)} %pad.82), kind=kLoop, calls=%fused_computation.7 | loop fusion | flops 8384512 | bytes 14696448 | tf_op jit(solution)/shard_map/reduce_sum | solution.py:52
  263.3 11.9 %all-gather.5 = f32[4,4,1024]{2,1,0:T(4,128)S(1)} all-gather(f32[1,4,1024]{2,1,0:T(4,128)S(1)} %bitcast.132), channel_id=4, replica_groups=mesh['sp_0'=8,'sp_1'=4,'sp_2'=2,'tp'=4] {'tp'}, dimensions={0}, use_global_device_ids=true | all-gather | bytes 81920 | tf_op jit(solution)/shard_map/all_gather | solution.py:32
  275.2 3.6 %multiply_convert_fusion = bf16[4,1024,256]{2,1,0:T(8,128)(2,1)} fusion(f32[4,1024,256]{2,1,0:T(8,128)} %get-tuple-element.18, f32[256]{0:T(256)S(1)} %copy-done.6, f32[4,1024]{1,0:T(4,128)S(1)} %add_rsqrt_fusion), kind=kLoop, calls=%fused_computation.6 | loop fusion | flops 3145728 | bytes 6308864 | tf_op jit(solution)/shard_map/convert_element_type | solution.py:55
  (98 shorter events, 1.9 us)
Async XLA Ops:
  7.5 2.0 copy-start.2
  12.1 1.6 copy-start.5
  15.0 79.6 %copy-start = (f32[4,1024,256]{2,1,0:T(8,128)}, f32[4,1024,256]{2,1,0:T(8,128)S(1)}, u32[]{:S(2)}) copy-start(f32[4,1024,256]{2,1,0:T(8,128)S(1)} %get-tuple-element.25) | copy-start | bytes 12582916
  220.9 1.4 copy-start.4
  234.1 3.5 %copy-start.1 = (f32[4,512,256]{2,1,0:T(8,128)S(1)}, f32[4,512,256]{2,1,0:T(8,128)}, u32[]{:S(2)}) copy-start(f32[4,512,256]{2,1,0:T(8,128)} %pad.80) | copy-start | bytes 6291460
  240.7 9.4 %copy-start.3 = (f32[4,512,256]{2,1,0:T(8,128)S(1)}, f32[4,512,256]{2,1,0:T(8,128)}, u32[]{:S(2)}) copy-start(f32[4,512,256]{2,1,0:T(8,128)} %add.348) | copy-start | bytes 6291460
  256.0 19.2 %copy-start.6 = (f32[256]{0:T(256)S(1)}, f32[256]{0:T(256)}, u32[]{:S(2)}) copy-start(f32[256]{0:T(256)} %param.9) | copy-start | bytes 3076
where the time goes:
time: 282 us; the launch traced here: 279 us
  local copies, waits for them, and re-layouts  140 us (50%)
  blocking collectives  93.2 us (33%)
  other arithmetic  44.6 us (16%)
    slice x59, local copies, waits for them, and re-layouts, shards(): forward = lax.associative_scan(join_pair, (keep, started), axis=1)[1]  113 us
    all_gather x6, blocking collectives, carried_in(): pieces = jax.tree.map(lambda part: lax.all_gather(part, axis), so_far)  81.3 us
    pad x18, local copies, waits for them, and re-layouts, shards(): forward = lax.associative_scan(join_pair, (keep, started), axis=1)[1]  23.9 us
    all_gather x1, blocking collectives, over_pieces(): return lax.all_gather(array, axis).sum(0)  11.9 us
    mul x10, other arithmetic, join_pair(): return (earlier[0] * later[0], later[0] * earlier[1] + later[1])  10.6 us
    reduce_sum x1, other arithmetic, shards(): jnp.sum(gated * gated, axis=-1, keepdims=True)  7.26 us

commit v1 on v0

v1 whole, which is shorter than its diff:
```python
import functools

import jax
import jax.numpy as jnp
from jax import lax
from jax.experimental import pallas as pl
from jax.experimental.pallas import tpu as pltpu
from jax.sharding import Mesh
from jax.sharding import PartitionSpec as P

SP = ("sp_0", "sp_1", "sp_2")
BLOCK = 256
MIB = 1 << 20


def triangle():
    row = lax.broadcasted_iota(jnp.int32, (BLOCK, BLOCK), 0)
    col = lax.broadcasted_iota(jnp.int32, (BLOCK, BLOCK), 1)
    return (row >= col).astype(jnp.bfloat16)


def running_sum(tri, x):
    high = x.astype(jnp.bfloat16)
    low = (x - high.astype(jnp.float32)).astype(jnp.bfloat16)
    dot = functools.partial(jnp.dot, preferred_element_type=jnp.float32)
    return dot(tri, high) + dot(tri, low)


def pieces(hbm, vmem, sems):
    batch, length, _ = hbm.shape
    steps = length // BLOCK

    def piece(i):
        b, at = i // steps, pl.ds(pl.multiple_of((i % steps) * BLOCK, BLOCK), BLOCK)
        return pltpu.make_async_copy(hbm.at[b, at, :], vmem.at[b, at, :], sems.at[i])

    return piece


def summary_kernel(total, rate_hbm, drive_hbm, depth_ref, term_ref, out_ref, rate, drive, tri_ref, rate_sem, drive_sem):
    batch, length, channels = rate.shape
    steps = length // BLOCK
    rate_piece, drive_piece = pieces(rate_hbm, rate, rate_sem), pieces(drive_hbm, drive, drive_sem)
    for i in range(batch * steps):
        rate_piece(i).start()
        drive_piece(i).start()
    tri_ref[...] = triangle()
    for b in range(batch):
        depth_in = jnp.zeros((1, channels), jnp.float32)
        sums = jnp.zeros((8, channels), jnp.float32)
        for s in range(steps):
            at = pl.ds(s * BLOCK, BLOCK)
            rate_piece(b * steps + s).wait()
            depth = running_sum(tri_ref[...], rate[b, at, :]) * (1.0 / total) + depth_in
            depth_ref[b, at, :] = depth
            depth_in = depth[BLOCK - 1 :, :]
            drive_piece(b * steps + s).wait()
            term = jnp.exp(depth) * (drive[b, at, :].astype(jnp.float32) * total**-0.5)
            term_ref[b, at, :] = term
            sums = sums + jnp.sum(term.reshape(BLOCK // 8, 8, channels), axis=0)
        out_ref[b : b + 1, :] = depth_in
        out_ref[batch + b : batch + b + 1, :] = jnp.sum(sums, axis=0, keepdims=True)


def summarize(decay_rate, drive_in, total):
    batch, length, channels = decay_rate.shape
    count = batch * length // BLOCK
    big = jax.ShapeDtypeStruct(decay_rate.shape, jnp.float32)
    vmem = pl.BlockSpec(memory_space=pltpu.VMEM)
    return pl.pallas_call(
        functools.partial(summary_kernel, total),
        out_shape=(big, big, jax.ShapeDtypeStruct((2 * batch, channels), jnp.float32)),
        in_specs=[pl.BlockSpec(memory_space=pl.ANY)] * 2,
        out_specs=(vmem, vmem, vmem),
        scratch_shapes=[
            pltpu.VMEM(decay_rate.shape, jnp.float32),
            pltpu.VMEM(drive_in.shape, jnp.bfloat16),
            pltpu.VMEM((BLOCK, BLOCK), jnp.bfloat16),
            pltpu.SemaphoreType.DMA((count,)),
            pltpu.SemaphoreType.DMA((count,)),
        ],
        compiler_params=pltpu.CompilerParams(vmem_limit_bytes=24 * MIB),
        cost_estimate=pl.CostEstimate(flops=2_000_000_000, bytes_accessed=6 * MIB, transcendentals=MIB),
        name="summarize",
    )(decay_rate, drive_in)


def local_kernel(depth_ref, term_ref, gate_hbm, factor_ref, sum_ref, gate, tri_ref, gate_sem):
    batch, length, channels = gate.shape
    steps = length // BLOCK
    gate_piece = pieces(gate_hbm, gate, gate_sem)
    for i in range(batch * steps):
        gate_piece(i).start()
    tri_ref[...] = triangle()
    for b in range(batch):
        carried = jnp.zeros((1, channels), jnp.float32)
        for s in range(steps):
            at = pl.ds(s * BLOCK, BLOCK)
            sums = running_sum(tri_ref[...], term_ref[b, at, :]) + carried
            sum_ref[b, at, :] = sums
            carried = sums[BLOCK - 1 :, :]
            gate_piece(b * steps + s).wait()
            opened = 0.5 * jnp.tanh(0.5 * gate[b, at, :].astype(jnp.float32)) + 0.5
            factor_ref[b, at, :] = jnp.exp(-depth_ref[b, at, :]) * opened


def localize(depth, term, gate_in):
    batch, length, channels = depth.shape
    count = batch * length // BLOCK
    big = jax.ShapeDtypeStruct(depth.shape, jnp.float32)
    vmem = pl.BlockSpec(memory_space=pltpu.VMEM)
    return pl.pallas_call(
        local_kernel,
        out_shape=(big, big),
        in_specs=[vmem, vmem, pl.BlockSpec(memory_space=pl.ANY)],
        out_specs=(vmem, vmem),
        scratch_shapes=[
            pltpu.VMEM(gate_in.shape, jnp.bfloat16),
            pltpu.VMEM((BLOCK, BLOCK), jnp.bfloat16),
            pltpu.SemaphoreType.DMA((count,)),
        ],
        compiler_params=pltpu.CompilerParams(vmem_limit_bytes=24 * MIB),
        cost_estimate=pl.CostEstimate(flops=2_000_000_000, bytes_accessed=2 * MIB, transcendentals=2 * MIB),
        name="localize",
    )(depth, term, gate_in)


def gate_kernel(factor_ref, sum_ref, enter_ref, gated_ref, power_ref):
    batch, length, channels = factor_ref.shape
    lane = lax.broadcasted_iota(jnp.int32, (8, 128), 1)
    for b in range(batch):
        enter = enter_ref[b : b + 1, :]

        def step(j, power):
            at = pl.ds(pl.multiple_of(j * 64, 64), 64)
            gated = factor_ref[b, at, :] * (sum_ref[b, at, :] + enter)
            gated_ref[b, at, :] = gated
            square = gated * gated
            for k in range(8):
                sums = jnp.sum(square[8 * k : 8 * k + 8, :], axis=-1, keepdims=True)
                power = jnp.where(lane == j * 8 + k, sums, power)
            return power

        power_ref[b] = lax.fori_loop(0, length // 64, step, jnp.zeros((8, 128), jnp.float32))


def gate_and_square(factor, sums, enter):
    batch, length, channels = factor.shape
    vmem = pl.BlockSpec(memory_space=pltpu.VMEM)
    return pl.pallas_call(
        gate_kernel,
        out_shape=(jax.ShapeDtypeStruct(factor.shape, jnp.float32), jax.ShapeDtypeStruct((batch, 8, length // 8), jnp.float32)),
        in_specs=[vmem] * 3,
        out_specs=(vmem, vmem),
        compiler_params=pltpu.CompilerParams(vmem_limit_bytes=16 * MIB),
        cost_estimate=pl.CostEstimate(flops=8_000_000, bytes_accessed=12 * MIB, transcendentals=0),
        name="gate_and_square",
    )(factor, sums, enter)


def scale_kernel(width, gated_ref, p0_ref, p1_ref, p2_ref, p3_ref, gain_ref, out_ref):
    batch, length, channels = gated_ref.shape
    gain = gain_ref[...]
    for b in range(batch):
        power = (p0_ref[b] + p1_ref[b]) + (p2_ref[b] + p3_ref[b])
        scale = lax.rsqrt(power * (1.0 / width) + 1e-06)
        for j in range(length // 16):
            at = pl.ds(j * 16, 16)
            rows = jnp.concatenate(
                [jnp.broadcast_to(scale[:, 2 * j + k : 2 * j + k + 1], (8, channels)) for k in range(2)], axis=0
            )
            out_ref[b, at, :] = (gated_ref[b, at, :] * rows * gain).astype(jnp.bfloat16)


def scale(gated, powers, gain, width):
    batch, length, channels = gated.shape
    vmem = pl.BlockSpec(memory_space=pltpu.VMEM)
    return pl.pallas_call(
        functools.partial(scale_kernel, width),
        out_shape=jax.ShapeDtypeStruct(gated.shape, jnp.bfloat16),
        in_specs=[vmem] * 6,
        out_specs=vmem,
        compiler_params=pltpu.CompilerParams(vmem_limit_bytes=16 * MIB),
        cost_estimate=pl.CostEstimate(flops=8_000_000, bytes_accessed=6 * MIB, transcendentals=0),
        name="scale",
    )(gated, *powers, gain.reshape(1, channels))


def join(earlier, later):
    return (earlier[0] + later[0], earlier[1] + jnp.exp(earlier[0]) * later[1])


def split(pair):
    half = pair.shape[0] // 2
    return (pair[:half], pair[half:])


def masked(pair, keep):
    return jnp.where(keep, pair, 0.0)


def entering_state(pair, ways):
    chips_z, chips_y = ways
    core, y = lax.axis_index("sp_2"), lax.axis_index("sp_1")
    first = lax.ppermute(pair, "sp_2", [(0, 1)])
    chip = jnp.concatenate(join(split(first), split(pair)))
    def on_second(axis_pairs):
        return [(2 * a + 1, 2 * b + 1) for a, b in axis_pairs]

    near = {
        k: lax.ppermute(chip, ("sp_1", "sp_2"), on_second([(i, (i + k) % chips_y) for i in range(chips_y)]))
        for k in (2, 3, 1)
    }
    before = split(masked(near[chips_y - 1], y >= chips_y - 1))
    after = split(masked(near[chips_y - 1], y < chips_y - 1))
    for k in range(chips_y - 2, 0, -1):
        before = join(before, split(masked(near[k], y >= k)))
        after = join(after, split(masked(near[k], y < k)))
    plane = jnp.concatenate(join(join(before, split(chip)), after))
    stride = 2 * chips_y
    others = [(c * 2 + 1) for c in range(chips_y)]
    far = {
        k: lax.ppermute(
            plane,
            SP,
            [(i * stride + c, (i + k) * stride + c) for i in range(chips_z - k) for c in others],
        )
        for k in range(chips_z - 1, 0, -1)
    }
    so_far = split(far[chips_z - 1])
    for k in range(chips_z - 2, 0, -1):
        so_far = join(so_far, split(far[k]))
    so_far = join(so_far, before)
    enter = so_far[1] * jnp.exp(-so_far[0])
    own = jnp.exp(-split(first)[0]) * (enter + split(first)[1])
    back = lax.ppermute(enter, "sp_2", [(1, 0)])
    return jnp.where(core == 1, own, back)


def shards(ways, decay_rate, drive_in, gate_in, norm_gain):
    total = decay_rate.shape[1] * lax.axis_size(SP)
    parts = lax.axis_size("tp")
    width = decay_rate.shape[2] * parts
    depth, term, pair = summarize(decay_rate, drive_in, total)
    factor, sums = localize(depth, term, gate_in)
    enter = entering_state(pair, ways)
    gated, power = gate_and_square(factor, sums, enter)
    powers = [power] + [
        lax.ppermute(power, "tp", [(i, (i + k) % parts) for i in range(parts)]) for k in (2, 1, 3)
    ]
    return scale(gated, powers, norm_gain, width)


def solution(mesh):
    torus = Mesh(mesh.devices.reshape(8, 4, 2, mesh.shape["tp"]), ("sp_0", "sp_1", "sp_2", "tp"))
    in_specs = (P(None, SP, "tp"), P(None, SP, "tp"), P(None, SP, "tp"), P("tp"))
    out_specs = P(None, SP, "tp")
    return jax.shard_map(
        functools.partial(shards, (8, 4)), mesh=torus, in_specs=in_specs, out_specs=out_specs, check_vma=False
    )
```

time: 282 us -> 91.2 us (0.32)
  the two profiles are of different devices: /device:TPU:2 before, /device:TPU:1 now
where the time goes in v1:
time: 91.2 us; the launch traced here: 90.7 us
  starting transfers between devices  35.3 us (39%)
  Pallas kernels  25.7 us (28%)
  local copies, waits for them, and re-layouts  20.6 us (23%)
  waiting for transfers between devices  8.69 us (10%)
    unnamed x24, local copies, waits for them, and re-layouts  20.6 us
    ppermute x7, starting transfers between devices, entering_state(): lax.ppermute(plane, SP, [(i * stride + c, (i + k) * stride + c) for i in...  19.1 us
    pallas_call x1, Pallas kernels, summarize(): pl.pallas_call(functools.partial(summary_kernel, total), out_shape=(big,...  8.94 us
    pallas_call x1, Pallas kernels, localize(): pl.pallas_call(local_kernel, out_shape=(big, big), in_specs=[vmem, vmem,...  8.77 us
    ppermute x3, starting transfers between devices, entering_state(): lax.ppermute(chip, ('sp_1', 'sp_2'), on_second([(i, (i + k) % chips_y) fo...  8.24 us
    pallas_call x1, Pallas kernels, gate_and_square(): pl.pallas_call(gate_kernel, out_shape=(jax.ShapeDtypeStruct(factor.shape,...  5.69 us
    ppermute x3, starting transfers between devices, shards(): lax.ppermute(power, 'tp', [(i, (i + k) % parts) for i in range(parts)])  5.44 us
    ppermute x1, waiting for transfers between devices, entering_state(): first = lax.ppermute(pair, 'sp_2', [(0, 1)])  3.84 us
  transfers between devices with their start and end apart: 15, of which 5 were waited for; matrix products, arithmetic and copies ran while one was open for 0% of the time, Pallas kernels for 10%

profile of v1, /device:TPU:1, one launch (start us, length us, event | category | flops | bytes accessed | tf_op | source)
XLA Modules:
  0.0 90.7 jit_solution(15397465949772612943)
XLA Ops:
  0.0 0.0 copy-start.8
  0.0 0.0 copy-start.10
  0.0 2.3 %copy-done.10 = f32[4,1024,256]{2,1,0:T(8,128)S(1)} copy-done((f32[4,1024,256]{2,1,0:T(8,128)S(1)}, f32[4,1024,256]{2,1,0:T(8,128)}, u32[]{:S(2)}) %copy-start.10) | copy-done | bytes 4194328
  2.3 0.0 copy-start.11
  2.3 1.6 %copy-done.11 = bf16[4,1024,256]{2,1,0:T(8,128)(2,1)S(1)} copy-done((bf16[4,1024,256]{2,1,0:T(8,128)(2,1)S(1)}, bf16[4,1024,256]{2,1,0:T(8,128)(2,1)}, u32[]{:S(2)}) %copy-start.11) | copy-done | bytes 2097176
  3.9 8.9 %summarize.1 = (f32[4,1024,256]{2,1,0:T(8,128)S(1)}, f32[4,1024,256]{2,1,0:T(8,128)S(1)}, f32[8,256]{1,0:T(8,128)S(1)}) custom-call(f32[4,1024,256]{2,1,0:T(8,128)S(1)} %copy-done.10, bf16[4,1024,256]{2,1,0:T(8,128)(2,1)S(1)} %copy-done.11), custom_call_target="tpu_custom_call" | custom-call | flops 2000000000 | bytes 6291456 | tf_op jit(solution)/shard_map/summarize/pallas_call | solution.py:70
  12.9 0.0 copy-start
  12.9 2.0 %copy-done = f32[4,1024,256]{2,1,0:T(8,128)} copy-done((f32[4,1024,256]{2,1,0:T(8,128)}, f32[4,1024,256]{2,1,0:T(8,128)S(1)}, u32[]{:S(2)}) %copy-start) | copy-done | bytes 4194328
  14.8 0.0 copy-start.2
  14.9 2.0 %copy-done.2 = f32[4,1024,256]{2,1,0:T(8,128)} copy-done((f32[4,1024,256]{2,1,0:T(8,128)}, f32[4,1024,256]{2,1,0:T(8,128)S(1)}, u32[]{:S(2)}) %copy-start.2) | copy-done | bytes 4194328
  16.9 1.3 %collective-permute-start = (f32[8,256]{1,0:T(8,128)S(1)}, f32[8,256]{1,0:T(8,128)S(1)}, u32[]{:S(2)}, u32[]{:S(2)}) collective-permute-start(f32[8,256]{1,0:T(8,128)S(1)} %get-tuple-element.16), channel_id=1, source_target_pairs={{0,4},{1,5},{2,6},{3,7},{8,12},{9,13},{10,14},{11,15},{16,20},{17,... | collective-permute-start | bytes 24584 | tf_op jit(solution)/shard_map/ppermute | solution.py:205
  18.2 3.8 %collective-permute-done = f32[8,256]{1,0:T(8,128)S(1)} collective-permute-done((f32[8,256]{1,0:T(8,128)S(1)}, f32[8,256]{1,0:T(8,128)S(1)}, u32[]{:S(2)}, u32[]{:S(2)}) %collective-permute-start) | collective-permute-done | bytes 8224 | tf_op jit(solution)/shard_map/ppermute | solution.py:205
  22.0 3.4 %collective-permute-start.1 = (f32[8,256]{1,0:T(8,128)S(1)}, f32[8,256]{1,0:T(8,128)S(1)}, u32[]{:S(2)}, u32[]{:S(2)}) collective-permute-start(f32[8,256]{1,0:T(8,128)S(1)} %pad_maximum_fusion), channel_id=1, source_target_pairs={{4,28},{12,4},{20,12},{28,20},{5,29},{13,5},{21,13},{29,21},{6,30}... | collective-permute-start | bytes 24584 | tf_op jit(solution)/shard_map/ppermute | solution.py:211
  25.4 2.3 %collective-permute-start.2 = (f32[8,256]{1,0:T(8,128)S(1)}, f32[8,256]{1,0:T(8,128)S(1)}, u32[]{:S(2)}, u32[]{:S(2)}) collective-permute-start(f32[8,256]{1,0:T(8,128)S(1)} %pad_maximum_fusion), channel_id=1, source_target_pairs={{4,20},{12,28},{20,4},{28,12},{5,21},{13,29},{21,5},{29,13},{6,22}... | collective-permute-start | bytes 24584 | tf_op jit(solution)/shard_map/ppermute | solution.py:211
  27.7 2.6 %collective-permute-start.3 = (f32[8,256]{1,0:T(8,128)S(1)}, f32[8,256]{1,0:T(8,128)S(1)}, u32[]{:S(2)}, u32[]{:S(2)}) collective-permute-start(f32[8,256]{1,0:T(8,128)S(1)} %pad_maximum_fusion), channel_id=1, source_target_pairs={{4,12},{12,20},{20,28},{28,4},{5,13},{13,21},{21,29},{29,5},{6,14}... | collective-permute-start | bytes 24584 | tf_op jit(solution)/shard_map/ppermute | solution.py:211
  30.3 0.0 collective-permute-done.1
  30.3 1.0 %collective-permute-done.2 = f32[8,256]{1,0:T(8,128)S(1)} collective-permute-done((f32[8,256]{1,0:T(8,128)S(1)}, f32[8,256]{1,0:T(8,128)S(1)}, u32[]{:S(2)}, u32[]{:S(2)}) %collective-permute-start.2) | collective-permute-done | bytes 8224 | tf_op jit(solution)/shard_map/ppermute | solution.py:211
  31.3 2.0 %collective-permute-done.3 = f32[8,256]{1,0:T(8,128)S(1)} collective-permute-done((f32[8,256]{1,0:T(8,128)S(1)}, f32[8,256]{1,0:T(8,128)S(1)}, u32[]{:S(2)}, u32[]{:S(2)}) %collective-permute-start.3) | collective-permute-done | bytes 8224 | tf_op jit(solution)/shard_map/ppermute | solution.py:211
  33.4 3.5 %collective-permute-start.10 = (f32[8,256]{1,0:T(8,128)S(1)}, f32[8,256]{1,0:T(8,128)S(1)}, u32[]{:S(2)}, u32[]{:S(2)}) collective-permute-start(f32[8,256]{1,0:T(8,128)S(1)} %pad_maximum_fusion.1), channel_id=1, source_target_pairs={{4,36},{12,44},{20,52},{28,60},{36,68},{44,76},{52,84},{60,92},{68... | collective-permute-start | bytes 24584 | tf_op jit(solution)/shard_map/ppermute | solution.py:223
  36.9 5.2 %collective-permute-start.4 = (f32[8,256]{1,0:T(8,128)S(1)}, f32[8,256]{1,0:T(8,128)S(1)}, u32[]{:S(2)}, u32[]{:S(2)}) collective-permute-start(f32[8,256]{1,0:T(8,128)S(1)} %pad_maximum_fusion.1), channel_id=1, source_target_pairs={{4,228},{12,236},{20,244},{28,252},{5,229},{13,237},{21,245},{29,2... | collective-permute-start | bytes 24584 | tf_op jit(solution)/shard_map/ppermute | solution.py:223
  42.2 2.5 %collective-permute-start.5 = (f32[8,256]{1,0:T(8,128)S(1)}, f32[8,256]{1,0:T(8,128)S(1)}, u32[]{:S(2)}, u32[]{:S(2)}) collective-permute-start(f32[8,256]{1,0:T(8,128)S(1)} %pad_maximum_fusion.1), channel_id=1, source_target_pairs={{4,196},{12,204},{20,212},{28,220},{36,228},{44,236},{52,244},{60,... | collective-permute-start | bytes 24584 | tf_op jit(solution)/shard_map/ppermute | solution.py:223
  44.6 1.3 %collective-permute-start.6 = (f32[8,256]{1,0:T(8,128)S(1)}, f32[8,256]{1,0:T(8,128)S(1)}, u32[]{:S(2)}, u32[]{:S(2)}) collective-permute-start(f32[8,256]{1,0:T(8,128)S(1)} %pad_maximum_fusion.1), channel_id=1, source_target_pairs={{4,164},{12,172},{20,180},{28,188},{36,196},{44,204},{52,212},{60,... | collective-permute-start | bytes 24584 | tf_op jit(solution)/shard_map/ppermute | solution.py:223
  45.9 1.3 %collective-permute-start.7 = (f32[8,256]{1,0:T(8,128)S(1)}, f32[8,256]{1,0:T(8,128)S(1)}, u32[]{:S(2)}, u32[]{:S(2)}) collective-permute-start(f32[8,256]{1,0:T(8,128)S(1)} %pad_maximum_fusion.1), channel_id=1, source_target_pairs={{4,132},{12,140},{20,148},{28,156},{36,164},{44,172},{52,180},{60,... | collective-permute-start | bytes 24584 | tf_op jit(solution)/shard_map/ppermute | solution.py:223
  47.2 0.0 collective-permute-done.10
  47.2 3.7 %collective-permute-start.8 = (f32[8,256]{1,0:T(8,128)S(1)}, f32[8,256]{1,0:T(8,128)S(1)}, u32[]{:S(2)}, u32[]{:S(2)}) collective-permute-start(f32[8,256]{1,0:T(8,128)S(1)} %pad_maximum_fusion.1), channel_id=1, source_target_pairs={{4,100},{12,108},{20,116},{28,124},{36,132},{44,140},{52,148},{60,... | collective-permute-start | bytes 24584 | tf_op jit(solution)/shard_map/ppermute | solution.py:223
  51.0 0.0 collective-permute-done.4
  51.0 1.6 %collective-permute-start.9 = (f32[8,256]{1,0:T(8,128)S(1)}, f32[8,256]{1,0:T(8,128)S(1)}, u32[]{:S(2)}, u32[]{:S(2)}) collective-permute-start(f32[8,256]{1,0:T(8,128)S(1)} %pad_maximum_fusion.1), channel_id=1, source_target_pairs={{4,68},{12,76},{20,84},{28,92},{36,100},{44,108},{52,116},{60,124}... | collective-permute-start | bytes 24584 | tf_op jit(solution)/shard_map/ppermute | solution.py:223
  52.5 0.0 collective-permute-done.5
  52.5 0.0 collective-permute-done.6
  52.6 0.0 collective-permute-done.7
  52.6 0.0 collective-permute-done.8
  52.6 0.7 collective-permute-done.9
  53.3 1.3 %collective-permute-start.11 = (f32[4,256]{1,0:T(4,128)S(1)}, f32[4,256]{1,0:T(4,128)S(1)}, u32[]{:S(2)}, u32[]{:S(2)}) collective-permute-start(f32[4,256]{1,0:T(4,128)S(1)} %fusion.2), channel_id=1, source_target_pairs={{4,0},{5,1},{6,2},{7,3},{12,8},{13,9},{14,10},{15,11},{20,16},{21,... | collective-permute-start | bytes 12296 | tf_op jit(solution)/shard_map/ppermute | solution.py:236
  54.6 0.0 copy-done.8
  54.6 0.0 copy-start.1
  54.6 2.2 %copy-done.1 = f32[4,1024,256]{2,1,0:T(8,128)S(1)} copy-done((f32[4,1024,256]{2,1,0:T(8,128)S(1)}, f32[4,1024,256]{2,1,0:T(8,128)}, u32[]{:S(2)}) %copy-start.1) | copy-done | bytes 4194328
  56.8 0.0 copy-start.3
  56.8 2.2 %copy-done.3 = f32[4,1024,256]{2,1,0:T(8,128)S(1)} copy-done((f32[4,1024,256]{2,1,0:T(8,128)S(1)}, f32[4,1024,256]{2,1,0:T(8,128)}, u32[]{:S(2)}) %copy-start.3) | copy-done | bytes 4194328
  59.0 8.8 %localize.1 = (f32[4,1024,256]{2,1,0:T(8,128)S(1)}, f32[4,1024,256]{2,1,0:T(8,128)S(1)}) custom-call(f32[4,1024,256]{2,1,0:T(8,128)S(1)} %copy-done.1, f32[4,1024,256]{2,1,0:T(8,128)S(1)} %copy-done.3, bf16[4,1024,256]{2,1,0:T(8,128)(2,1)S(1)} %copy-done.8), custom_call_target="tpu_custom_call" | custom-call | flops 2000000000 | bytes 2097152 | tf_op jit(solution)/shard_map/localize/pallas_call | solution.py:112
  67.8 0.0 copy-start.4
  67.8 2.0 %copy-done.4 = f32[4,1024,256]{2,1,0:T(8,128)} copy-done((f32[4,1024,256]{2,1,0:T(8,128)}, f32[4,1024,256]{2,1,0:T(8,128)S(1)}, u32[]{:S(2)}) %copy-start.4) | copy-done | bytes 4194328
  69.8 0.0 copy-start.6
  69.8 2.0 %copy-done.6 = f32[4,1024,256]{2,1,0:T(8,128)} copy-done((f32[4,1024,256]{2,1,0:T(8,128)}, f32[4,1024,256]{2,1,0:T(8,128)S(1)}, u32[]{:S(2)}) %copy-start.6) | copy-done | bytes 4194328
  71.8 0.0 collective-permute-done.11
  71.8 0.0 copy-start.5
  71.8 2.2 %copy-done.5 = f32[4,1024,256]{2,1,0:T(8,128)S(1)} copy-done((f32[4,1024,256]{2,1,0:T(8,128)S(1)}, f32[4,1024,256]{2,1,0:T(8,128)}, u32[]{:S(2)}) %copy-start.5) | copy-done | bytes 4194328
  74.0 0.0 copy-start.7
  74.0 2.2 %copy-done.7 = f32[4,1024,256]{2,1,0:T(8,128)S(1)} copy-done((f32[4,1024,256]{2,1,0:T(8,128)S(1)}, f32[4,1024,256]{2,1,0:T(8,128)}, u32[]{:S(2)}) %copy-start.7) | copy-done | bytes 4194328
  76.2 0.0 copy-start.9
  76.2 5.7 %gate_and_square.1 = (f32[4,1024,256]{2,1,0:T(8,128)S(1)}, f32[4,8,128]{2,1,0:T(8,128)S(1)}) custom-call(f32[4,1024,256]{2,1,0:T(8,128)S(1)} %copy-done.5, f32[4,1024,256]{2,1,0:T(8,128)S(1)} %copy-done.7, f32[4,256]{1,0:T(4,128)S(1)} %multiply_select_fusion.enter_ref), custom_call_target="tpu_custom_call" | custom-call | flops 8000000 | bytes 12582912 | tf_op jit(solution)/shard_map/gate_and_square/pallas_call | solution.py:150
  81.9 2.8 %collective-permute-start.12 = (f32[4,8,128]{2,1,0:T(8,128)S(1)}, f32[4,8,128]{2,1,0:T(8,128)S(1)}, u32[]{:S(2)}, u32[]{:S(2)}) collective-permute-start(f32[4,8,128]{2,1,0:T(8,128)S(1)} %get-tuple-element.18.p0_ref), channel_id=1, source_target_pairs={{0,2},{1,3},{2,0},{3,1},{4,6},{5,7},{6,4},{7,5},{8,10},{9,11},{10,... | collective-permute-start | bytes 49160 | tf_op jit(solution)/shard_map/ppermute | solution.py:249
  84.6 0.3 collective-permute-start.13
  84.9 2.4 %collective-permute-start.14 = (f32[4,8,128]{2,1,0:T(8,128)S(1)}, f32[4,8,128]{2,1,0:T(8,128)S(1)}, u32[]{:S(2)}, u32[]{:S(2)}) collective-permute-start(f32[4,8,128]{2,1,0:T(8,128)S(1)} %get-tuple-element.18.p0_ref), channel_id=1, source_target_pairs={{0,3},{1,0},{2,1},{3,2},{4,7},{5,4},{6,5},{7,6},{8,11},{9,8},{10,9... | collective-permute-start | bytes 49160 | tf_op jit(solution)/shard_map/ppermute | solution.py:249
  87.3 0.0 collective-permute-done.12.p1_ref
  87.3 1.1 %collective-permute-done.13.p2_ref = f32[4,8,128]{2,1,0:T(8,128)S(1)} collective-permute-done((f32[4,8,128]{2,1,0:T(8,128)S(1)}, f32[4,8,128]{2,1,0:T(8,128)S(1)}, u32[]{:S(2)}, u32[]{:S(2)}) %collective-permute-start.13) | collective-permute-done | bytes 16416 | tf_op jit(solution)/shard_map/ppermute | solution.py:249
  88.4 0.0 collective-permute-done.14.p3_ref
  88.4 0.0 copy-done.9
  88.4 2.3 %scale.1 = bf16[4,1024,256]{2,1,0:T(8,128)(2,1)} custom-call(f32[4,1024,256]{2,1,0:T(8,128)S(1)} %get-tuple-element.17.gated_ref, f32[4,8,128]{2,1,0:T(8,128)S(1)} %get-tuple-element.18.p0_ref, f32[4,8,128]{2,1,0:T(8,128)S(1)} %collective-permute-done.12.p1_ref, f32[4,8,128]{2,1,0:T(8,128)S(1)} %collective-permute-done.13.p2_ref, ...), custom_call_target="tpu_custom_call" | custom-call | flops 8000000 | bytes 6291456 | tf_op jit(solution)/shard_map/scale/pallas_call | solution.py:178
  (10 shorter events, 0.1 us)
Async XLA Ops:
  0.0 54.6 %copy-start.8 = (bf16[4,1024,256]{2,1,0:T(8,128)(2,1)S(1)}, bf16[4,1024,256]{2,1,0:T(8,128)(2,1)}, u32[]{:S(2)}) copy-start(bf16[4,1024,256]{2,1,0:T(8,128)(2,1)} %gate_hbm.1) | copy-start | bytes 6291460
  0.0 2.3 %copy-start.10 = (f32[4,1024,256]{2,1,0:T(8,128)S(1)}, f32[4,1024,256]{2,1,0:T(8,128)}, u32[]{:S(2)}) copy-start(f32[4,1024,256]{2,1,0:T(8,128)} %rate_hbm.1) | copy-start | bytes 12582916
  2.3 1.6 %copy-start.11 = (bf16[4,1024,256]{2,1,0:T(8,128)(2,1)S(1)}, bf16[4,1024,256]{2,1,0:T(8,128)(2,1)}, u32[]{:S(2)}) copy-start(bf16[4,1024,256]{2,1,0:T(8,128)(2,1)} %drive_hbm.1) | copy-start | bytes 6291460
  12.9 2.0 %copy-start = (f32[4,1024,256]{2,1,0:T(8,128)}, f32[4,1024,256]{2,1,0:T(8,128)S(1)}, u32[]{:S(2)}) copy-start(f32[4,1024,256]{2,1,0:T(8,128)S(1)} %get-tuple-element.12.depth_ref) | copy-start | bytes 12582916
  14.8 2.0 %copy-start.2 = (f32[4,1024,256]{2,1,0:T(8,128)}, f32[4,1024,256]{2,1,0:T(8,128)S(1)}, u32[]{:S(2)}) copy-start(f32[4,1024,256]{2,1,0:T(8,128)S(1)} %get-tuple-element.13.term_ref) | copy-start | bytes 12582916
  16.9 5.1 %collective-permute-start = (f32[8,256]{1,0:T(8,128)S(1)}, f32[8,256]{1,0:T(8,128)S(1)}, u32[]{:S(2)}, u32[]{:S(2)}) collective-permute-start(f32[8,256]{1,0:T(8,128)S(1)} %get-tuple-element.16), channel_id=1, source_target_pairs={{0,4},{1,5},{2,6},{3,7},{8,12},{9,13},{10,14},{11,15},{16,20},{17,... | collective-permute-start | bytes 24584 | tf_op jit(solution)/shard_map/ppermute | solution.py:205
  22.0 8.3 %collective-permute-start.1 = (f32[8,256]{1,0:T(8,128)S(1)}, f32[8,256]{1,0:T(8,128)S(1)}, u32[]{:S(2)}, u32[]{:S(2)}) collective-permute-start(f32[8,256]{1,0:T(8,128)S(1)} %pad_maximum_fusion), channel_id=1, source_target_pairs={{4,28},{12,4},{20,12},{28,20},{5,29},{13,5},{21,13},{29,21},{6,30}... | collective-permute-start | bytes 24584 | tf_op jit(solution)/shard_map/ppermute | solution.py:211
  25.4 5.9 %collective-permute-start.2 = (f32[8,256]{1,0:T(8,128)S(1)}, f32[8,256]{1,0:T(8,128)S(1)}, u32[]{:S(2)}, u32[]{:S(2)}) collective-permute-start(f32[8,256]{1,0:T(8,128)S(1)} %pad_maximum_fusion), channel_id=1, source_target_pairs={{4,20},{12,28},{20,4},{28,12},{5,21},{13,29},{21,5},{29,13},{6,22}... | collective-permute-start | bytes 24584 | tf_op jit(solution)/shard_map/ppermute | solution.py:211
  27.7 5.6 %collective-permute-start.3 = (f32[8,256]{1,0:T(8,128)S(1)}, f32[8,256]{1,0:T(8,128)S(1)}, u32[]{:S(2)}, u32[]{:S(2)}) collective-permute-start(f32[8,256]{1,0:T(8,128)S(1)} %pad_maximum_fusion), channel_id=1, source_target_pairs={{4,12},{12,20},{20,28},{28,4},{5,13},{13,21},{21,29},{29,5},{6,14}... | collective-permute-start | bytes 24584 | tf_op jit(solution)/shard_map/ppermute | solution.py:211
  33.4 13.9 %collective-permute-start.10 = (f32[8,256]{1,0:T(8,128)S(1)}, f32[8,256]{1,0:T(8,128)S(1)}, u32[]{:S(2)}, u32[]{:S(2)}) collective-permute-start(f32[8,256]{1,0:T(8,128)S(1)} %pad_maximum_fusion.1), channel_id=1, source_target_pairs={{4,36},{12,44},{20,52},{28,60},{36,68},{44,76},{52,84},{60,92},{68... | collective-permute-start | bytes 24584 | tf_op jit(solution)/shard_map/ppermute | solution.py:223
  36.9 14.0 %collective-permute-start.4 = (f32[8,256]{1,0:T(8,128)S(1)}, f32[8,256]{1,0:T(8,128)S(1)}, u32[]{:S(2)}, u32[]{:S(2)}) collective-permute-start(f32[8,256]{1,0:T(8,128)S(1)} %pad_maximum_fusion.1), channel_id=1, source_target_pairs={{4,228},{12,236},{20,244},{28,252},{5,229},{13,237},{21,245},{29,2... | collective-permute-start | bytes 24584 | tf_op jit(solution)/shard_map/ppermute | solution.py:223
  42.2 10.4 %collective-permute-start.5 = (f32[8,256]{1,0:T(8,128)S(1)}, f32[8,256]{1,0:T(8,128)S(1)}, u32[]{:S(2)}, u32[]{:S(2)}) collective-permute-start(f32[8,256]{1,0:T(8,128)S(1)} %pad_maximum_fusion.1), channel_id=1, source_target_pairs={{4,196},{12,204},{20,212},{28,220},{36,228},{44,236},{52,244},{60,... | collective-permute-start | bytes 24584 | tf_op jit(solution)/shard_map/ppermute | solution.py:223
  44.6 7.9 %collective-permute-start.6 = (f32[8,256]{1,0:T(8,128)S(1)}, f32[8,256]{1,0:T(8,128)S(1)}, u32[]{:S(2)}, u32[]{:S(2)}) collective-permute-start(f32[8,256]{1,0:T(8,128)S(1)} %pad_maximum_fusion.1), channel_id=1, source_target_pairs={{4,164},{12,172},{20,180},{28,188},{36,196},{44,204},{52,212},{60,... | collective-permute-start | bytes 24584 | tf_op jit(solution)/shard_map/ppermute | solution.py:223
  45.9 6.6 %collective-permute-start.7 = (f32[8,256]{1,0:T(8,128)S(1)}, f32[8,256]{1,0:T(8,128)S(1)}, u32[]{:S(2)}, u32[]{:S(2)}) collective-permute-start(f32[8,256]{1,0:T(8,128)S(1)} %pad_maximum_fusion.1), channel_id=1, source_target_pairs={{4,132},{12,140},{20,148},{28,156},{36,164},{44,172},{52,180},{60,... | collective-permute-start | bytes 24584 | tf_op jit(solution)/shard_map/ppermute | solution.py:223
  47.2 5.3 %collective-permute-start.8 = (f32[8,256]{1,0:T(8,128)S(1)}, f32[8,256]{1,0:T(8,128)S(1)}, u32[]{:S(2)}, u32[]{:S(2)}) collective-permute-start(f32[8,256]{1,0:T(8,128)S(1)} %pad_maximum_fusion.1), channel_id=1, source_target_pairs={{4,100},{12,108},{20,116},{28,124},{36,132},{44,140},{52,148},{60,... | collective-permute-start | bytes 24584 | tf_op jit(solution)/shard_map/ppermute | solution.py:223
  51.0 2.3 %collective-permute-start.9 = (f32[8,256]{1,0:T(8,128)S(1)}, f32[8,256]{1,0:T(8,128)S(1)}, u32[]{:S(2)}, u32[]{:S(2)}) collective-permute-start(f32[8,256]{1,0:T(8,128)S(1)} %pad_maximum_fusion.1), channel_id=1, source_target_pairs={{4,68},{12,76},{20,84},{28,92},{36,100},{44,108},{52,116},{60,124}... | collective-permute-start | bytes 24584 | tf_op jit(solution)/shard_map/ppermute | solution.py:223
  53.3 18.4 %collective-permute-start.11 = (f32[4,256]{1,0:T(4,128)S(1)}, f32[4,256]{1,0:T(4,128)S(1)}, u32[]{:S(2)}, u32[]{:S(2)}) collective-permute-start(f32[4,256]{1,0:T(4,128)S(1)} %fusion.2), channel_id=1, source_target_pairs={{4,0},{5,1},{6,2},{7,3},{12,8},{13,9},{14,10},{15,11},{20,16},{21,... | collective-permute-start | bytes 12296 | tf_op jit(solution)/shard_map/ppermute | solution.py:236
  54.6 2.2 %copy-start.1 = (f32[4,1024,256]{2,1,0:T(8,128)S(1)}, f32[4,1024,256]{2,1,0:T(8,128)}, u32[]{:S(2)}) copy-start(f32[4,1024,256]{2,1,0:T(8,128)} %copy-done) | copy-start | bytes 12582916
  56.8 2.2 %copy-start.3 = (f32[4,1024,256]{2,1,0:T(8,128)S(1)}, f32[4,1024,256]{2,1,0:T(8,128)}, u32[]{:S(2)}) copy-start(f32[4,1024,256]{2,1,0:T(8,128)} %copy-done.2) | copy-start | bytes 12582916
  67.8 2.0 %copy-start.4 = (f32[4,1024,256]{2,1,0:T(8,128)}, f32[4,1024,256]{2,1,0:T(8,128)S(1)}, u32[]{:S(2)}) copy-start(f32[4,1024,256]{2,1,0:T(8,128)S(1)} %get-tuple-element.14.factor_ref) | copy-start | bytes 12582916
  69.8 2.0 %copy-start.6 = (f32[4,1024,256]{2,1,0:T(8,128)}, f32[4,1024,256]{2,1,0:T(8,128)S(1)}, u32[]{:S(2)}) copy-start(f32[4,1024,256]{2,1,0:T(8,128)S(1)} %get-tuple-element.15.sum_ref) | copy-start | bytes 12582916
  71.8 2.2 %copy-start.5 = (f32[4,1024,256]{2,1,0:T(8,128)S(1)}, f32[4,1024,256]{2,1,0:T(8,128)}, u32[]{:S(2)}) copy-start(f32[4,1024,256]{2,1,0:T(8,128)} %copy-done.4) | copy-start | bytes 12582916
  74.0 2.2 %copy-start.7 = (f32[4,1024,256]{2,1,0:T(8,128)S(1)}, f32[4,1024,256]{2,1,0:T(8,128)}, u32[]{:S(2)}) copy-start(f32[4,1024,256]{2,1,0:T(8,128)} %copy-done.6) | copy-start | bytes 12582916
  76.2 12.3 %copy-start.9 = (f32[256]{0:T(256)S(1)}, f32[256]{0:T(256)}, u32[]{:S(2)}) copy-start(f32[256]{0:T(256)} %param.7) | copy-start | bytes 3076
  81.9 5.4 %collective-permute-start.12 = (f32[4,8,128]{2,1,0:T(8,128)S(1)}, f32[4,8,128]{2,1,0:T(8,128)S(1)}, u32[]{:S(2)}, u32[]{:S(2)}) collective-permute-start(f32[4,8,128]{2,1,0:T(8,128)S(1)} %get-tuple-element.18.p0_ref), channel_id=1, source_target_pairs={{0,2},{1,3},{2,0},{3,1},{4,6},{5,7},{6,4},{7,5},{8,10},{9,11},{10,... | collective-permute-start | bytes 49160 | tf_op jit(solution)/shard_map/ppermute | solution.py:249
  84.6 3.8 %collective-permute-start.13 = (f32[4,8,128]{2,1,0:T(8,128)S(1)}, f32[4,8,128]{2,1,0:T(8,128)S(1)}, u32[]{:S(2)}, u32[]{:S(2)}) collective-permute-start(f32[4,8,128]{2,1,0:T(8,128)S(1)} %get-tuple-element.18.p0_ref), channel_id=1, source_target_pairs={{0,1},{1,2},{2,3},{3,0},{4,5},{5,6},{6,7},{7,4},{8,9},{9,10},{10,1... | collective-permute-start | bytes 49160 | tf_op jit(solution)/shard_map/ppermute | solution.py:249
  84.9 3.5 %collective-permute-start.14 = (f32[4,8,128]{2,1,0:T(8,128)S(1)}, f32[4,8,128]{2,1,0:T(8,128)S(1)}, u32[]{:S(2)}, u32[]{:S(2)}) collective-permute-start(f32[4,8,128]{2,1,0:T(8,128)S(1)} %get-tuple-element.18.p0_ref), channel_id=1, source_target_pairs={{0,3},{1,0},{2,1},{3,2},{4,7},{5,4},{6,5},{7,6},{8,11},{9,8},{10,9... | collective-permute-start | bytes 49160 | tf_op jit(solution)/shard_map/ppermute | solution.py:249

commit v2 on v0

v2 whole, which is shorter than its diff:
```python
import functools
import math

import jax
import jax.numpy as jnp
from jax import lax
from jax.experimental import pallas as pl
from jax.experimental.pallas import tpu as pltpu
from jax.sharding import Mesh
from jax.sharding import PartitionSpec as P

SP = ("sp_0", "sp_1", "sp_2")
CHIPS = ("sp_0", "sp_1")
BLOCK = 128
PIECE = 256
MIB = 1 << 20
VMEM = pl.BlockSpec(memory_space=pltpu.VMEM)
HBM = pl.BlockSpec(memory_space=pltpu.HBM)
SMEM = pl.BlockSpec(memory_space=pltpu.SMEM)


def stacked_triangle():
    row = lax.broadcasted_iota(jnp.int32, (BLOCK, 2 * BLOCK), 0)
    col = lax.broadcasted_iota(jnp.int32, (BLOCK, 2 * BLOCK), 1)
    return (row >= col % BLOCK).astype(jnp.bfloat16)


def running_sum(tri, x):
    high = x.astype(jnp.bfloat16)
    low = (x - high.astype(jnp.float32)).astype(jnp.bfloat16)
    return jnp.dot(tri, jnp.concatenate([high, low], axis=0), preferred_element_type=jnp.float32)


def piece_copy(hbm, vmem, sems, b, i):
    at = pl.ds(pl.multiple_of(i * PIECE, PIECE), PIECE)
    return pltpu.make_async_copy(hbm.at[b, at, :], vmem.at[b, at, :], sems.at[b * (hbm.shape[1] // PIECE) + i])


def start_all(sets):
    batch, length, _ = sets[0][0].shape
    for b in range(batch):
        for i in range(length // PIECE):
            for one in sets:
                piece_copy(*one, b, i).start()


def wait_at(sets, b, row):
    if row % PIECE == 0:
        for one in sets:
            piece_copy(*one, b, row // PIECE).wait()


def summary_kernel(total, rate_hbm, drive_hbm, out_ref, rate, drive, tri_ref, rate_sem, drive_sem):
    batch, length, channels = rate.shape
    sets = ((rate_hbm, rate, rate_sem), (drive_hbm, drive, drive_sem))
    start_all(sets)
    tri_ref[...] = stacked_triangle()
    to_log2 = math.log2(math.e) / total

    def one_batch(b, _):
        tri = tri_ref[...]
        lost = jnp.zeros((1, channels), jnp.float32)
        sums = jnp.zeros((8, channels), jnp.float32)
        for row in range(0, length, BLOCK):
            at = pl.ds(row, BLOCK)
            wait_at(sets, b, row)
            log_lost = running_sum(tri, rate[b, at, :]) * to_log2 + lost
            lost = log_lost[BLOCK - 1 :, :]
            term = jnp.exp2(log_lost) * drive[b, at, :].astype(jnp.float32)
            sums = sums + jnp.sum(term.reshape(BLOCK // 8, 8, channels), axis=0)
        out_ref[b, 0:1, :] = -lost
        out_ref[b, 1:2, :] = jnp.sum(sums, axis=0, keepdims=True)
        return 0

    lax.fori_loop(0, batch, one_batch, 0)


def summarize(decay_rate, drive_in, total):
    batch, length, channels = decay_rate.shape
    sems = pltpu.SemaphoreType.DMA((batch * length // PIECE,))
    return pl.pallas_call(
        functools.partial(summary_kernel, total),
        out_shape=jax.ShapeDtypeStruct((batch, 2, channels), jnp.float32),
        in_specs=[HBM] * 2,
        out_specs=VMEM,
        scratch_shapes=[
            pltpu.VMEM(decay_rate.shape, jnp.float32),
            pltpu.VMEM(drive_in.shape, jnp.bfloat16),
            pltpu.VMEM((BLOCK, 2 * BLOCK), jnp.bfloat16),
            sems,
            sems,
        ],
        compiler_params=pltpu.CompilerParams(vmem_limit_bytes=62 * MIB),
        cost_estimate=pl.CostEstimate(flops=1_000_000_000, bytes_accessed=6 * MIB, transcendentals=MIB),
        name="summarize",
    )(decay_rate, drive_in)


def local_kernel(
    total, rate_hbm, drive_hbm, gate_hbm, factor_ref, sum_ref, rate, drive, gate, tri_ref, rate_sem, drive_sem, gate_sem
):
    batch, length, channels = rate.shape
    sets = ((rate_hbm, rate, rate_sem), (drive_hbm, drive, drive_sem), (gate_hbm, gate, gate_sem))
    start_all(sets)
    tri_ref[...] = stacked_triangle()
    to_log2 = -math.log2(math.e) / total
    half = 0.5 * total**-0.5

    def one_batch(b, _):
        log_in = jnp.zeros((1, channels), jnp.float32)
        sum_in = jnp.zeros((1, channels), jnp.float32)
        tri = tri_ref[...]
        for row in range(0, length, BLOCK):
            at = pl.ds(row, BLOCK)
            wait_at(sets, b, row)
            log_kept = running_sum(tri, rate[b, at, :]) * to_log2 + log_in
            log_in = log_kept[BLOCK - 1 :, :]
            term = jnp.exp2(-log_kept) * drive[b, at, :].astype(jnp.float32)
            opened = half * jnp.tanh((0.5 * gate[b, at, :]).astype(jnp.float32)) + half
            factor_ref[b, at, :] = jnp.exp2(log_kept) * opened
            sums = running_sum(tri, term) + sum_in
            sum_in = sums[BLOCK - 1 :, :]
            sum_ref[b, at, :] = sums
        return 0

    lax.fori_loop(0, batch, one_batch, 0)


def localize(decay_rate, drive_in, gate_in, total):
    batch, length, channels = decay_rate.shape
    big = jax.ShapeDtypeStruct(decay_rate.shape, jnp.float32)
    sems = pltpu.SemaphoreType.DMA((batch * length // PIECE,))
    return pl.pallas_call(
        functools.partial(local_kernel, total),
        out_shape=(big, big),
        in_specs=[HBM] * 3,
        out_specs=(VMEM,) * 2,
        scratch_shapes=[
            pltpu.VMEM(decay_rate.shape, jnp.float32),
            pltpu.VMEM(drive_in.shape, jnp.bfloat16),
            pltpu.VMEM(gate_in.shape, jnp.bfloat16),
            pltpu.VMEM((BLOCK, 2 * BLOCK), jnp.bfloat16),
            sems,
            sems,
            sems,
        ],
        compiler_params=pltpu.CompilerParams(vmem_limit_bytes=20 * MIB),
        cost_estimate=pl.CostEstimate(flops=4_000_000_000, bytes_accessed=8 * MIB, transcendentals=3 * MIB),
        name="localize",
    )(decay_rate, drive_in, gate_in)


def enter_kernel(place_ref, all_ref, first_ref, out_ref):
    chips, pairs, _, channels = all_ref.shape
    place = place_ref[0]
    for p in range(pairs):
        state = jnp.zeros((1, channels), jnp.float32)
        for j in range(chips):
            kept = jnp.exp2(jnp.where(j < place, all_ref[j, p, 0:1, :], 0.0))
            state = kept * (state + jnp.where(j < place, all_ref[j, p, 1:2, :], 0.0))
        out_ref[0, p : p + 1, :] = state
        out_ref[1, p : p + 1, :] = jnp.exp2(first_ref[p, 0:1, :]) * (state + first_ref[p, 1:2, :])


def entering(place, everyone, first):
    chips, pairs, _, channels = everyone.shape
    return pl.pallas_call(
        enter_kernel,
        out_shape=jax.ShapeDtypeStruct((2, pairs, channels), jnp.float32),
        in_specs=[SMEM, VMEM, VMEM],
        out_specs=VMEM,
        compiler_params=pltpu.CompilerParams(vmem_limit_bytes=2 * MIB),
        name="entering",
    )(place, everyone, first)


def gate_kernel(factor_ref, sum_ref, enter_ref, gated_ref, power_ref):
    batch, length, channels = factor_ref.shape
    lane = lax.broadcasted_iota(jnp.int32, (8, 128), 1)

    def one_batch(b, _):
        enter = jnp.broadcast_to(enter_ref[pl.ds(b, 1), :], (8, channels))
        power = jnp.zeros((8, length // 8), jnp.float32)
        for j in range(length // 8):
            at = pl.ds(8 * j, 8)
            gated = factor_ref[b, at, :] * (sum_ref[b, at, :] + enter)
            gated_ref[b, at, :] = gated
            power = jnp.where(lane == j, jnp.sum(gated * gated, axis=-1, keepdims=True), power)
        power_ref[b] = power
        return 0

    lax.fori_loop(0, batch, one_batch, 0)


def gate_and_square(factor, sums, enter):
    batch, length, channels = factor.shape
    return pl.pallas_call(
        gate_kernel,
        out_shape=(
            jax.ShapeDtypeStruct(factor.shape, jnp.float32),
            jax.ShapeDtypeStruct((batch, 8, length // 8), jnp.float32),
        ),
        in_specs=[VMEM] * 3,
        out_specs=(VMEM, VMEM),
        compiler_params=pltpu.CompilerParams(vmem_limit_bytes=14 * MIB),
        cost_estimate=pl.CostEstimate(flops=8_000_000, bytes_accessed=12 * MIB, transcendentals=0),
        name="gate_and_square",
    )(factor, sums, enter)


def scale_kernel(width, gated_ref, p0_ref, p1_ref, p2_ref, p3_ref, gain_ref, out_hbm, out, sem):
    batch, length, channels = gated_ref.shape

    def copy(b):
        return pltpu.make_async_copy(out.at[b], out_hbm.at[b], sem.at[b])

    def one_batch(b, _):
        gain = jnp.broadcast_to(gain_ref[...], (8, channels))
        power = (p0_ref[b] + p1_ref[b]) + (p2_ref[b] + p3_ref[b])
        scale = lax.rsqrt(power * (1.0 / width) + 1e-06)
        for j in range(length // 16):
            parts = []
            for k in range(2):
                column = jnp.full((8, 128), 2 * j + k, jnp.int32)
                rows = jnp.take_along_axis(scale, column, axis=1)
                rows = jnp.concatenate([rows] * (channels // 128), axis=1)
                parts.append(gated_ref[b, pl.ds(16 * j + 8 * k, 8), :] * rows * gain)
            out[b, pl.ds(16 * j, 16), :] = jnp.concatenate(parts, axis=0).astype(jnp.bfloat16)
        copy(b).start()
        return 0

    lax.fori_loop(0, batch, one_batch, 0)
    for b in range(batch):
        copy(b).wait()


def scale(gated, powers, gain, width):
    batch, length, channels = gated.shape
    return pl.pallas_call(
        functools.partial(scale_kernel, width),
        out_shape=jax.ShapeDtypeStruct(gated.shape, jnp.bfloat16),
        in_specs=[VMEM] * 6,
        out_specs=HBM,
        scratch_shapes=[pltpu.VMEM(gated.shape, jnp.bfloat16), pltpu.SemaphoreType.DMA((batch,))],
        compiler_params=pltpu.CompilerParams(vmem_limit_bytes=8 * MIB),
        cost_estimate=pl.CostEstimate(flops=8_000_000, bytes_accessed=6 * MIB, transcendentals=0),
        name="scale",
    )(gated, *powers, gain.reshape(1, channels))


def join(earlier, later):
    return jnp.stack([earlier[:, 0] + later[:, 0], earlier[:, 1] + jnp.exp2(-earlier[:, 0]) * later[:, 1]], axis=1)


def entering_state(pair):
    half = pair.shape[0] // 2
    first_core = lax.axis_index("sp_2") == 0
    low, high = pair[:half], pair[half:]
    swap = [(0, 1), (1, 0)]
    got = lax.ppermute(jnp.where(first_core, high, low), "sp_2", swap)
    first = jnp.where(first_core, low, got)
    second = jnp.where(first_core, got, high)
    chip = join(first, second)
    chips = lax.axis_size(CHIPS)
    everyone = lax.all_to_all(jnp.broadcast_to(chip, (chips,) + chip.shape), CHIPS, 0, 0)
    both = entering(lax.axis_index(CHIPS).reshape(1), everyone, first)
    back = lax.ppermute(jnp.where(first_core, both[1], both[0]), "sp_2", swap)
    return jnp.where(
        first_core, jnp.concatenate([both[0], back], axis=0), jnp.concatenate([back, both[1]], axis=0)
    )


def shards(decay_rate, drive_in, gate_in, norm_gain):
    total = decay_rate.shape[1] * lax.axis_size(SP)
    parts = lax.axis_size("tp")
    width = decay_rate.shape[2] * parts
    enter = entering_state(summarize(decay_rate, drive_in, total))
    factor, sums = localize(decay_rate, drive_in, gate_in, total)
    gated, power = gate_and_square(factor, sums, enter)
    powers = [power] + [lax.ppermute(power, "tp", [(i, i ^ k) for i in range(parts)]) for k in (2, 1, 3)]
    return scale(gated, powers, norm_gain, width)


def solution(mesh):
    torus = Mesh(mesh.devices.reshape(8, 4, 2, mesh.shape["tp"]), ("sp_0", "sp_1", "sp_2", "tp"))
    in_specs = (P(None, SP, "tp"), P(None, SP, "tp"), P(None, SP, "tp"), P("tp"))
    out_specs = P(None, SP, "tp")
    return jax.shard_map(shards, mesh=torus, in_specs=in_specs, out_specs=out_specs, check_vma=False)
```

time: 282 us -> 60.5 us (0.21)
  the two profiles are of different devices: /device:TPU:2 before, /device:TPU:10 now
where the time goes in v2:
time: 60.5 us; the launch traced here: 60.1 us
  Pallas kernels  21.5 us (36%)
  starting transfers between devices  15.4 us (25%)
  local copies, waits for them, and re-layouts  14.4 us (24%)
  waiting for transfers between devices  7.35 us (12%)
  other arithmetic  1.46 us (2%)
    unnamed x16, local copies, waits for them, and re-layouts  13.7 us
    pallas_call x1, Pallas kernels, localize(): pl.pallas_call(functools.partial(local_kernel, total), out_shape=(big, bi...  12.8 us
    all_to_all x1, starting transfers between devices, entering_state(): lax.all_to_all(jnp.broadcast_to(chip, (chips,) + chip.shape), CHIPS, 0, 0)  11.7 us
    pallas_call x1, Pallas kernels, summarize(): pl.pallas_call(functools.partial(summary_kernel, total), out_shape=jax.Sh...  5.63 us
    ppermute x3, waiting for transfers between devices, shards(): lax.ppermute(power, 'tp', [(i, i ^ k) for i in range(parts)])  5.04 us
    ppermute x3, starting transfers between devices, shards(): lax.ppermute(power, 'tp', [(i, i ^ k) for i in range(parts)])  3.57 us
    pallas_call x1, Pallas kernels, scale(): pl.pallas_call(functools.partial(scale_kernel, width), out_shape=jax.Shap...  2.05 us
  transfers between devices with their start and end apart: 6, of which 5 were waited for; matrix products, arithmetic and copies ran while one was open for 0% of the time, Pallas kernels for 21%

profile of v2, /device:TPU:10, one launch (start us, length us, event | category | flops | bytes accessed | tf_op | source)
XLA Modules:
  0.0 60.1 jit_solution(10997336236735902461)
XLA Ops:
  0.0 5.6 %summarize.1 = f32[4,2,256]{2,1,0:T(2,128)} custom-call(f32[4,1024,256]{2,1,0:T(8,128)} %rate_hbm.3, bf16[4,1024,256]{2,1,0:T(8,128)(2,1)} %drive_hbm.3), custom_call_target="tpu_custom_call" | custom-call | flops 1000000000 | bytes 6291456 | tf_op jit(solution)/shard_map/summarize/pallas_call | solution.py:81
  5.6 0.7 %broadcast_select_fusion.2 = f32[2,2,256]{2,1,0:T(2,128)S(1)} fusion(pred[]{:T(512)S(6)} %eq.3, f32[4,2,256]{2,1,0:T(2,128)} %summarize.1), kind=kLoop, calls=%fused_computation.4 | loop fusion | flops 1024 | bytes 12289 | tf_op jit(solution)/shard_map/jit(_where)/select_n | solution.py:260
  6.4 0.0 collective-permute-start
  6.4 1.2 %collective-permute-done = f32[2,2,256]{2,1,0:T(2,128)S(1)} collective-permute-done((f32[2,2,256]{2,1,0:T(2,128)S(1)}, f32[2,2,256]{2,1,0:T(2,128)S(1)}, u32[]{:S(2)}, u32[]{:S(2)}) %collective-permute-start) | collective-permute-done | bytes 4128 | tf_op jit(solution)/shard_map/ppermute | solution.py:260
  7.5 0.7 %broadcast_select_fusion.1 = (f32[2,2,256]{2,1,0:T(2,128)S(1)}, f32[2,2,256]{2,1,0:T(2,128)S(1)}) fusion(f32[2,2,256]{2,1,0:T(2,128)S(1)} %collective-permute-done, pred[]{:T(512)S(6)} %eq.3, f32[4,2,256]{2,1,0:T(2,128)} %summarize.1), kind=kLoop, calls=%fused_computation.3 | loop fusion | flops 2048 | bytes 20481 | tf_op jit(solution)/shard_map/jit(_where)/select_n | solution.py:261
  8.3 0.7 %broadcast_in_dim.3 = f32[32,2,2,256]{3,2,1,0:T(2,128)} broadcast(f32[2,2,256]{2,1,0:T(2,128)S(1)} %pad_maximum_fusion), dimensions={1,2,3} | broadcast | bytes 135168 | tf_op jit(solution)/shard_map/broadcast_in_dim | solution.py:265
  9.0 11.7 %all-to-all-start = ((f32[32,2,2,256]{3,2,1,0:T(2,128)}), f32[32,2,2,256]{3,2,1,0:T(2,128)S(1)}, u32[]{:S(2)}, u32[]{:S(2)}) async-start(f32[32,2,2,256]{3,2,1,0:T(2,128)} %broadcast_in_dim.3), calls=%async_computation | async-start | bytes 262144 | tf_op jit(solution)/shard_map/all_to_all | solution.py:265
  20.7 0.0 copy-start
  20.7 2.2 %copy-done = f32[4,1024,256]{2,1,0:T(8,128)S(1)} copy-done((f32[4,1024,256]{2,1,0:T(8,128)S(1)}, f32[4,1024,256]{2,1,0:T(8,128)}, u32[]{:S(2)}) %copy-start) | copy-done | bytes 4194328
  22.9 0.0 copy-start.5
  22.9 1.6 %copy-done.5 = bf16[4,1024,256]{2,1,0:T(8,128)(2,1)S(1)} copy-done((bf16[4,1024,256]{2,1,0:T(8,128)(2,1)S(1)}, bf16[4,1024,256]{2,1,0:T(8,128)(2,1)}, u32[]{:S(2)}) %copy-start.5) | copy-done | bytes 2097176
  24.4 0.0 copy-start.7
  24.4 1.6 %copy-done.7 = bf16[4,1024,256]{2,1,0:T(8,128)(2,1)S(1)} copy-done((bf16[4,1024,256]{2,1,0:T(8,128)(2,1)S(1)}, bf16[4,1024,256]{2,1,0:T(8,128)(2,1)}, u32[]{:S(2)}) %copy-start.7) | copy-done | bytes 2097176
  26.0 12.8 %localize.1 = (f32[4,1024,256]{2,1,0:T(8,128)S(1)}, f32[4,1024,256]{2,1,0:T(8,128)S(1)}) custom-call(f32[4,1024,256]{2,1,0:T(8,128)S(1)} %copy-done, bf16[4,1024,256]{2,1,0:T(8,128)(2,1)S(1)} %copy-done.5, bf16[4,1024,256]{2,1,0:T(8,128)(2,1)S(1)} %copy-done.7), custom_call_target="tpu_custom_call" | custom-call | flops 4000000000 | bytes 8388608 | tf_op jit(solution)/shard_map/localize/pallas_call | solution.py:133
  38.8 0.0 copy-start.1
  38.8 1.9 %copy-done.1 = f32[4,1024,256]{2,1,0:T(8,128)} copy-done((f32[4,1024,256]{2,1,0:T(8,128)}, f32[4,1024,256]{2,1,0:T(8,128)S(1)}, u32[]{:S(2)}) %copy-start.1) | copy-done | bytes 4194328
  40.8 0.0 copy-start.3
  40.8 2.0 %copy-done.3 = f32[4,1024,256]{2,1,0:T(8,128)} copy-done((f32[4,1024,256]{2,1,0:T(8,128)}, f32[4,1024,256]{2,1,0:T(8,128)S(1)}, u32[]{:S(2)}) %copy-start.3) | copy-done | bytes 4194328
  42.8 0.0 all-to-all-done.all_ref
  42.8 0.1 entering.1
  42.9 0.1 collective-permute-start.1
  43.0 1.1 %collective-permute-done.1 = f32[2,256]{1,0:T(2,128)S(1)} collective-permute-done((f32[2,256]{1,0:T(2,128)S(1)}, f32[2,256]{1,0:T(2,128)S(1)}, u32[]{:S(2)}, u32[]{:S(2)}) %collective-permute-start.1) | collective-permute-done | bytes 2080 | tf_op jit(solution)/shard_map/ppermute | solution.py:267
  44.2 0.0 copy-start.2
  44.2 2.2 %copy-done.2 = f32[4,1024,256]{2,1,0:T(8,128)S(1)} copy-done((f32[4,1024,256]{2,1,0:T(8,128)S(1)}, f32[4,1024,256]{2,1,0:T(8,128)}, u32[]{:S(2)}) %copy-start.2) | copy-done | bytes 4194328
  46.3 0.0 copy-start.4
  46.3 2.2 %copy-done.4 = f32[4,1024,256]{2,1,0:T(8,128)S(1)} copy-done((f32[4,1024,256]{2,1,0:T(8,128)S(1)}, f32[4,1024,256]{2,1,0:T(8,128)}, u32[]{:S(2)}) %copy-start.4) | copy-done | bytes 4194328
  48.5 0.0 copy-start.6
  48.5 0.9 %gate_and_square.1 = (f32[4,1024,256]{2,1,0:T(8,128)S(1)}, f32[4,8,128]{2,1,0:T(8,128)S(1)}) custom-call(f32[4,1024,256]{2,1,0:T(8,128)S(1)} %copy-done.2, f32[4,1024,256]{2,1,0:T(8,128)S(1)} %copy-done.4, f32[4,256]{1,0:T(4,128)S(1)} %maximum_select_fusion.enter_ref), custom_call_target="tpu_custom_call" | custom-call | flops 8000000 | bytes 12582912 | tf_op jit(solution)/shard_map/gate_and_square/pallas_call | solution.py:197
  49.4 1.6 %collective-permute-start.4 = (f32[4,8,128]{2,1,0:T(8,128)S(1)}, f32[4,8,128]{2,1,0:T(8,128)S(1)}, u32[]{:S(2)}, u32[]{:S(2)}) collective-permute-start(f32[4,8,128]{2,1,0:T(8,128)S(1)} %get-tuple-element.12.p0_ref), channel_id=1, source_target_pairs={{0,3},{1,2},{2,1},{3,0},{4,7},{5,6},{6,5},{7,4},{8,11},{9,10},{10,... | collective-permute-start | bytes 49160 | tf_op jit(solution)/shard_map/ppermute | solution.py:280
  51.0 1.8 %collective-permute-start.3 = (f32[4,8,128]{2,1,0:T(8,128)S(1)}, f32[4,8,128]{2,1,0:T(8,128)S(1)}, u32[]{:S(2)}, u32[]{:S(2)}) collective-permute-start(f32[4,8,128]{2,1,0:T(8,128)S(1)} %get-tuple-element.12.p0_ref), channel_id=1, source_target_pairs={{0,1},{1,0},{2,3},{3,2},{4,5},{5,4},{6,7},{7,6},{8,9},{9,8},{10,11... | collective-permute-start | bytes 49160 | tf_op jit(solution)/shard_map/ppermute | solution.py:280
  52.8 0.2 collective-permute-start.2
  53.0 0.2 collective-permute-done.4.p3_ref
  53.3 1.5 %collective-permute-done.3.p2_ref = f32[4,8,128]{2,1,0:T(8,128)S(1)} collective-permute-done((f32[4,8,128]{2,1,0:T(8,128)S(1)}, f32[4,8,128]{2,1,0:T(8,128)S(1)}, u32[]{:S(2)}, u32[]{:S(2)}) %collective-permute-start.3) | collective-permute-done | bytes 16416 | tf_op jit(solution)/shard_map/ppermute | solution.py:280
  54.7 3.3 %collective-permute-done.2.p1_ref = f32[4,8,128]{2,1,0:T(8,128)S(1)} collective-permute-done((f32[4,8,128]{2,1,0:T(8,128)S(1)}, f32[4,8,128]{2,1,0:T(8,128)S(1)}, u32[]{:S(2)}, u32[]{:S(2)}) %collective-permute-start.2) | collective-permute-done | bytes 16416 | tf_op jit(solution)/shard_map/ppermute | solution.py:280
  58.1 0.0 copy-done.6
  58.1 2.1 %scale.1 = bf16[4,1024,256]{2,1,0:T(8,128)(2,1)} custom-call(f32[4,1024,256]{2,1,0:T(8,128)S(1)} %get-tuple-element.11.gated_ref, f32[4,8,128]{2,1,0:T(8,128)S(1)} %get-tuple-element.12.p0_ref, f32[4,8,128]{2,1,0:T(8,128)S(1)} %collective-permute-done.2.p1_ref, f32[4,8,128]{2,1,0:T(8,128)S(1)} %collective-permute-done.3.p2_ref, ...), custom_call_target="tpu_custom_call" | custom-call | flops 8000000 | bytes 6291456 | tf_op jit(solution)/shard_map/scale/pallas_call | solution.py:239
  (5 shorter events, 0.0 us)
Async XLA Ops:
  6.4 1.2 %collective-permute-start = (f32[2,2,256]{2,1,0:T(2,128)S(1)}, f32[2,2,256]{2,1,0:T(2,128)S(1)}, u32[]{:S(2)}, u32[]{:S(2)}) collective-permute-start(f32[2,2,256]{2,1,0:T(2,128)S(1)} %broadcast_select_fusion.2), channel_id=1, source_target_pairs={{0,4},{4,0},{1,5},{5,1},{2,6},{6,2},{3,7},{7,3},{8,12},{12,8},{9,1... | collective-permute-start | bytes 12296 | tf_op jit(solution)/shard_map/ppermute | solution.py:260
  9.0 33.8 %all-to-all-start = ((f32[32,2,2,256]{3,2,1,0:T(2,128)}), f32[32,2,2,256]{3,2,1,0:T(2,128)S(1)}, u32[]{:S(2)}, u32[]{:S(2)}) async-start(f32[32,2,2,256]{3,2,1,0:T(2,128)} %broadcast_in_dim.3), calls=%async_computation | async-start | bytes 262144 | tf_op jit(solution)/shard_map/all_to_all | solution.py:265
  20.7 2.2 %copy-start = (f32[4,1024,256]{2,1,0:T(8,128)S(1)}, f32[4,1024,256]{2,1,0:T(8,128)}, u32[]{:S(2)}) copy-start(f32[4,1024,256]{2,1,0:T(8,128)} %rate_hbm.3) | copy-start | bytes 12582916
  22.9 1.6 %copy-start.5 = (bf16[4,1024,256]{2,1,0:T(8,128)(2,1)S(1)}, bf16[4,1024,256]{2,1,0:T(8,128)(2,1)}, u32[]{:S(2)}) copy-start(bf16[4,1024,256]{2,1,0:T(8,128)(2,1)} %drive_hbm.3) | copy-start | bytes 6291460
  24.4 1.6 %copy-start.7 = (bf16[4,1024,256]{2,1,0:T(8,128)(2,1)S(1)}, bf16[4,1024,256]{2,1,0:T(8,128)(2,1)}, u32[]{:S(2)}) copy-start(bf16[4,1024,256]{2,1,0:T(8,128)(2,1)} %gate_hbm.1) | copy-start | bytes 6291460
  38.8 2.0 %copy-start.1 = (f32[4,1024,256]{2,1,0:T(8,128)}, f32[4,1024,256]{2,1,0:T(8,128)S(1)}, u32[]{:S(2)}) copy-start(f32[4,1024,256]{2,1,0:T(8,128)S(1)} %get-tuple-element.9.factor_ref) | copy-start | bytes 12582916
  40.8 2.0 %copy-start.3 = (f32[4,1024,256]{2,1,0:T(8,128)}, f32[4,1024,256]{2,1,0:T(8,128)S(1)}, u32[]{:S(2)}) copy-start(f32[4,1024,256]{2,1,0:T(8,128)S(1)} %get-tuple-element.10.sum_ref) | copy-start | bytes 12582916
  42.9 1.2 %collective-permute-start.1 = (f32[2,256]{1,0:T(2,128)S(1)}, f32[2,256]{1,0:T(2,128)S(1)}, u32[]{:S(2)}, u32[]{:S(2)}) collective-permute-start(f32[2,256]{1,0:T(2,128)S(1)} %broadcast_select_fusion.3), channel_id=1, source_target_pairs={{0,4},{4,0},{1,5},{5,1},{2,6},{6,2},{3,7},{7,3},{8,12},{12,8},{9,1... | collective-permute-start | bytes 6152 | tf_op jit(solution)/shard_map/ppermute | solution.py:267
  44.2 2.2 %copy-start.2 = (f32[4,1024,256]{2,1,0:T(8,128)S(1)}, f32[4,1024,256]{2,1,0:T(8,128)}, u32[]{:S(2)}) copy-start(f32[4,1024,256]{2,1,0:T(8,128)} %copy-done.1) | copy-start | bytes 12582916
  46.3 2.2 %copy-start.4 = (f32[4,1024,256]{2,1,0:T(8,128)S(1)}, f32[4,1024,256]{2,1,0:T(8,128)}, u32[]{:S(2)}) copy-start(f32[4,1024,256]{2,1,0:T(8,128)} %copy-done.3) | copy-start | bytes 12582916
  48.5 9.5 %copy-start.6 = (f32[256]{0:T(256)S(1)}, f32[256]{0:T(256)}, u32[]{:S(2)}) copy-start(f32[256]{0:T(256)} %param.7) | copy-start | bytes 3076
  49.4 3.8 %collective-permute-start.4 = (f32[4,8,128]{2,1,0:T(8,128)S(1)}, f32[4,8,128]{2,1,0:T(8,128)S(1)}, u32[]{:S(2)}, u32[]{:S(2)}) collective-permute-start(f32[4,8,128]{2,1,0:T(8,128)S(1)} %get-tuple-element.12.p0_ref), channel_id=1, source_target_pairs={{0,3},{1,2},{2,1},{3,0},{4,7},{5,6},{6,5},{7,4},{8,11},{9,10},{10,... | collective-permute-start | bytes 49160 | tf_op jit(solution)/shard_map/ppermute | solution.py:280
  51.0 3.7 %collective-permute-start.3 = (f32[4,8,128]{2,1,0:T(8,128)S(1)}, f32[4,8,128]{2,1,0:T(8,128)S(1)}, u32[]{:S(2)}, u32[]{:S(2)}) collective-permute-start(f32[4,8,128]{2,1,0:T(8,128)S(1)} %get-tuple-element.12.p0_ref), channel_id=1, source_target_pairs={{0,1},{1,0},{2,3},{3,2},{4,5},{5,4},{6,7},{7,6},{8,9},{9,8},{10,11... | collective-permute-start | bytes 49160 | tf_op jit(solution)/shard_map/ppermute | solution.py:280
  52.8 5.2 %collective-permute-start.2 = (f32[4,8,128]{2,1,0:T(8,128)S(1)}, f32[4,8,128]{2,1,0:T(8,128)S(1)}, u32[]{:S(2)}, u32[]{:S(2)}) collective-permute-start(f32[4,8,128]{2,1,0:T(8,128)S(1)} %get-tuple-element.12.p0_ref), channel_id=1, source_target_pairs={{0,2},{1,3},{2,0},{3,1},{4,6},{5,7},{6,4},{7,5},{8,10},{9,11},{10,... | collective-permute-start | bytes 49160 | tf_op jit(solution)/shard_map/ppermute | solution.py:280

commit v3 on v2

v3 whole, which is shorter than its diff:
```python
import functools
import math

import jax
import jax.numpy as jnp
from jax import lax
from jax.experimental import pallas as pl
from jax.experimental.pallas import tpu as pltpu
from jax.sharding import Mesh
from jax.sharding import PartitionSpec as P

SP = ("sp_0", "sp_1", "sp_2")
CHIPS = ("sp_0", "sp_1")
BLOCK = 128
MIB = 1 << 20
VMEM = pl.BlockSpec(memory_space=pltpu.VMEM)
HBM = pl.BlockSpec(memory_space=pltpu.HBM)


def running_sum(tri, high, low):
    return jnp.dot(tri, jnp.concatenate([high, low], axis=0), preferred_element_type=jnp.float32)


def local_kernel(
    total, rate_hbm, drive_hbm, gate_hbm, factor_ref, sum_ref, mine_ref, other_ref, rate, drive, gate, pair, tri_ref, rate_sem, drive_sem, gate_sem
):
    batch, length, channels = rate.shape
    sets = ((rate_hbm, rate, rate_sem), (drive_hbm, drive, drive_sem), (gate_hbm, gate, gate_sem))

    def copies(b):
        return [pltpu.make_async_copy(hbm.at[b], vmem.at[b], sems.at[b]) for hbm, vmem, sems in sets]

    for b in range(batch):
        for copy in copies(b):
            copy.start()
    row = lax.broadcasted_iota(jnp.int32, (BLOCK, 2 * BLOCK), 0)
    col = lax.broadcasted_iota(jnp.int32, (BLOCK, 2 * BLOCK), 1)
    tri_ref[...] = (row >= col % BLOCK).astype(jnp.bfloat16)
    to_log2 = math.log2(math.e) / total
    middle = 0.5 * total**-0.5

    def one_batch(b, _):
        for copy in copies(b):
            copy.wait()
        tri = tri_ref[...]
        lost_in = jnp.zeros((1, channels), jnp.float32)
        sum_in = jnp.zeros((1, channels), jnp.float32)
        for first in range(0, length, BLOCK):
            at = pl.ds(first, BLOCK)
            rates = rate[b, at, :]
            high = rates.astype(jnp.bfloat16)
            low = (rates - high.astype(jnp.float32)).astype(jnp.bfloat16)
            lost = running_sum(tri, high, low) * to_log2 + lost_in
            lost_in = lost[BLOCK - 1 :, :]
            opened = middle * jnp.tanh((0.5 * gate[b, at, :]).astype(jnp.float32)) + middle
            factor_ref[b, at, :] = jnp.exp2(-lost) * opened
            drives = drive[b, at, :]
            grown = ((jnp.exp2(lost) - 1.0) * drives.astype(jnp.float32)).astype(jnp.bfloat16)
            sums = running_sum(tri, drives, grown) + sum_in
            sum_in = sums[BLOCK - 1 :, :]
            sum_ref[b, at, :] = sums
        pair[b, 0:1, :] = -lost_in
        pair[b, 1:2, :] = sum_in
        return 0

    lax.fori_loop(0, batch, one_batch, 0)
    core, half = lax.axis_index("sp_2"), batch // 2
    mine_ref[...] = pair[pl.ds(core * half, half)]
    other_ref[...] = pair[pl.ds((1 - core) * half, half)]


def localize(decay_rate, drive_in, gate_in, total):
    batch, length, channels = decay_rate.shape
    big = jax.ShapeDtypeStruct(decay_rate.shape, jnp.float32)
    pair = jax.ShapeDtypeStruct((batch // 2, 2, channels), jnp.float32)
    sems = pltpu.SemaphoreType.DMA((batch,))
    return pl.pallas_call(
        functools.partial(local_kernel, total),
        out_shape=(big, big, pair, pair),
        in_specs=[HBM] * 3,
        out_specs=(VMEM,) * 4,
        scratch_shapes=[
            pltpu.VMEM(decay_rate.shape, jnp.float32),
            pltpu.VMEM(drive_in.shape, jnp.bfloat16),
            pltpu.VMEM(gate_in.shape, jnp.bfloat16),
            pltpu.VMEM((batch, 2, channels), jnp.float32),
            pltpu.VMEM((BLOCK, 2 * BLOCK), jnp.bfloat16),
            sems,
            sems,
            sems,
        ],
        compiler_params=pltpu.CompilerParams(vmem_limit_bytes=20 * MIB),
        cost_estimate=pl.CostEstimate(flops=2_000_000_000, bytes_accessed=8 * MIB, transcendentals=3 * MIB),
        name="localize",
    )(decay_rate, drive_in, gate_in)


def meet_kernel(mine_ref, got_ref, first_ref, every_ref):
    first_core = lax.axis_index("sp_2") == 0
    for p in range(mine_ref.shape[0]):
        mine, got = mine_ref[p], got_ref[p]
        first = jnp.where(first_core, mine, got)
        second = jnp.where(first_core, got, mine)
        first_ref[p] = first
        kept = first[0:1] + second[0:1]
        sums = first[1:2] + jnp.exp2(-first[0:1]) * second[1:2]
        for j in range(every_ref.shape[0]):
            every_ref[j, p, 0:1, :] = kept
            every_ref[j, p, 1:2, :] = sums


def meet(mine, got, chips):
    return pl.pallas_call(
        meet_kernel,
        out_shape=(
            jax.ShapeDtypeStruct(mine.shape, jnp.float32),
            jax.ShapeDtypeStruct((chips,) + mine.shape, jnp.float32),
        ),
        in_specs=[VMEM] * 2,
        out_specs=(VMEM,) * 2,
        compiler_params=pltpu.CompilerParams(vmem_limit_bytes=2 * MIB),
        name="meet",
    )(mine, got)


def enter_kernel(every_ref, first_ref, mine_ref, other_ref):
    chips, pairs, _, channels = every_ref.shape
    place = lax.axis_index(CHIPS)
    first_core = lax.axis_index("sp_2") == 0
    for p in range(pairs):
        state = jnp.zeros((1, channels), jnp.float32)
        for j in range(chips):
            kept = jnp.exp2(jnp.where(j < place, every_ref[j, p, 0:1, :], 0.0))
            state = kept * (state + jnp.where(j < place, every_ref[j, p, 1:2, :], 0.0))
        after = jnp.exp2(first_ref[p, 0:1, :]) * (state + first_ref[p, 1:2, :])
        mine_ref[p : p + 1, :] = jnp.where(first_core, state, after)
        other_ref[p : p + 1, :] = jnp.where(first_core, after, state)


def entering(every, first):
    chips, pairs, _, channels = every.shape
    out = jax.ShapeDtypeStruct((pairs, channels), jnp.float32)
    return pl.pallas_call(
        enter_kernel,
        out_shape=(out, out),
        in_specs=[VMEM] * 2,
        out_specs=(VMEM,) * 2,
        compiler_params=pltpu.CompilerParams(vmem_limit_bytes=2 * MIB),
        name="entering",
    )(every, first)


def gate_kernel(factor_ref, sum_ref, mine_ref, got_ref, gated_ref, power_ref):
    batch, length, channels = factor_ref.shape
    lane = lax.broadcasted_iota(jnp.int32, (8, 128), 1)
    core, half = lax.axis_index("sp_2"), batch // 2

    def one_batch(b, _):
        mine, got = mine_ref[pl.ds(b % half, 1), :], got_ref[pl.ds(b % half, 1), :]
        enter = jnp.broadcast_to(jnp.where(b // half == core, mine, got), (8, channels))
        power = jnp.zeros((8, length // 8), jnp.float32)
        for j in range(length // 8):
            at = pl.ds(8 * j, 8)
            gated = factor_ref[b, at, :] * (sum_ref[b, at, :] + enter)
            gated_ref[b, at, :] = gated
            power = jnp.where(lane == j, jnp.sum(gated * gated, axis=-1, keepdims=True), power)
        power_ref[b] = power
        return 0

    lax.fori_loop(0, batch, one_batch, 0)


def gate_and_square(factor, sums, mine, got):
    batch, length, channels = factor.shape
    return pl.pallas_call(
        gate_kernel,
        out_shape=(
            jax.ShapeDtypeStruct(factor.shape, jnp.float32),
            jax.ShapeDtypeStruct((batch, 8, length // 8), jnp.float32),
        ),
        in_specs=[VMEM] * 4,
        out_specs=(VMEM, VMEM),
        compiler_params=pltpu.CompilerParams(vmem_limit_bytes=14 * MIB),
        cost_estimate=pl.CostEstimate(flops=8_000_000, bytes_accessed=12 * MIB, transcendentals=0),
        name="gate_and_square",
    )(factor, sums, mine, got)


def scale_kernel(width, gated_ref, p0_ref, p1_ref, p2_ref, p3_ref, gain_ref, out_hbm, out, sem):
    batch, length, channels = gated_ref.shape

    def copy(b):
        return pltpu.make_async_copy(out.at[b], out_hbm.at[b], sem.at[b])

    def one_batch(b, _):
        gain = jnp.broadcast_to(gain_ref[...], (8, channels))
        power = (p0_ref[b] + p1_ref[b]) + (p2_ref[b] + p3_ref[b])
        scale = lax.rsqrt(power * (1.0 / width) + 1e-06)
        for j in range(length // 16):
            parts = []
            for k in range(2):
                column = jnp.full((8, 128), 2 * j + k, jnp.int32)
                rows = jnp.take_along_axis(scale, column, axis=1)
                rows = jnp.concatenate([rows] * (channels // 128), axis=1)
                parts.append(gated_ref[b, pl.ds(16 * j + 8 * k, 8), :] * rows * gain)
            out[b, pl.ds(16 * j, 16), :] = jnp.concatenate(parts, axis=0).astype(jnp.bfloat16)
        copy(b).start()
        return 0

    lax.fori_loop(0, batch, one_batch, 0)
    for b in range(batch):
        copy(b).wait()


def scale(gated, powers, gain, width):
    batch, length, channels = gated.shape
    return pl.pallas_call(
        functools.partial(scale_kernel, width),
        out_shape=jax.ShapeDtypeStruct(gated.shape, jnp.bfloat16),
        in_specs=[VMEM] * 6,
        out_specs=HBM,
        scratch_shapes=[pltpu.VMEM(gated.shape, jnp.bfloat16), pltpu.SemaphoreType.DMA((batch,))],
        compiler_params=pltpu.CompilerParams(vmem_limit_bytes=8 * MIB),
        cost_estimate=pl.CostEstimate(flops=8_000_000, bytes_accessed=6 * MIB, transcendentals=0),
        name="scale",
    )(gated, *powers, gain.reshape(1, channels))


def shards(decay_rate, drive_in, gate_in, norm_gain):
    total = decay_rate.shape[1] * lax.axis_size(SP)
    parts = lax.axis_size("tp")
    width = decay_rate.shape[2] * parts
    swap = [(0, 1), (1, 0)]
    decay_rate, drive_in, gate_in = (
        pltpu.with_memory_space_constraint(array, pltpu.HBM) for array in (decay_rate, drive_in, gate_in)
    )
    factor, sums, mine, other = localize(decay_rate, drive_in, gate_in, total)
    first, every = meet(mine, lax.ppermute(other, "sp_2", swap), lax.axis_size(CHIPS))
    every = lax.all_to_all(every, CHIPS, 0, 0)
    every, norm_gain = lax.optimization_barrier((every, norm_gain))
    mine, other = entering(every, first)
    gated, power = gate_and_square(factor, sums, mine, lax.ppermute(other, "sp_2", swap))
    powers = [power] + [lax.ppermute(power, "tp", [(i, i ^ k) for i in range(parts)]) for k in (2, 1, 3)]
    return scale(gated, powers, norm_gain, width)


def solution(mesh):
    torus = Mesh(mesh.devices.reshape(8, 4, 2, mesh.shape["tp"]), ("sp_0", "sp_1", "sp_2", "tp"))
    in_specs = (P(None, SP, "tp"), P(None, SP, "tp"), P(None, SP, "tp"), P("tp"))
    out_specs = P(None, SP, "tp")
    return jax.shard_map(shards, mesh=torus, in_specs=in_specs, out_specs=out_specs, check_vma=False)
```

time: 60.5 us -> 41.5 us (0.69)
  the two profiles are of different devices: /device:TPU:10 before, /device:TPU:2 now
where the time goes in v3:
time: 41.5 us; the launch traced here: 41.4 us
  blocking collectives  22.1 us (53%)
  Pallas kernels  8.12 us (20%)
  waiting for transfers between devices  7.35 us (18%)
  starting transfers between devices  3.75 us (9%)
    all_to_all x1, blocking collectives, shards(): every = lax.all_to_all(every, CHIPS, 0, 0)  22.1 us
    ppermute x3, waiting for transfers between devices, shards(): lax.ppermute(power, 'tp', [(i, i ^ k) for i in range(parts)])  5.05 us
    pallas_call x1, Pallas kernels, localize(): pl.pallas_call(functools.partial(local_kernel, total), out_shape=(big, bi...  4.98 us
    ppermute x3, starting transfers between devices, shards(): lax.ppermute(power, 'tp', [(i, i ^ k) for i in range(parts)])  3.57 us
    ppermute x2, waiting for transfers between devices, shards(): lax.ppermute(other, 'sp_2', swap)  2.3 us
    pallas_call x1, Pallas kernels, scale(): pl.pallas_call(functools.partial(scale_kernel, width), out_shape=jax.Shap...  2.05 us
    pallas_call x1, Pallas kernels, gate_and_square(): pl.pallas_call(gate_kernel, out_shape=(jax.ShapeDtypeStruct(factor.shape,...  0.92 us
  transfers between devices with their start and end apart: 5, of which 5 were waited for; matrix products, arithmetic and copies ran while one was open for 0% of the time, Pallas kernels for 0%

profile of v3, /device:TPU:2, one launch (start us, length us, event | category | flops | bytes accessed | tf_op | source)
XLA Modules:
  0.0 41.4 jit_solution(6037988308259811357)
XLA Ops:
  0.0 5.0 %localize.1 = (f32[4,1024,256]{2,1,0:T(8,128)S(1)}, f32[4,1024,256]{2,1,0:T(8,128)S(1)}, f32[2,2,256]{2,1,0:T(2,128)S(1)}, f32[2,2,256]{2,1,0:T(2,128)S(1)}) custom-call(f32[4,1024,256]{2,1,0:T(8,128)} %rate_hbm.1, bf16[4,1024,256]{2,1,0:T(8,128)(2,1)} %drive_hbm.1, bf16[4,1024,256]{2,1,0:T(8,128)(2,1)} %gate_hbm.1), custom_call_target="tpu_custom_call" | custom-call | flops 2000000000 | bytes 8388608 | tf_op jit(solution)/shard_map/localize/pallas_call | solution.py:77
  5.0 0.1 collective-permute-start
  5.1 1.2 %collective-permute-done.got_ref = f32[2,2,256]{2,1,0:T(2,128)S(1)} collective-permute-done((f32[2,2,256]{2,1,0:T(2,128)S(1)}, f32[2,2,256]{2,1,0:T(2,128)S(1)}, u32[]{:S(2)}, u32[]{:S(2)}) %collective-permute-start) | collective-permute-done | bytes 4128 | tf_op jit(solution)/shard_map/ppermute | solution.py:238
  6.3 22.1 %all_to_all.5.every_ref = f32[32,2,2,256]{3,2,1,0:T(2,128)S(1)} all-to-all(f32[32,2,2,256]{3,2,1,0:T(2,128)S(1)} %get-tuple-element.21), channel_id=1, replica_groups=mesh['sp_0'=8,'sp_1'=4,'sp_2'=2,'tp'=4] {'sp_0','sp_1'}, dimensions={0} | all-to-all | bytes 262144 | tf_op jit(solution)/shard_map/all_to_all | solution.py:239
  28.4 0.1 entering.1
  28.5 0.1 collective-permute-start.1
  28.6 1.1 %collective-permute-done.1.got_ref = f32[2,256]{1,0:T(2,128)S(1)} collective-permute-done((f32[2,256]{1,0:T(2,128)S(1)}, f32[2,256]{1,0:T(2,128)S(1)}, u32[]{:S(2)}, u32[]{:S(2)}) %collective-permute-start.1) | collective-permute-done | bytes 2080 | tf_op jit(solution)/shard_map/ppermute | solution.py:242
  29.8 0.0 copy-start
  29.8 0.9 %gate_and_square.1 = (f32[4,1024,256]{2,1,0:T(8,128)S(1)}, f32[4,8,128]{2,1,0:T(8,128)S(1)}) custom-call(f32[4,1024,256]{2,1,0:T(8,128)S(1)} %get-tuple-element.17.factor_ref, f32[4,1024,256]{2,1,0:T(8,128)S(1)} %get-tuple-element.18.sum_ref, f32[2,256]{1,0:T(2,128)S(1)} %get-tuple-element.24.mine_ref, f32[2,256]{1,0:T(2,128)S(1)} %collective-permute-done.1.got_ref), custom_call_target="tpu_custom_call" | custom-call | flops 8000000 | bytes 12582912 | tf_op jit(solution)/shard_map/gate_and_square/pallas_call | solution.py:175
  30.7 1.6 %collective-permute-start.4 = (f32[4,8,128]{2,1,0:T(8,128)S(1)}, f32[4,8,128]{2,1,0:T(8,128)S(1)}, u32[]{:S(2)}, u32[]{:S(2)}) collective-permute-start(f32[4,8,128]{2,1,0:T(8,128)S(1)} %get-tuple-element.27.p0_ref), channel_id=1, source_target_pairs={{0,3},{1,2},{2,1},{3,0},{4,7},{5,6},{6,5},{7,4},{8,11},{9,10},{10,... | collective-permute-start | bytes 49160 | tf_op jit(solution)/shard_map/ppermute | solution.py:243
  32.3 1.8 %collective-permute-start.3 = (f32[4,8,128]{2,1,0:T(8,128)S(1)}, f32[4,8,128]{2,1,0:T(8,128)S(1)}, u32[]{:S(2)}, u32[]{:S(2)}) collective-permute-start(f32[4,8,128]{2,1,0:T(8,128)S(1)} %get-tuple-element.27.p0_ref), channel_id=1, source_target_pairs={{0,1},{1,0},{2,3},{3,2},{4,5},{5,4},{6,7},{7,6},{8,9},{9,8},{10,11... | collective-permute-start | bytes 49160 | tf_op jit(solution)/shard_map/ppermute | solution.py:243
  34.1 0.2 collective-permute-start.2
  34.3 0.2 collective-permute-done.4.p3_ref
  34.5 1.5 %collective-permute-done.3.p2_ref = f32[4,8,128]{2,1,0:T(8,128)S(1)} collective-permute-done((f32[4,8,128]{2,1,0:T(8,128)S(1)}, f32[4,8,128]{2,1,0:T(8,128)S(1)}, u32[]{:S(2)}, u32[]{:S(2)}) %collective-permute-start.3) | collective-permute-done | bytes 16416 | tf_op jit(solution)/shard_map/ppermute | solution.py:243
  36.0 3.3 %collective-permute-done.2.p1_ref = f32[4,8,128]{2,1,0:T(8,128)S(1)} collective-permute-done((f32[4,8,128]{2,1,0:T(8,128)S(1)}, f32[4,8,128]{2,1,0:T(8,128)S(1)}, u32[]{:S(2)}, u32[]{:S(2)}) %collective-permute-start.2) | collective-permute-done | bytes 16416 | tf_op jit(solution)/shard_map/ppermute | solution.py:243
  39.3 0.0 copy-done
  39.3 2.1 %scale.1 = bf16[4,1024,256]{2,1,0:T(8,128)(2,1)} custom-call(f32[4,1024,256]{2,1,0:T(8,128)S(1)} %get-tuple-element.26.gated_ref, f32[4,8,128]{2,1,0:T(8,128)S(1)} %get-tuple-element.27.p0_ref, f32[4,8,128]{2,1,0:T(8,128)S(1)} %collective-permute-done.2.p1_ref, f32[4,8,128]{2,1,0:T(8,128)S(1)} %collective-permute-done.3.p2_ref, ...), custom_call_target="tpu_custom_call" | custom-call | flops 8000000 | bytes 6291456 | tf_op jit(solution)/shard_map/scale/pallas_call | solution.py:217
  (1 shorter events, 0.0 us)
Async XLA Ops:
  5.0 1.3 %collective-permute-start = (f32[2,2,256]{2,1,0:T(2,128)S(1)}, f32[2,2,256]{2,1,0:T(2,128)S(1)}, u32[]{:S(2)}, u32[]{:S(2)}) collective-permute-start(f32[2,2,256]{2,1,0:T(2,128)S(1)} %get-tuple-element.20), channel_id=1, source_target_pairs={{0,4},{4,0},{1,5},{5,1},{2,6},{6,2},{3,7},{7,3},{8,12},{12,8},{9,1... | collective-permute-start | bytes 12296 | tf_op jit(solution)/shard_map/ppermute | solution.py:238
  28.5 1.2 %collective-permute-start.1 = (f32[2,256]{1,0:T(2,128)S(1)}, f32[2,256]{1,0:T(2,128)S(1)}, u32[]{:S(2)}, u32[]{:S(2)}) collective-permute-start(f32[2,256]{1,0:T(2,128)S(1)} %get-tuple-element.25), channel_id=1, source_target_pairs={{0,4},{4,0},{1,5},{5,1},{2,6},{6,2},{3,7},{7,3},{8,12},{12,8},{9,1... | collective-permute-start | bytes 6152 | tf_op jit(solution)/shard_map/ppermute | solution.py:242
  29.8 9.6 %copy-start = (f32[256]{0:T(256)S(1)}, f32[256]{0:T(256)}, u32[]{:S(2)}) copy-start(f32[256]{0:T(256)} %param.7) | copy-start | bytes 3076
  30.7 3.8 %collective-permute-start.4 = (f32[4,8,128]{2,1,0:T(8,128)S(1)}, f32[4,8,128]{2,1,0:T(8,128)S(1)}, u32[]{:S(2)}, u32[]{:S(2)}) collective-permute-start(f32[4,8,128]{2,1,0:T(8,128)S(1)} %get-tuple-element.27.p0_ref), channel_id=1, source_target_pairs={{0,3},{1,2},{2,1},{3,0},{4,7},{5,6},{6,5},{7,4},{8,11},{9,10},{10,... | collective-permute-start | bytes 49160 | tf_op jit(solution)/shard_map/ppermute | solution.py:243
  32.3 3.7 %collective-permute-start.3 = (f32[4,8,128]{2,1,0:T(8,128)S(1)}, f32[4,8,128]{2,1,0:T(8,128)S(1)}, u32[]{:S(2)}, u32[]{:S(2)}) collective-permute-start(f32[4,8,128]{2,1,0:T(8,128)S(1)} %get-tuple-element.27.p0_ref), channel_id=1, source_target_pairs={{0,1},{1,0},{2,3},{3,2},{4,5},{5,4},{6,7},{7,6},{8,9},{9,8},{10,11... | collective-permute-start | bytes 49160 | tf_op jit(solution)/shard_map/ppermute | solution.py:243
  34.1 5.2 %collective-permute-start.2 = (f32[4,8,128]{2,1,0:T(8,128)S(1)}, f32[4,8,128]{2,1,0:T(8,128)S(1)}, u32[]{:S(2)}, u32[]{:S(2)}) collective-permute-start(f32[4,8,128]{2,1,0:T(8,128)S(1)} %get-tuple-element.27.p0_ref), channel_id=1, source_target_pairs={{0,2},{1,3},{2,0},{3,1},{4,6},{5,7},{6,4},{7,5},{8,10},{9,11},{10,... | collective-permute-start | bytes 49160 | tf_op jit(solution)/shard_map/ppermute | solution.py:243

commit v4 on v3

v4 whole, which is shorter than its diff:
```python
import functools
import math

import jax
import jax.numpy as jnp
from jax import lax
from jax.experimental import pallas as pl
from jax.experimental.pallas import tpu as pltpu
from jax.sharding import Mesh
from jax.sharding import PartitionSpec as P

SP = ("sp_0", "sp_1", "sp_2")
CHIPS = ("sp_0", "sp_1")
BLOCK = 128
MIB = 1 << 20
VMEM = pl.BlockSpec(memory_space=pltpu.VMEM)
HBM = pl.BlockSpec(memory_space=pltpu.HBM)


def local_kernel(
    total,
    rate_hbm,
    drive_hbm,
    gate_hbm,
    factor_ref,
    sum_ref,
    lost_ref,
    carry_ref,
    mine_ref,
    other_ref,
    rate,
    drive,
    gate,
    pair,
    tri_ref,
    rate_sem,
    drive_sem,
    gate_sem,
):
    batch, length, channels = rate.shape
    sets = ((rate_hbm, rate, rate_sem), (drive_hbm, drive, drive_sem), (gate_hbm, gate, gate_sem))

    def copies(b):
        return [pltpu.make_async_copy(hbm.at[b], vmem.at[b], sems.at[b]) for hbm, vmem, sems in sets]

    for b in range(batch):
        for copy in copies(b):
            copy.start()
    row = lax.broadcasted_iota(jnp.int32, (BLOCK, 2 * BLOCK), 0)
    col = lax.broadcasted_iota(jnp.int32, (BLOCK, 2 * BLOCK), 1)
    tri_ref[...] = (row >= col % BLOCK).astype(jnp.bfloat16)
    to_log2 = math.log2(math.e) / total

    def one_batch(b, _):
        for copy in copies(b):
            copy.wait()
        lost_in = jnp.zeros((1, channels), jnp.float32)
        carry = jnp.zeros((1, channels), jnp.float32)
        for k in range(length // BLOCK):
            at = pl.ds(k * BLOCK, BLOCK)
            rates = rate[b, at, :]
            lost = to_log2 * jnp.dot(
                tri_ref[:, :BLOCK], rates.astype(jnp.bfloat16), preferred_element_type=jnp.float32
            )
            opened = jnp.tanh((0.5 * gate[b, at, :]).astype(jnp.float32)) + 1.0
            factor_ref[b, at, :] = jnp.exp2(-lost) * opened
            drives = drive[b, at, :]
            grown = (jnp.exp2(lost) - 1.0).astype(jnp.bfloat16) * drives
            sums = jnp.dot(
                tri_ref[...], jnp.concatenate([drives, grown], axis=0), preferred_element_type=jnp.float32
            )
            sum_ref[b, at, :] = sums
            lost_ref[b, k : k + 1, :] = lost_in
            carry_ref[b, k : k + 1, :] = carry
            carry = carry + jnp.exp2(lost_in) * sums[BLOCK - 1 :, :]
            whole = jnp.sum(rates.reshape(BLOCK // 8, 8, channels), axis=0)
            lost_in = lost_in + to_log2 * jnp.sum(whole, axis=0, keepdims=True)
        pair[b, 0:1, :] = lost_in
        pair[b, 1:2, :] = carry
        return 0

    lax.fori_loop(0, batch, one_batch, 0)
    core, half = lax.axis_index("sp_2"), batch // 2
    mine_ref[...] = pair[pl.ds(core * half, half)]
    other_ref[...] = pair[pl.ds((1 - core) * half, half)]


def localize(decay_rate, drive_in, gate_in, total):
    batch, length, channels = decay_rate.shape
    big = jax.ShapeDtypeStruct(decay_rate.shape, jnp.float32)
    blocks = jax.ShapeDtypeStruct((batch, length // BLOCK, channels), jnp.float32)
    pair = jax.ShapeDtypeStruct((batch // 2, 2, channels), jnp.float32)
    sems = pltpu.SemaphoreType.DMA((batch,))
    return pl.pallas_call(
        functools.partial(local_kernel, total),
        out_shape=(big, big, blocks, blocks, pair, pair),
        in_specs=[HBM] * 3,
        out_specs=(VMEM,) * 6,
        scratch_shapes=[
            pltpu.VMEM(decay_rate.shape, jnp.float32),
            pltpu.VMEM(drive_in.shape, jnp.bfloat16),
            pltpu.VMEM(gate_in.shape, jnp.bfloat16),
            pltpu.VMEM((batch, 2, channels), jnp.float32),
            pltpu.VMEM((BLOCK, 2 * BLOCK), jnp.bfloat16),
            sems,
            sems,
            sems,
        ],
        compiler_params=pltpu.CompilerParams(vmem_limit_bytes=20 * MIB),
        cost_estimate=pl.CostEstimate(flops=2_000_000_000, bytes_accessed=8 * MIB, transcendentals=3 * MIB),
        name="localize",
    )(decay_rate, drive_in, gate_in)


def meet_kernel(mine_ref, got_ref, first_ref, every_ref):
    first_core = lax.axis_index("sp_2") == 0
    for p in range(mine_ref.shape[0]):
        mine, got = mine_ref[p], got_ref[p]
        first = jnp.where(first_core, mine, got)
        second = jnp.where(first_core, got, mine)
        first_ref[p] = first
        lost = first[0:1] + second[0:1]
        sums = first[1:2] + jnp.exp2(first[0:1]) * second[1:2]
        for j in range(every_ref.shape[0]):
            every_ref[j, p, 0:1, :] = lost
            every_ref[j, p, 1:2, :] = sums


def meet(mine, got, chips):
    return pl.pallas_call(
        meet_kernel,
        out_shape=(
            jax.ShapeDtypeStruct(mine.shape, jnp.float32),
            jax.ShapeDtypeStruct((chips,) + mine.shape, jnp.float32),
        ),
        in_specs=[VMEM] * 2,
        out_specs=(VMEM,) * 2,
        compiler_params=pltpu.CompilerParams(vmem_limit_bytes=2 * MIB),
        name="meet",
    )(mine, got)


def enter_kernel(every_ref, first_ref, mine_ref, other_ref):
    chips, pairs, _, channels = every_ref.shape
    place = lax.axis_index(CHIPS)
    first_core = lax.axis_index("sp_2") == 0
    for p in range(pairs):
        state = jnp.zeros((1, channels), jnp.float32)
        for j in range(chips):
            kept = jnp.exp2(-jnp.where(j < place, every_ref[j, p, 0:1, :], 0.0))
            state = kept * (state + jnp.where(j < place, every_ref[j, p, 1:2, :], 0.0))
        after = jnp.exp2(-first_ref[p, 0:1, :]) * (state + first_ref[p, 1:2, :])
        mine_ref[p : p + 1, :] = jnp.where(first_core, state, after)
        other_ref[p : p + 1, :] = jnp.where(first_core, after, state)


def entering(every, first):
    chips, pairs, _, channels = every.shape
    out = jax.ShapeDtypeStruct((pairs, channels), jnp.float32)
    return pl.pallas_call(
        enter_kernel,
        out_shape=(out, out),
        in_specs=[VMEM] * 2,
        out_specs=(VMEM,) * 2,
        compiler_params=pltpu.CompilerParams(vmem_limit_bytes=2 * MIB),
        name="entering",
    )(every, first)


def gate_kernel(mine, factor_ref, sum_ref, lost_ref, carry_ref, enter_ref, gated_ref, power_ref):
    half, length, channels = gated_ref.shape
    lane = lax.broadcasted_iota(jnp.int32, (8, length // 8), 1)
    core = lax.axis_index("sp_2")
    start = half * (core if mine else 1 - core)

    def one_batch(p, _):
        b = start + p
        enter = jnp.exp2(-lost_ref[b]) * (enter_ref[pl.ds(p, 1), :] + carry_ref[b])
        power = jnp.zeros((8, length // 8), jnp.float32)
        for k in range(length // BLOCK):
            state = jnp.broadcast_to(enter[k : k + 1, :], (8, channels))
            for j in range(k * BLOCK // 8, (k + 1) * BLOCK // 8):
                at = pl.ds(8 * j, 8)
                gated = factor_ref[b, at, :] * (sum_ref[b, at, :] + state)
                gated_ref[p, at, :] = gated
                power = jnp.where(lane == j, jnp.sum(gated * gated, axis=-1, keepdims=True), power)
        power_ref[p] = power
        return 0

    lax.fori_loop(0, half, one_batch, 0)


def gate_and_square(mine, local, enter, name):
    batch, length, channels = local[0].shape
    half = batch // 2
    return pl.pallas_call(
        functools.partial(gate_kernel, mine),
        out_shape=(
            jax.ShapeDtypeStruct((half, length, channels), jnp.float32),
            jax.ShapeDtypeStruct((half, 8, length // 8), jnp.float32),
        ),
        in_specs=[VMEM] * 5,
        out_specs=(VMEM, VMEM),
        compiler_params=pltpu.CompilerParams(vmem_limit_bytes=14 * MIB),
        cost_estimate=pl.CostEstimate(flops=4_000_000, bytes_accessed=6 * MIB, transcendentals=0),
        name=name,
    )(*local, enter)


def scale_kernel(middle, width, mine_ref, got_ref, p0_ref, p1_ref, p2_ref, p3_ref, gain_ref, out_hbm, out, sem):
    half, length, channels = mine_ref.shape
    core = lax.axis_index("sp_2")

    def copy(h, p):
        b = half * (core if h == 0 else 1 - core) + p
        return pltpu.make_async_copy(out.at[h, p], out_hbm.at[b], sem.at[h, p])

    def one_batch(p, _):
        gain = jnp.broadcast_to(gain_ref[...], (8, channels))
        for h, gated_ref in enumerate((mine_ref, got_ref)):
            power = (p0_ref[h, p] + p1_ref[h, p]) + (p2_ref[h, p] + p3_ref[h, p])
            scale = middle * lax.rsqrt(power * (middle * middle / width) + 1e-06)
            for j in range(length // 16):
                parts = []
                for k in range(2):
                    column = jnp.full((8, 128), 2 * j + k, jnp.int32)
                    rows = jnp.take_along_axis(scale, column, axis=1)
                    rows = jnp.concatenate([rows] * (channels // 128), axis=1)
                    parts.append(gated_ref[p, pl.ds(16 * j + 8 * k, 8), :] * rows * gain)
                out[h, p, pl.ds(16 * j, 16), :] = jnp.concatenate(parts, axis=0).astype(jnp.bfloat16)
            copy(h, p).start()
        return 0

    lax.fori_loop(0, half, one_batch, 0)
    for p in range(half):
        for h in range(2):
            copy(h, p).wait()


def scale(mine, got, powers, gain, middle, width):
    half, length, channels = mine.shape
    return pl.pallas_call(
        functools.partial(scale_kernel, middle, width),
        out_shape=jax.ShapeDtypeStruct((2 * half, length, channels), jnp.bfloat16),
        in_specs=[VMEM] * 7,
        out_specs=HBM,
        scratch_shapes=[pltpu.VMEM((2,) + mine.shape, jnp.bfloat16), pltpu.SemaphoreType.DMA((2, half))],
        compiler_params=pltpu.CompilerParams(vmem_limit_bytes=8 * MIB),
        cost_estimate=pl.CostEstimate(flops=8_000_000, bytes_accessed=6 * MIB, transcendentals=0),
        name="scale",
    )(mine, got, *powers, gain.reshape(1, channels))


def shards(decay_rate, drive_in, gate_in, norm_gain):
    total = decay_rate.shape[1] * lax.axis_size(SP)
    parts = lax.axis_size("tp")
    width = decay_rate.shape[2] * parts
    swap = [(0, 1), (1, 0)]
    decay_rate, drive_in, gate_in = (
        pltpu.with_memory_space_constraint(array, pltpu.HBM) for array in (decay_rate, drive_in, gate_in)
    )
    *local, mine, other = localize(decay_rate, drive_in, gate_in, total)
    first, every = meet(mine, lax.ppermute(other, "sp_2", swap), lax.axis_size(CHIPS))
    every = lax.all_to_all(every, CHIPS, 0, 0)
    every, norm_gain = lax.optimization_barrier((every, norm_gain))
    mine, other = entering(every, first)
    got = lax.ppermute(other, "sp_2", swap)
    gated_mine, power_mine = gate_and_square(True, local, mine, "gate_mine")
    gated_got, power_got = gate_and_square(False, local, got, "gate_got")
    power = jnp.stack([power_mine, power_got])
    powers = [power] + [lax.ppermute(power, "tp", [(i, i ^ k) for i in range(parts)]) for k in (1, 3, 2)]
    return scale(gated_mine, gated_got, powers, norm_gain, 0.5 * total**-0.5, width)


def solution(mesh):
    torus = Mesh(mesh.devices.reshape(8, 4, 2, mesh.shape["tp"]), ("sp_0", "sp_1", "sp_2", "tp"))
    in_specs = (P(None, SP, "tp"), P(None, SP, "tp"), P(None, SP, "tp"), P("tp"))
    out_specs = P(None, SP, "tp")
    return jax.shard_map(shards, mesh=torus, in_specs=in_specs, out_specs=out_specs, check_vma=False)
```

time: 41.5 us -> 39.6 us (0.954)
  the two profiles are of different devices: /device:TPU:2 before, /device:TPU:1 now
where the time goes in v4:
time: 39.6 us; the launch traced here: 39.5 us
  blocking collectives  18.6 us (47%)
  starting transfers between devices  9.15 us (23%)
  Pallas kernels  7.54 us (19%)
  waiting for transfers between devices  4.1 us (10%)
    all_to_all x1, blocking collectives, shards(): every = lax.all_to_all(every, CHIPS, 0, 0)  18.6 us
    pallas_call x1, Pallas kernels, localize(): pl.pallas_call(functools.partial(local_kernel, total), out_shape=(big, bi...  4.55 us
    ppermute x3, starting transfers between devices, shards(): lax.ppermute(power, 'tp', [(i, i ^ k) for i in range(parts)])  3.69 us
    ppermute x1, starting transfers between devices, shards(): lax.ppermute(other, 'sp_2', swap)  3.29 us
    ppermute x3, waiting for transfers between devices, shards(): lax.ppermute(power, 'tp', [(i, i ^ k) for i in range(parts)])  2.94 us
    ppermute x1, starting transfers between devices, shards(): got = lax.ppermute(other, 'sp_2', swap)  2.18 us
    pallas_call x1, Pallas kernels, scale(): pl.pallas_call(functools.partial(scale_kernel, middle, width), out_shape=...  1.89 us
    pallas_call x2, Pallas kernels, gate_and_square(): pl.pallas_call(functools.partial(gate_kernel, mine), out_shape=(jax.Shape...  0.93 us
  transfers between devices with their start and end apart: 5, of which 4 were waited for; matrix products, arithmetic and copies ran while one was open for 0% of the time, Pallas kernels for 1%

profile of v4, /device:TPU:1, one launch (start us, length us, event | category | flops | bytes accessed | tf_op | source)
XLA Modules:
  0.0 39.5 jit_solution(9072562385890728198)
XLA Ops:
  0.0 4.6 %localize.1 = (f32[4,1024,256]{2,1,0:T(8,128)S(1)}, f32[4,1024,256]{2,1,0:T(8,128)S(1)}, f32[4,8,256]{2,1,0:T(8,128)S(1)}, f32[4,8,256]{2,1,0:T(8,128)S(1)}, f32...) custom-call(f32[4,1024,256]{2,1,0:T(8,128)} %rate_hbm.1, bf16[4,1024,256]{2,1,0:T(8,128)(2,1)} %drive_hbm.1, ...), custom_call_target="tpu_custom_call" | custom-call | flops 2000000000 | bytes 8388608 | tf_op jit(solution)/shard_map/localize/pallas_call | solution.py:94
  4.6 3.3 %collective-permute-start = (f32[2,2,256]{2,1,0:T(2,128)S(1)}, f32[2,2,256]{2,1,0:T(2,128)S(1)}, u32[]{:S(2)}, u32[]{:S(2)}) collective-permute-start(f32[2,2,256]{2,1,0:T(2,128)S(1)} %get-tuple-element.26), channel_id=1, source_target_pairs={{0,4},{4,0},{1,5},{5,1},{2,6},{6,2},{3,7},{7,3},{8,12},{12,8},{9,1... | collective-permute-start | bytes 12296 | tf_op jit(solution)/shard_map/ppermute | solution.py:263
  7.8 0.8 %collective-permute-done.got_ref = f32[2,2,256]{2,1,0:T(2,128)S(1)} collective-permute-done((f32[2,2,256]{2,1,0:T(2,128)S(1)}, f32[2,2,256]{2,1,0:T(2,128)S(1)}, u32[]{:S(2)}, u32[]{:S(2)}) %collective-permute-start) | collective-permute-done | bytes 4128 | tf_op jit(solution)/shard_map/ppermute | solution.py:263
  8.7 18.6 %all_to_all.5.every_ref = f32[32,2,2,256]{3,2,1,0:T(2,128)S(1)} all-to-all(f32[32,2,2,256]{3,2,1,0:T(2,128)S(1)} %get-tuple-element.27), channel_id=1, replica_groups=mesh['sp_0'=8,'sp_1'=4,'sp_2'=2,'tp'=4] {'sp_0','sp_1'}, dimensions={0} | all-to-all | bytes 262144 | tf_op jit(solution)/shard_map/all_to_all | solution.py:264
  27.4 0.1 entering.1
  27.5 2.2 %collective-permute-start.1 = (f32[2,256]{1,0:T(2,128)S(1)}, f32[2,256]{1,0:T(2,128)S(1)}, u32[]{:S(2)}, u32[]{:S(2)}) collective-permute-start(f32[2,256]{1,0:T(2,128)S(1)} %get-tuple-element.32), channel_id=1, source_target_pairs={{0,4},{4,0},{1,5},{5,1},{2,6},{6,2},{3,7},{7,3},{8,12},{12,8},{9,1... | collective-permute-start | bytes 6152 | tf_op jit(solution)/shard_map/ppermute | solution.py:267
  29.7 0.5 %gate_mine.1 = (f32[2,1024,256]{2,1,0:T(8,128)S(1)}, f32[2,8,128]{2,1,0:T(8,128)S(1)}) custom-call(f32[4,1024,256]{2,1,0:T(8,128)S(1)} %get-tuple-element.21.factor_ref, f32[4,1024,256]{2,1,0:T(8,128)S(1)} %get-tuple-element.22.sum_ref, f32[4,8,256]{2,1,0:T(8,128)S(1)} %get-tuple-element.23.lost_ref, f32[4,8,256]{2,1,0:T(8,128)S(1)} %get-tuple-element.24.carry_ref, ...), custom_call_target="tpu_custom_call" | custom-call | flops 4000000 | bytes 6291456 | tf_op jit(solution)/shard_map/gate_mine/pallas_call | solution.py:196
  30.1 0.0 copy-start
  30.1 0.3 collective-permute-done.1.enter_ref
  30.5 0.5 %gate_got.1 = (f32[2,1024,256]{2,1,0:T(8,128)S(1)}, f32[2,8,128]{2,1,0:T(8,128)S(1)}) custom-call(f32[4,1024,256]{2,1,0:T(8,128)S(1)} %get-tuple-element.21.factor_ref, f32[4,1024,256]{2,1,0:T(8,128)S(1)} %get-tuple-element.22.sum_ref, f32[4,8,256]{2,1,0:T(8,128)S(1)} %get-tuple-element.23.lost_ref, f32[4,8,256]{2,1,0:T(8,128)S(1)} %get-tuple-element.24.carry_ref, ...), custom_call_target="tpu_custom_call" | custom-call | flops 4000000 | bytes 6291456 | tf_op jit(solution)/shard_map/gate_got/pallas_call | solution.py:196
  31.0 2.8 %collective-permute-start.4 = (f32[2,2,8,128]{3,2,1,0:T(8,128)S(1)}, f32[2,2,8,128]{3,2,1,0:T(8,128)S(1)}, u32[]{:S(2)}, u32[]{:S(2)}) collective-permute-start(f32[2,2,8,128]{3,2,1,0:T(8,128)S(1)} %pad_maximum_fusion.p0_ref), channel_id=1, source_target_pairs={{0,2},{1,3},{2,0},{3,1},{4,6},{5,7},{6,4},{7,5},{8,10},{9,11},{10,... | collective-permute-start | bytes 49160 | tf_op jit(solution)/shard_map/ppermute | solution.py:271
  33.8 0.9 %collective-permute-start.3 = (f32[2,2,8,128]{3,2,1,0:T(8,128)S(1)}, f32[2,2,8,128]{3,2,1,0:T(8,128)S(1)}, u32[]{:S(2)}, u32[]{:S(2)}) collective-permute-start(f32[2,2,8,128]{3,2,1,0:T(8,128)S(1)} %pad_maximum_fusion.p0_ref), channel_id=1, source_target_pairs={{0,3},{1,2},{2,1},{3,0},{4,7},{5,6},{6,5},{7,4},{8,11},{9,10},{10,... | collective-permute-start | bytes 49160 | tf_op jit(solution)/shard_map/ppermute | solution.py:271
  34.7 0.0 collective-permute-start.2
  34.7 0.5 %collective-permute-done.4.p3_ref = f32[2,2,8,128]{3,2,1,0:T(8,128)S(1)} collective-permute-done((f32[2,2,8,128]{3,2,1,0:T(8,128)S(1)}, f32[2,2,8,128]{3,2,1,0:T(8,128)S(1)}, u32[]{:S(2)}, u32[]{:S(2)}) %collective-permute-start.4) | collective-permute-done | bytes 16416 | tf_op jit(solution)/shard_map/ppermute | solution.py:271
  35.1 2.5 %collective-permute-done.3.p2_ref = f32[2,2,8,128]{3,2,1,0:T(8,128)S(1)} collective-permute-done((f32[2,2,8,128]{3,2,1,0:T(8,128)S(1)}, f32[2,2,8,128]{3,2,1,0:T(8,128)S(1)}, u32[]{:S(2)}, u32[]{:S(2)}) %collective-permute-start.3) | collective-permute-done | bytes 16416 | tf_op jit(solution)/shard_map/ppermute | solution.py:271
  37.6 0.0 collective-permute-done.2.p1_ref
  37.6 0.0 copy-done
  37.6 1.9 %scale.1 = bf16[4,1024,256]{2,1,0:T(8,128)(2,1)} custom-call(f32[2,1024,256]{2,1,0:T(8,128)S(1)} %get-tuple-element.31.mine_ref, f32[2,1024,256]{2,1,0:T(8,128)S(1)} %get-tuple-element.33.got_ref, f32[2,2,8,128]{3,2,1,0:T(8,128)S(1)} %pad_maximum_fusion.p0_ref, f32[2,2,8,128]{3,2,1,0:T(8,128)S(1)} %collective-permute-done.2.p1_ref, ...), custom_call_target="tpu_custom_call" | custom-call | flops 8000000 | bytes 6291456 | tf_op jit(solution)/shard_map/scale/pallas_call | solution.py:242
  (2 shorter events, 0.0 us)
Async XLA Ops:
  4.6 4.1 %collective-permute-start = (f32[2,2,256]{2,1,0:T(2,128)S(1)}, f32[2,2,256]{2,1,0:T(2,128)S(1)}, u32[]{:S(2)}, u32[]{:S(2)}) collective-permute-start(f32[2,2,256]{2,1,0:T(2,128)S(1)} %get-tuple-element.26), channel_id=1, source_target_pairs={{0,4},{4,0},{1,5},{5,1},{2,6},{6,2},{3,7},{7,3},{8,12},{12,8},{9,1... | collective-permute-start | bytes 12296 | tf_op jit(solution)/shard_map/ppermute | solution.py:263
  27.5 3.0 %collective-permute-start.1 = (f32[2,256]{1,0:T(2,128)S(1)}, f32[2,256]{1,0:T(2,128)S(1)}, u32[]{:S(2)}, u32[]{:S(2)}) collective-permute-start(f32[2,256]{1,0:T(2,128)S(1)} %get-tuple-element.32), channel_id=1, source_target_pairs={{0,4},{4,0},{1,5},{5,1},{2,6},{6,2},{3,7},{7,3},{8,12},{12,8},{9,1... | collective-permute-start | bytes 6152 | tf_op jit(solution)/shard_map/ppermute | solution.py:267
  30.1 7.5 %copy-start = (f32[256]{0:T(256)S(1)}, f32[256]{0:T(256)}, u32[]{:S(2)}) copy-start(f32[256]{0:T(256)} %param.7) | copy-start | bytes 3076
  31.0 4.2 %collective-permute-start.4 = (f32[2,2,8,128]{3,2,1,0:T(8,128)S(1)}, f32[2,2,8,128]{3,2,1,0:T(8,128)S(1)}, u32[]{:S(2)}, u32[]{:S(2)}) collective-permute-start(f32[2,2,8,128]{3,2,1,0:T(8,128)S(1)} %pad_maximum_fusion.p0_ref), channel_id=1, source_target_pairs={{0,2},{1,3},{2,0},{3,1},{4,6},{5,7},{6,4},{7,5},{8,10},{9,11},{10,... | collective-permute-start | bytes 49160 | tf_op jit(solution)/shard_map/ppermute | solution.py:271
  33.8 3.8 %collective-permute-start.3 = (f32[2,2,8,128]{3,2,1,0:T(8,128)S(1)}, f32[2,2,8,128]{3,2,1,0:T(8,128)S(1)}, u32[]{:S(2)}, u32[]{:S(2)}) collective-permute-start(f32[2,2,8,128]{3,2,1,0:T(8,128)S(1)} %pad_maximum_fusion.p0_ref), channel_id=1, source_target_pairs={{0,3},{1,2},{2,1},{3,0},{4,7},{5,6},{6,5},{7,4},{8,11},{9,10},{10,... | collective-permute-start | bytes 49160 | tf_op jit(solution)/shard_map/ppermute | solution.py:271
  34.7 2.9 %collective-permute-start.2 = (f32[2,2,8,128]{3,2,1,0:T(8,128)S(1)}, f32[2,2,8,128]{3,2,1,0:T(8,128)S(1)}, u32[]{:S(2)}, u32[]{:S(2)}) collective-permute-start(f32[2,2,8,128]{3,2,1,0:T(8,128)S(1)} %pad_maximum_fusion.p0_ref), channel_id=1, source_target_pairs={{0,1},{1,0},{2,3},{3,2},{4,5},{5,4},{6,7},{7,6},{8,9},{9,8},{10,11... | collective-permute-start | bytes 49160 | tf_op jit(solution)/shard_map/ppermute | solution.py:271

commit v5 on v4

--- a/solution.py
+++ b/solution.py
@@ -12,6 +12,7 @@
 SP = ("sp_0", "sp_1", "sp_2")
 CHIPS = ("sp_0", "sp_1")
 BLOCK = 128
+PIECE = 1024
 MIB = 1 << 20
 VMEM = pl.BlockSpec(memory_space=pltpu.VMEM)
 HBM = pl.BlockSpec(memory_space=pltpu.HBM)
@@ -22,15 +23,15 @@
     rate_hbm,
     drive_hbm,
     gate_hbm,
-    factor_ref,
+    kept_ref,
     sum_ref,
     lost_ref,
     carry_ref,
+    gate_ref,
     mine_ref,
     other_ref,
     rate,
     drive,
-    gate,
     pair,
     tri_ref,
     rate_sem,
@@ -38,51 +39,62 @@
     gate_sem,
 ):
     batch, length, channels = rate.shape
-    sets = ((rate_hbm, rate, rate_sem), (drive_hbm, drive, drive_sem), (gate_hbm, gate, gate_sem))
-
-    def copies(b):
-        return [pltpu.make_async_copy(hbm.at[b], vmem.at[b], sems.at[b]) for hbm, vmem, sems in sets]
+    sets = ((rate_hbm, rate, rate_sem), (drive_hbm, drive, drive_sem))
+    pieces = length // PIECE
+
+    def copies(b, i):
+        at = pl.ds(pl.multiple_of(i * PIECE, PIECE), PIECE)
+        return [
+            pltpu.make_async_copy(hbm.at[b, at, :], vmem.at[b, at, :], sems.at[b * pieces + i]) for hbm, vmem, sems in sets
+        ]
 
     for b in range(batch):
-        for copy in copies(b):
-            copy.start()
+        for i in range(pieces):
+            for copy in copies(b, i):
+                copy.start()
+    gates = [pltpu.make_async_copy(gate_hbm.at[b], gate_ref.at[b], gate_sem.at[b]) for b in range(batch)]
+    for copy in gates:
+        copy.start()
     row = lax.broadcasted_iota(jnp.int32, (BLOCK, 2 * BLOCK), 0)
     col = lax.broadcasted_iota(jnp.int32, (BLOCK, 2 * BLOCK), 1)
     tri_ref[...] = (row >= col % BLOCK).astype(jnp.bfloat16)
     to_log2 = math.log2(math.e) / total
 
-    def one_batch(b, _):
-        for copy in copies(b):
+    def one_piece(n, entered):
+        b, i = n // pieces, n % pieces
+        for copy in copies(b, i):
             copy.wait()
-        lost_in = jnp.zeros((1, channels), jnp.float32)
-        carry = jnp.zeros((1, channels), jnp.float32)
-        for k in range(length // BLOCK):
-            at = pl.ds(k * BLOCK, BLOCK)
+        lost_in, carry = (jnp.where(i == 0, 0.0, rows) for rows in entered)
+        for k in range(PIECE // BLOCK):
+            block = i * (PIECE // BLOCK) + k
+            at = pl.ds(pl.multiple_of(block * BLOCK, BLOCK), BLOCK)
             rates = rate[b, at, :]
             lost = to_log2 * jnp.dot(
                 tri_ref[:, :BLOCK], rates.astype(jnp.bfloat16), preferred_element_type=jnp.float32
             )
-            opened = jnp.tanh((0.5 * gate[b, at, :]).astype(jnp.float32)) + 1.0
-            factor_ref[b, at, :] = jnp.exp2(-lost) * opened
+            kept_ref[b, at, :] = jnp.exp2(-lost)
             drives = drive[b, at, :]
             grown = (jnp.exp2(lost) - 1.0).astype(jnp.bfloat16) * drives
             sums = jnp.dot(
                 tri_ref[...], jnp.concatenate([drives, grown], axis=0), preferred_element_type=jnp.float32
             )
             sum_ref[b, at, :] = sums
-            lost_ref[b, k : k + 1, :] = lost_in
-            carry_ref[b, k : k + 1, :] = carry
+            lost_ref[b, pl.ds(block, 1), :] = lost_in
+            carry_ref[b, pl.ds(block, 1), :] = carry
             carry = carry + jnp.exp2(lost_in) * sums[BLOCK - 1 :, :]
             whole = jnp.sum(rates.reshape(BLOCK // 8, 8, channels), axis=0)
             lost_in = lost_in + to_log2 * jnp.sum(whole, axis=0, keepdims=True)
         pair[b, 0:1, :] = lost_in
         pair[b, 1:2, :] = carry
-        return 0
-
-    lax.fori_loop(0, batch, one_batch, 0)
+        return lost_in, carry
+
+    start = jnp.zeros((1, channels), jnp.float32)
+    lax.fori_loop(0, batch * pieces, one_piece, (start, start))
     core, half = lax.axis_index("sp_2"), batch // 2
     mine_ref[...] = pair[pl.ds(core * half, half)]
     other_ref[...] = pair[pl.ds((1 - core) * half, half)]
+    for copy in gates:
+        copy.wait()
 
 
 def localize(decay_rate, drive_in, gate_in, total):
@@ -90,26 +102,51 @@
     big = jax.ShapeDtypeStruct(decay_rate.shape, jnp.float32)
     blocks = jax.ShapeDtypeStruct((batch, length // BLOCK, channels), jnp.float32)
     pair = jax.ShapeDtypeStruct((batch // 2, 2, channels), jnp.float32)
-    sems = pltpu.SemaphoreType.DMA((batch,))
+    sems = pltpu.SemaphoreType.DMA((batch * length // PIECE,))
     return pl.pallas_call(
         functools.partial(local_kernel, total),
-        out_shape=(big, big, blocks, blocks, pair, pair),
+        out_shape=(big, big, blocks, blocks, jax.ShapeDtypeStruct(gate_in.shape, gate_in.dtype), pair, pair),
         in_specs=[HBM] * 3,
-        out_specs=(VMEM,) * 6,
+        out_specs=(VMEM,) * 7,
         scratch_shapes=[
             pltpu.VMEM(decay_rate.shape, jnp.float32),
             pltpu.VMEM(drive_in.shape, jnp.bfloat16),
-            pltpu.VMEM(gate_in.shape, jnp.bfloat16),
             pltpu.VMEM((batch, 2, channels), jnp.float32),
             pltpu.VMEM((BLOCK, 2 * BLOCK), jnp.bfloat16),
             sems,
             sems,
-            sems,
+            pltpu.SemaphoreType.DMA((batch,)),
         ],
         compiler_params=pltpu.CompilerParams(vmem_limit_bytes=20 * MIB),
-        cost_estimate=pl.CostEstimate(flops=2_000_000_000, bytes_accessed=8 * MIB, transcendentals=3 * MIB),
+        cost_estimate=pl.CostEstimate(flops=2_000_000_000, bytes_accessed=8 * MIB, transcendentals=2 * MIB),
         name="localize",
     )(decay_rate, drive_in, gate_in)
+
+
+def open_kernel(kept_ref, gate_ref, factor_ref):
+    batch, length, channels = kept_ref.shape
+
+    def one_piece(n, _):
+        at = pl.ds(pl.multiple_of(n * BLOCK, BLOCK), BLOCK)
+        for b in range(batch):
+            opened = jnp.tanh((0.5 * gate_ref[b, at, :]).astype(jnp.float32)) + 1.0
+            factor_ref[b, at, :] = kept_ref[b, at, :] * opened
+        return 0
+
+    lax.fori_loop(0, length // BLOCK, one_piece, 0)
+
+
+def open_gate(kept, gate):
+    return pl.pallas_call(
+        open_kernel,
+        out_shape=jax.ShapeDtypeStruct(kept.shape, jnp.float32),
+        in_specs=[VMEM] * 2,
+        out_specs=VMEM,
+        input_output_aliases={0: 0},
+        compiler_params=pltpu.CompilerParams(vmem_limit_bytes=12 * MIB),
+        cost_estimate=pl.CostEstimate(flops=8_000_000, bytes_accessed=10 * MIB, transcendentals=MIB),
+        name="open_gate",
+    )(kept, gate)
 
 
 def meet_kernel(mine_ref, got_ref, first_ref, every_ref):
@@ -167,7 +204,7 @@
     )(every, first)
 
 
-def gate_kernel(mine, factor_ref, sum_ref, lost_ref, carry_ref, enter_ref, gated_ref, power_ref):
+def gate_kernel(mine, factor_ref, sum_ref, lost_ref, carry_ref, enter_ref, gain_ref, gated_ref, power_ref):
     half, length, channels = gated_ref.shape
     lane = lax.broadcasted_iota(jnp.int32, (8, length // 8), 1)
     core = lax.axis_index("sp_2")
@@ -176,13 +213,14 @@
     def one_batch(p, _):
         b = start + p
         enter = jnp.exp2(-lost_ref[b]) * (enter_ref[pl.ds(p, 1), :] + carry_ref[b])
+        gain = jnp.broadcast_to(gain_ref[...], (8, channels))
         power = jnp.zeros((8, length // 8), jnp.float32)
         for k in range(length // BLOCK):
             state = jnp.broadcast_to(enter[k : k + 1, :], (8, channels))
             for j in range(k * BLOCK // 8, (k + 1) * BLOCK // 8):
                 at = pl.ds(8 * j, 8)
                 gated = factor_ref[b, at, :] * (sum_ref[b, at, :] + state)
-                gated_ref[p, at, :] = gated
+                gated_ref[p, at, :] = gated * gain
                 power = jnp.where(lane == j, jnp.sum(gated * gated, axis=-1, keepdims=True), power)
         power_ref[p] = power
         return 0
@@ -190,7 +228,7 @@
     lax.fori_loop(0, half, one_batch, 0)
 
 
-def gate_and_square(mine, local, enter, name):
+def gate_and_square(mine, local, enter, gain, name):
     batch, length, channels = local[0].shape
     half = batch // 2
     return pl.pallas_call(
@@ -199,15 +237,15 @@
             jax.ShapeDtypeStruct((half, length, channels), jnp.float32),
             jax.ShapeDtypeStruct((half, 8, length // 8), jnp.float32),
         ),
-        in_specs=[VMEM] * 5,
+        in_specs=[VMEM] * 6,
         out_specs=(VMEM, VMEM),
         compiler_params=pltpu.CompilerParams(vmem_limit_bytes=14 * MIB),
         cost_estimate=pl.CostEstimate(flops=4_000_000, bytes_accessed=6 * MIB, transcendentals=0),
         name=name,
-    )(*local, enter)
-
-
-def scale_kernel(middle, width, mine_ref, got_ref, p0_ref, p1_ref, p2_ref, p3_ref, gain_ref, out_hbm, out, sem):
+    )(*local, enter, gain)
+
+
+def scale_kernel(middle, width, mine_ref, got_ref, p0_ref, p1_ref, p2_ref, p3_ref, out_hbm, out, sem):
     half, length, channels = mine_ref.shape
     core = lax.axis_index("sp_2")
 
@@ -216,7 +254,6 @@
         return pltpu.make_async_copy(out.at[h, p], out_hbm.at[b], sem.at[h, p])
 
     def one_batch(p, _):
-        gain = jnp.broadcast_to(gain_ref[...], (8, channels))
         for h, gated_ref in enumerate((mine_ref, got_ref)):
             power = (p0_ref[h, p] + p1_ref[h, p]) + (p2_ref[h, p] + p3_ref[h, p])
             scale = middle * lax.rsqrt(power * (middle * middle / width) + 1e-06)
@@ -226,7 +263,7 @@
                     column = jnp.full((8, 128), 2 * j + k, jnp.int32)
                     rows = jnp.take_along_axis(scale, column, axis=1)
                     rows = jnp.concatenate([rows] * (channels // 128), axis=1)
-                    parts.append(gated_ref[p, pl.ds(16 * j + 8 * k, 8), :] * rows * gain)
+                    parts.append(gated_ref[p, pl.ds(16 * j + 8 * k, 8), :] * rows)
                 out[h, p, pl.ds(16 * j, 16), :] = jnp.concatenate(parts, axis=0).astype(jnp.bfloat16)
             copy(h, p).start()
         return 0
@@ -237,18 +274,18 @@
             copy(h, p).wait()
 
 
-def scale(mine, got, powers, gain, middle, width):
+def scale(mine, got, powers, middle, width):
     half, length, channels = mine.shape
     return pl.pallas_call(
         functools.partial(scale_kernel, middle, width),
         out_shape=jax.ShapeDtypeStruct((2 * half, length, channels), jnp.bfloat16),
-        in_specs=[VMEM] * 7,
+        in_specs=[VMEM] * 6,
         out_specs=HBM,
         scratch_shapes=[pltpu.VMEM((2,) + mine.shape, jnp.bfloat16), pltpu.SemaphoreType.DMA((2, half))],
         compiler_params=pltpu.CompilerParams(vmem_limit_bytes=8 * MIB),
         cost_estimate=pl.CostEstimate(flops=8_000_000, bytes_accessed=6 * MIB, transcendentals=0),
         name="scale",
-    )(mine, got, *powers, gain.reshape(1, channels))
+    )(mine, got, *powers)
 
 
 def shards(decay_rate, drive_in, gate_in, norm_gain):
@@ -259,17 +296,21 @@
     decay_rate, drive_in, gate_in = (
         pltpu.with_memory_space_constraint(array, pltpu.HBM) for array in (decay_rate, drive_in, gate_in)
     )
-    *local, mine, other = localize(decay_rate, drive_in, gate_in, total)
-    first, every = meet(mine, lax.ppermute(other, "sp_2", swap), lax.axis_size(CHIPS))
+    kept, sums, lost, carry, gate, mine, other = localize(decay_rate, drive_in, gate_in, total)
+    got = lax.ppermute(other, "sp_2", swap)
+    factor = open_gate(kept, gate)
+    got, factor = lax.optimization_barrier((got, factor))
+    first, every = meet(mine, got, lax.axis_size(CHIPS))
     every = lax.all_to_all(every, CHIPS, 0, 0)
-    every, norm_gain = lax.optimization_barrier((every, norm_gain))
+    every, factor, norm_gain = lax.optimization_barrier((every, factor, norm_gain))
     mine, other = entering(every, first)
     got = lax.ppermute(other, "sp_2", swap)
-    gated_mine, power_mine = gate_and_square(True, local, mine, "gate_mine")
-    gated_got, power_got = gate_and_square(False, local, got, "gate_got")
+    local, gain = (factor, sums, lost, carry), norm_gain.reshape(1, -1)
+    gated_mine, power_mine = gate_and_square(True, local, mine, gain, "gate_mine")
+    gated_got, power_got = gate_and_square(False, local, got, gain, "gate_got")
     power = jnp.stack([power_mine, power_got])
     powers = [power] + [lax.ppermute(power, "tp", [(i, i ^ k) for i in range(parts)]) for k in (1, 3, 2)]
-    return scale(gated_mine, gated_got, powers, norm_gain, 0.5 * total**-0.5, width)
+    return scale(gated_mine, gated_got, powers, 0.5 * total**-0.5, width)
 
 
 def solution(mesh):

time: 39.6 us -> 39 us (0.985)
  waiting for transfers between devices: 4.1 us -> 3.35 us
    ppermute x1 -> x2, starting transfers between devices: 2.18 us -> 5.46 us  [shards(): got = lax.ppermute(other, 'sp_2', swap)]
    ppermute x1 -> x0, starting transfers between devices: 3.29 us -> none  [shards(): lax.ppermute(other, 'sp_2', swap)]
    ppermute x1 -> x0, waiting for transfers between devices: 0.82 us -> none  [shards(): lax.ppermute(other, 'sp_2', swap)]
    pallas_call x0 -> x1, Pallas kernels: none -> 0.7 us  [open_gate(): pl.pallas_call(open_kernel, out_shape=jax.ShapeDtypeStruct(kept.shape, jn...]
    pallas_call x1, Pallas kernels: 4.55 us -> 3.91 us  [localize(): pl.pallas_call(functools.partial(local_kernel, total), out_shape=(big, bi...]
  transfers between devices with their start and end apart: 5 -> 5, of which waited for: 4 -> 4; matrix products, arithmetic and copies ran while one was open for 0% -> 0% of each run, Pallas kernels for 1% -> 3%
where the time goes in v5:
time: 39 us; the launch traced here: 38.9 us
  blocking collectives  18.6 us (48%)
  starting transfers between devices  9.16 us (23%)
  Pallas kernels  7.71 us (20%)
  waiting for transfers between devices  3.35 us (9%)
    all_to_all x1, blocking collectives, shards(): every = lax.all_to_all(every, CHIPS, 0, 0)  18.6 us
    ppermute x2, starting transfers between devices, shards(): got = lax.ppermute(other, 'sp_2', swap)  5.46 us
    pallas_call x1, Pallas kernels, localize(): pl.pallas_call(functools.partial(local_kernel, total), out_shape=(big, bi...  3.91 us
    ppermute x3, starting transfers between devices, shards(): lax.ppermute(power, 'tp', [(i, i ^ k) for i in range(parts)])  3.69 us
    ppermute x3, waiting for transfers between devices, shards(): lax.ppermute(power, 'tp', [(i, i ^ k) for i in range(parts)])  2.94 us
    pallas_call x1, Pallas kernels, scale(): pl.pallas_call(functools.partial(scale_kernel, middle, width), out_shape=...  1.89 us
    pallas_call x2, Pallas kernels, gate_and_square(): pl.pallas_call(functools.partial(gate_kernel, mine), out_shape=(jax.Shape...  1.06 us
  transfers between devices with their start and end apart: 5, of which 4 were waited for; matrix products, arithmetic and copies ran while one was open for 0% of the time, Pallas kernels for 3%

profile of v5, /device:TPU:1, one launch (start us, length us, event | category | flops | bytes accessed | tf_op | source)
XLA Modules:
  0.0 38.9 jit_solution(11322501780062803339)
XLA Ops:
  0.0 3.9 %localize.1 = (f32[4,1024,256]{2,1,0:T(8,128)S(1)}, f32[4,1024,256]{2,1,0:T(8,128)S(1)}, f32[4,8,256]{2,1,0:T(8,128)S(1)}, f32[4,8,256]{2,1,0:T(8,128)S(1)}, bf1...) custom-call(f32[4,1024,256]{2,1,0:T(8,128)} %rate_hbm.1, ...), custom_call_target="tpu_custom_call" | custom-call | flops 2000000000 | bytes 8388608 | tf_op jit(solution)/shard_map/localize/pallas_call | solution.py:106
  3.9 3.3 %collective-permute-start = (f32[2,2,256]{2,1,0:T(2,128)S(1)}, f32[2,2,256]{2,1,0:T(2,128)S(1)}, u32[]{:S(2)}, u32[]{:S(2)}) collective-permute-start(f32[2,2,256]{2,1,0:T(2,128)S(1)} %get-tuple-element.26), channel_id=1, source_target_pairs={{0,4},{4,0},{1,5},{5,1},{2,6},{6,2},{3,7},{7,3},{8,12},{12,8},{9,1... | collective-permute-start | bytes 12296 | tf_op jit(solution)/shard_map/ppermute | solution.py:300
  7.2 0.0 copy-start
  7.2 0.7 %open_gate.1.factor_ref = f32[4,1024,256]{2,1,0:T(8,128)S(1)} custom-call(f32[4,1024,256]{2,1,0:T(8,128)S(1)} %get-tuple-element.27.kept_ref, bf16[4,1024,256]{2,1,0:T(8,128)(2,1)S(1)} %get-tuple-element.28.gate_ref), custom_call_target="tpu_custom_call", output_to_operand_aliasing={{}: (0, {})} | custom-call | flops 8000000 | bytes 10485760 | tf_op jit(solution)/shard_map/open_gate/pallas_call | solution.py:140
  7.9 0.1 collective-permute-done.got_ref
  8.1 18.6 %all_to_all.5.every_ref = f32[32,2,2,256]{3,2,1,0:T(2,128)S(1)} all-to-all(f32[32,2,2,256]{3,2,1,0:T(2,128)S(1)} %get-tuple-element.30), channel_id=1, replica_groups=mesh['sp_0'=8,'sp_1'=4,'sp_2'=2,'tp'=4] {'sp_0','sp_1'}, dimensions={0} | all-to-all | bytes 262144 | tf_op jit(solution)/shard_map/all_to_all | solution.py:304
  26.7 0.1 entering.1
  26.8 2.2 %collective-permute-start.1 = (f32[2,256]{1,0:T(2,128)S(1)}, f32[2,256]{1,0:T(2,128)S(1)}, u32[]{:S(2)}, u32[]{:S(2)}) collective-permute-start(f32[2,256]{1,0:T(2,128)S(1)} %get-tuple-element.41), channel_id=1, source_target_pairs={{0,4},{4,0},{1,5},{5,1},{2,6},{6,2},{3,7},{7,3},{8,12},{12,8},{9,1... | collective-permute-start | bytes 6152 | tf_op jit(solution)/shard_map/ppermute | solution.py:307
  29.0 0.0 copy-done
  29.0 0.5 %gate_mine.1 = (f32[2,1024,256]{2,1,0:T(8,128)S(1)}, f32[2,8,128]{2,1,0:T(8,128)S(1)}) custom-call(f32[4,1024,256]{2,1,0:T(8,128)S(1)} %open_gate.1.factor_ref, f32[4,1024,256]{2,1,0:T(8,128)S(1)} %get-tuple-element.33.sum_ref, f32[4,8,256]{2,1,0:T(8,128)S(1)} %get-tuple-element.34.lost_ref, f32[4,8,256]{2,1,0:T(8,128)S(1)} %get-tuple-element.35.carry_ref, ...), custom_call_target="tpu_custom_call" | custom-call | flops 4000000 | bytes 6291456 | tf_op jit(solution)/shard_map/gate_mine/pallas_call | solution.py:234
  29.5 0.3 collective-permute-done.1.enter_ref
  29.8 0.5 %gate_got.1 = (f32[2,1024,256]{2,1,0:T(8,128)S(1)}, f32[2,8,128]{2,1,0:T(8,128)S(1)}) custom-call(f32[4,1024,256]{2,1,0:T(8,128)S(1)} %open_gate.1.factor_ref, f32[4,1024,256]{2,1,0:T(8,128)S(1)} %get-tuple-element.33.sum_ref, f32[4,8,256]{2,1,0:T(8,128)S(1)} %get-tuple-element.34.lost_ref, f32[4,8,256]{2,1,0:T(8,128)S(1)} %get-tuple-element.35.carry_ref, ...), custom_call_target="tpu_custom_call" | custom-call | flops 4000000 | bytes 6291456 | tf_op jit(solution)/shard_map/gate_got/pallas_call | solution.py:234
  30.4 2.8 %collective-permute-start.4 = (f32[2,2,8,128]{3,2,1,0:T(8,128)S(1)}, f32[2,2,8,128]{3,2,1,0:T(8,128)S(1)}, u32[]{:S(2)}, u32[]{:S(2)}) collective-permute-start(f32[2,2,8,128]{3,2,1,0:T(8,128)S(1)} %pad_maximum_fusion.p0_ref), channel_id=1, source_target_pairs={{0,2},{1,3},{2,0},{3,1},{4,6},{5,7},{6,4},{7,5},{8,10},{9,11},{10,... | collective-permute-start | bytes 49160 | tf_op jit(solution)/shard_map/ppermute | solution.py:312
  33.2 0.9 %collective-permute-start.3 = (f32[2,2,8,128]{3,2,1,0:T(8,128)S(1)}, f32[2,2,8,128]{3,2,1,0:T(8,128)S(1)}, u32[]{:S(2)}, u32[]{:S(2)}) collective-permute-start(f32[2,2,8,128]{3,2,1,0:T(8,128)S(1)} %pad_maximum_fusion.p0_ref), channel_id=1, source_target_pairs={{0,3},{1,2},{2,1},{3,0},{4,7},{5,6},{6,5},{7,4},{8,11},{9,10},{10,... | collective-permute-start | bytes 49160 | tf_op jit(solution)/shard_map/ppermute | solution.py:312
  34.1 0.0 collective-permute-start.2
  34.1 0.5 %collective-permute-done.4.p3_ref = f32[2,2,8,128]{3,2,1,0:T(8,128)S(1)} collective-permute-done((f32[2,2,8,128]{3,2,1,0:T(8,128)S(1)}, f32[2,2,8,128]{3,2,1,0:T(8,128)S(1)}, u32[]{:S(2)}, u32[]{:S(2)}) %collective-permute-start.4) | collective-permute-done | bytes 16416 | tf_op jit(solution)/shard_map/ppermute | solution.py:312
  34.6 2.5 %collective-permute-done.3.p2_ref = f32[2,2,8,128]{3,2,1,0:T(8,128)S(1)} collective-permute-done((f32[2,2,8,128]{3,2,1,0:T(8,128)S(1)}, f32[2,2,8,128]{3,2,1,0:T(8,128)S(1)}, u32[]{:S(2)}, u32[]{:S(2)}) %collective-permute-start.3) | collective-permute-done | bytes 16416 | tf_op jit(solution)/shard_map/ppermute | solution.py:312
  37.0 0.0 collective-permute-done.2.p1_ref
  37.0 1.9 %scale.1 = bf16[4,1024,256]{2,1,0:T(8,128)(2,1)} custom-call(f32[2,1024,256]{2,1,0:T(8,128)S(1)} %get-tuple-element.40.mine_ref, f32[2,1024,256]{2,1,0:T(8,128)S(1)} %get-tuple-element.42.got_ref, f32[2,2,8,128]{3,2,1,0:T(8,128)S(1)} %pad_maximum_fusion.p0_ref, f32[2,2,8,128]{3,2,1,0:T(8,128)S(1)} %collective-permute-done.2.p1_ref, ...), custom_call_target="tpu_custom_call" | custom-call | flops 8000000 | bytes 6291456 | tf_op jit(solution)/shard_map/scale/pallas_call | solution.py:279
  (2 shorter events, 0.0 us)
Async XLA Ops:
  3.9 4.1 %collective-permute-start = (f32[2,2,256]{2,1,0:T(2,128)S(1)}, f32[2,2,256]{2,1,0:T(2,128)S(1)}, u32[]{:S(2)}, u32[]{:S(2)}) collective-permute-start(f32[2,2,256]{2,1,0:T(2,128)S(1)} %get-tuple-element.26), channel_id=1, source_target_pairs={{0,4},{4,0},{1,5},{5,1},{2,6},{6,2},{3,7},{7,3},{8,12},{12,8},{9,1... | collective-permute-start | bytes 12296 | tf_op jit(solution)/shard_map/ppermute | solution.py:300
  7.2 21.8 %copy-start = (f32[256]{0:T(256)S(1)}, f32[256]{0:T(256)}, u32[]{:S(2)}) copy-start(f32[256]{0:T(256)} %param.7) | copy-start | bytes 3076
  26.8 3.0 %collective-permute-start.1 = (f32[2,256]{1,0:T(2,128)S(1)}, f32[2,256]{1,0:T(2,128)S(1)}, u32[]{:S(2)}, u32[]{:S(2)}) collective-permute-start(f32[2,256]{1,0:T(2,128)S(1)} %get-tuple-element.41), channel_id=1, source_target_pairs={{0,4},{4,0},{1,5},{5,1},{2,6},{6,2},{3,7},{7,3},{8,12},{12,8},{9,1... | collective-permute-start | bytes 6152 | tf_op jit(solution)/shard_map/ppermute | solution.py:307
  30.4 4.2 %collective-permute-start.4 = (f32[2,2,8,128]{3,2,1,0:T(8,128)S(1)}, f32[2,2,8,128]{3,2,1,0:T(8,128)S(1)}, u32[]{:S(2)}, u32[]{:S(2)}) collective-permute-start(f32[2,2,8,128]{3,2,1,0:T(8,128)S(1)} %pad_maximum_fusion.p0_ref), channel_id=1, source_target_pairs={{0,2},{1,3},{2,0},{3,1},{4,6},{5,7},{6,4},{7,5},{8,10},{9,11},{10,... | collective-permute-start | bytes 49160 | tf_op jit(solution)/shard_map/ppermute | solution.py:312
  33.2 3.8 %collective-permute-start.3 = (f32[2,2,8,128]{3,2,1,0:T(8,128)S(1)}, f32[2,2,8,128]{3,2,1,0:T(8,128)S(1)}, u32[]{:S(2)}, u32[]{:S(2)}) collective-permute-start(f32[2,2,8,128]{3,2,1,0:T(8,128)S(1)} %pad_maximum_fusion.p0_ref), channel_id=1, source_target_pairs={{0,3},{1,2},{2,1},{3,0},{4,7},{5,6},{6,5},{7,4},{8,11},{9,10},{10,... | collective-permute-start | bytes 49160 | tf_op jit(solution)/shard_map/ppermute | solution.py:312
  34.1 2.9 %collective-permute-start.2 = (f32[2,2,8,128]{3,2,1,0:T(8,128)S(1)}, f32[2,2,8,128]{3,2,1,0:T(8,128)S(1)}, u32[]{:S(2)}, u32[]{:S(2)}) collective-permute-start(f32[2,2,8,128]{3,2,1,0:T(8,128)S(1)} %pad_maximum_fusion.p0_ref), channel_id=1, source_target_pairs={{0,1},{1,0},{2,3},{3,2},{4,5},{5,4},{6,7},{7,6},{8,9},{9,8},{10,11... | collective-permute-start | bytes 49160 | tf_op jit(solution)/shard_map/ppermute | solution.py:312

commit v6 on v5

--- a/solution.py
+++ b/solution.py
@@ -13,6 +13,7 @@
 CHIPS = ("sp_0", "sp_1")
 BLOCK = 128
 PIECE = 1024
+LEAVING = 256
 MIB = 1 << 20
 VMEM = pl.BlockSpec(memory_space=pltpu.VMEM)
 HBM = pl.BlockSpec(memory_space=pltpu.HBM)
@@ -210,7 +211,7 @@
     core = lax.axis_index("sp_2")
     start = half * (core if mine else 1 - core)
 
-    def one_batch(p, _):
+    for p in range(half):
         b = start + p
         enter = jnp.exp2(-lost_ref[b]) * (enter_ref[pl.ds(p, 1), :] + carry_ref[b])
         gain = jnp.broadcast_to(gain_ref[...], (8, channels))
@@ -223,9 +224,6 @@
                 gated_ref[p, at, :] = gated * gain
                 power = jnp.where(lane == j, jnp.sum(gated * gated, axis=-1, keepdims=True), power)
         power_ref[p] = power
-        return 0
-
-    lax.fori_loop(0, half, one_batch, 0)
 
 
 def gate_and_square(mine, local, enter, gain, name):
@@ -248,30 +246,33 @@
 def scale_kernel(middle, width, mine_ref, got_ref, p0_ref, p1_ref, p2_ref, p3_ref, out_hbm, out, sem):
     half, length, channels = mine_ref.shape
     core = lax.axis_index("sp_2")
-
-    def copy(h, p):
+    which = [(h, p) for h in range(2) for p in range(half)]
+
+    def copy(h, p, i):
         b = half * (core if h == 0 else 1 - core) + p
-        return pltpu.make_async_copy(out.at[h, p], out_hbm.at[b], sem.at[h, p])
-
-    def one_batch(p, _):
-        for h, gated_ref in enumerate((mine_ref, got_ref)):
-            power = (p0_ref[h, p] + p1_ref[h, p]) + (p2_ref[h, p] + p3_ref[h, p])
-            scale = middle * lax.rsqrt(power * (middle * middle / width) + 1e-06)
-            for j in range(length // 16):
+        at = pl.ds(i * LEAVING, LEAVING)
+        return pltpu.make_async_copy(out.at[h, p, at, :], out_hbm.at[b, at, :], sem.at[(h * half + p) * (length // LEAVING) + i])
+
+    lane = lax.broadcasted_iota(jnp.int32, (8, length // 8), 1)
+    scales = []
+    for h, p in which:
+        power = (p0_ref[h, p] + p1_ref[h, p]) + (p2_ref[h, p] + p3_ref[h, p])
+        scales.append(middle * lax.rsqrt(power * (middle * middle / width) + 1e-06))
+    for i in range(length // LEAVING):
+        for j in range(i * LEAVING // 16, (i + 1) * LEAVING // 16):
+            columns = [lane == 2 * j + k for k in range(2)]
+            for (h, p), scale in zip(which, scales):
+                gated_ref = (mine_ref, got_ref)[h]
                 parts = []
-                for k in range(2):
-                    column = jnp.full((8, 128), 2 * j + k, jnp.int32)
-                    rows = jnp.take_along_axis(scale, column, axis=1)
-                    rows = jnp.concatenate([rows] * (channels // 128), axis=1)
+                for k, column in enumerate(columns):
+                    rows = jnp.sum(jnp.where(column, scale, 0.0), axis=-1, keepdims=True)
                     parts.append(gated_ref[p, pl.ds(16 * j + 8 * k, 8), :] * rows)
                 out[h, p, pl.ds(16 * j, 16), :] = jnp.concatenate(parts, axis=0).astype(jnp.bfloat16)
-            copy(h, p).start()
-        return 0
-
-    lax.fori_loop(0, half, one_batch, 0)
-    for p in range(half):
-        for h in range(2):
-            copy(h, p).wait()
+        for h, p in which:
+            copy(h, p, i).start()
+    for i in range(length // LEAVING):
+        for h, p in which:
+            copy(h, p, i).wait()
 
 
 def scale(mine, got, powers, middle, width):
@@ -281,7 +282,7 @@
         out_shape=jax.ShapeDtypeStruct((2 * half, length, channels), jnp.bfloat16),
         in_specs=[VMEM] * 6,
         out_specs=HBM,
-        scratch_shapes=[pltpu.VMEM((2,) + mine.shape, jnp.bfloat16), pltpu.SemaphoreType.DMA((2, half))],
+        scratch_shapes=[pltpu.VMEM((2,) + mine.shape, jnp.bfloat16), pltpu.SemaphoreType.DMA((2 * half * length // LEAVING,))],
         compiler_params=pltpu.CompilerParams(vmem_limit_bytes=8 * MIB),
         cost_estimate=pl.CostEstimate(flops=8_000_000, bytes_accessed=6 * MIB, transcendentals=0),
         name="scale",

time: 39 us -> 38.7 us (level)
  no operation moved by 1% of the time
where the time goes in v6:
time: 38.7 us; the launch traced here: 38.6 us
  blocking collectives  18.6 us (48%)
  starting transfers between devices  9.16 us (24%)
  Pallas kernels  7.33 us (19%)
  waiting for transfers between devices  3.42 us (9%)
    all_to_all x1, blocking collectives, shards(): every = lax.all_to_all(every, CHIPS, 0, 0)  18.6 us
    ppermute x2, starting transfers between devices, shards(): got = lax.ppermute(other, 'sp_2', swap)  5.46 us
    pallas_call x1, Pallas kernels, localize(): pl.pallas_call(functools.partial(local_kernel, total), out_shape=(big, bi...  3.91 us
    ppermute x3, starting transfers between devices, shards(): lax.ppermute(power, 'tp', [(i, i ^ k) for i in range(parts)])  3.69 us
    ppermute x3, waiting for transfers between devices, shards(): lax.ppermute(power, 'tp', [(i, i ^ k) for i in range(parts)])  2.94 us
    pallas_call x1, Pallas kernels, scale(): pl.pallas_call(functools.partial(scale_kernel, middle, width), out_shape=...  1.66 us
    pallas_call x2, Pallas kernels, gate_and_square(): pl.pallas_call(functools.partial(gate_kernel, mine), out_shape=(jax.Shape...  0.91 us
  transfers between devices with their start and end apart: 5, of which 4 were waited for; matrix products, arithmetic and copies ran while one was open for 0% of the time, Pallas kernels for 3%

profile of v6, /device:TPU:1, one launch (start us, length us, event | category | flops | bytes accessed | tf_op | source)
XLA Modules:
  0.0 38.6 jit_solution(16627605000527001555)
XLA Ops:
  0.0 3.9 %localize.1 = (f32[4,1024,256]{2,1,0:T(8,128)S(1)}, f32[4,1024,256]{2,1,0:T(8,128)S(1)}, f32[4,8,256]{2,1,0:T(8,128)S(1)}, f32[4,8,256]{2,1,0:T(8,128)S(1)}, bf1...) custom-call(f32[4,1024,256]{2,1,0:T(8,128)} %rate_hbm.1, ...), custom_call_target="tpu_custom_call" | custom-call | flops 2000000000 | bytes 8388608 | tf_op jit(solution)/shard_map/localize/pallas_call | solution.py:107
  3.9 3.3 %collective-permute-start = (f32[2,2,256]{2,1,0:T(2,128)S(1)}, f32[2,2,256]{2,1,0:T(2,128)S(1)}, u32[]{:S(2)}, u32[]{:S(2)}) collective-permute-start(f32[2,2,256]{2,1,0:T(2,128)S(1)} %get-tuple-element.26), channel_id=1, source_target_pairs={{0,4},{4,0},{1,5},{5,1},{2,6},{6,2},{3,7},{7,3},{8,12},{12,8},{9,1... | collective-permute-start | bytes 12296 | tf_op jit(solution)/shard_map/ppermute | solution.py:301
  7.2 0.0 copy-start
  7.2 0.7 %open_gate.1.factor_ref = f32[4,1024,256]{2,1,0:T(8,128)S(1)} custom-call(f32[4,1024,256]{2,1,0:T(8,128)S(1)} %get-tuple-element.27.kept_ref, bf16[4,1024,256]{2,1,0:T(8,128)(2,1)S(1)} %get-tuple-element.28.gate_ref), custom_call_target="tpu_custom_call", output_to_operand_aliasing={{}: (0, {})} | custom-call | flops 8000000 | bytes 10485760 | tf_op jit(solution)/shard_map/open_gate/pallas_call | solution.py:141
  7.9 0.1 collective-permute-done.got_ref
  8.1 18.6 %all_to_all.5.every_ref = f32[32,2,2,256]{3,2,1,0:T(2,128)S(1)} all-to-all(f32[32,2,2,256]{3,2,1,0:T(2,128)S(1)} %get-tuple-element.30), channel_id=1, replica_groups=mesh['sp_0'=8,'sp_1'=4,'sp_2'=2,'tp'=4] {'sp_0','sp_1'}, dimensions={0} | all-to-all | bytes 262144 | tf_op jit(solution)/shard_map/all_to_all | solution.py:305
  26.7 0.1 entering.1
  26.8 2.2 %collective-permute-start.1 = (f32[2,256]{1,0:T(2,128)S(1)}, f32[2,256]{1,0:T(2,128)S(1)}, u32[]{:S(2)}, u32[]{:S(2)}) collective-permute-start(f32[2,256]{1,0:T(2,128)S(1)} %get-tuple-element.41), channel_id=1, source_target_pairs={{0,4},{4,0},{1,5},{5,1},{2,6},{6,2},{3,7},{7,3},{8,12},{12,8},{9,1... | collective-permute-start | bytes 6152 | tf_op jit(solution)/shard_map/ppermute | solution.py:308
  29.0 0.0 copy-done
  29.0 0.5 %gate_mine.1 = (f32[2,1024,256]{2,1,0:T(8,128)S(1)}, f32[2,8,128]{2,1,0:T(8,128)S(1)}) custom-call(f32[4,1024,256]{2,1,0:T(8,128)S(1)} %open_gate.1.factor_ref, f32[4,1024,256]{2,1,0:T(8,128)S(1)} %get-tuple-element.33.sum_ref, f32[4,8,256]{2,1,0:T(8,128)S(1)} %get-tuple-element.34.lost_ref, f32[4,8,256]{2,1,0:T(8,128)S(1)} %get-tuple-element.35.carry_ref, ...), custom_call_target="tpu_custom_call" | custom-call | flops 4000000 | bytes 6291456 | tf_op jit(solution)/shard_map/gate_mine/pallas_call | solution.py:232
  29.5 0.4 collective-permute-done.1.enter_ref
  29.8 0.5 %gate_got.1 = (f32[2,1024,256]{2,1,0:T(8,128)S(1)}, f32[2,8,128]{2,1,0:T(8,128)S(1)}) custom-call(f32[4,1024,256]{2,1,0:T(8,128)S(1)} %open_gate.1.factor_ref, f32[4,1024,256]{2,1,0:T(8,128)S(1)} %get-tuple-element.33.sum_ref, f32[4,8,256]{2,1,0:T(8,128)S(1)} %get-tuple-element.34.lost_ref, f32[4,8,256]{2,1,0:T(8,128)S(1)} %get-tuple-element.35.carry_ref, ...), custom_call_target="tpu_custom_call" | custom-call | flops 4000000 | bytes 6291456 | tf_op jit(solution)/shard_map/gate_got/pallas_call | solution.py:232
  30.3 2.8 %collective-permute-start.4 = (f32[2,2,8,128]{3,2,1,0:T(8,128)S(1)}, f32[2,2,8,128]{3,2,1,0:T(8,128)S(1)}, u32[]{:S(2)}, u32[]{:S(2)}) collective-permute-start(f32[2,2,8,128]{3,2,1,0:T(8,128)S(1)} %pad_maximum_fusion.p0_ref), channel_id=1, source_target_pairs={{0,2},{1,3},{2,0},{3,1},{4,6},{5,7},{6,4},{7,5},{8,10},{9,11},{10,... | collective-permute-start | bytes 49160 | tf_op jit(solution)/shard_map/ppermute | solution.py:313
  33.1 0.9 %collective-permute-start.3 = (f32[2,2,8,128]{3,2,1,0:T(8,128)S(1)}, f32[2,2,8,128]{3,2,1,0:T(8,128)S(1)}, u32[]{:S(2)}, u32[]{:S(2)}) collective-permute-start(f32[2,2,8,128]{3,2,1,0:T(8,128)S(1)} %pad_maximum_fusion.p0_ref), channel_id=1, source_target_pairs={{0,3},{1,2},{2,1},{3,0},{4,7},{5,6},{6,5},{7,4},{8,11},{9,10},{10,... | collective-permute-start | bytes 49160 | tf_op jit(solution)/shard_map/ppermute | solution.py:313
  34.0 0.0 collective-permute-start.2
  34.0 0.5 %collective-permute-done.4.p3_ref = f32[2,2,8,128]{3,2,1,0:T(8,128)S(1)} collective-permute-done((f32[2,2,8,128]{3,2,1,0:T(8,128)S(1)}, f32[2,2,8,128]{3,2,1,0:T(8,128)S(1)}, u32[]{:S(2)}, u32[]{:S(2)}) %collective-permute-start.4) | collective-permute-done | bytes 16416 | tf_op jit(solution)/shard_map/ppermute | solution.py:313
  34.5 2.5 %collective-permute-done.3.p2_ref = f32[2,2,8,128]{3,2,1,0:T(8,128)S(1)} collective-permute-done((f32[2,2,8,128]{3,2,1,0:T(8,128)S(1)}, f32[2,2,8,128]{3,2,1,0:T(8,128)S(1)}, u32[]{:S(2)}, u32[]{:S(2)}) %collective-permute-start.3) | collective-permute-done | bytes 16416 | tf_op jit(solution)/shard_map/ppermute | solution.py:313
  36.9 0.0 collective-permute-done.2.p1_ref
  36.9 1.7 %scale.1 = bf16[4,1024,256]{2,1,0:T(8,128)(2,1)} custom-call(f32[2,1024,256]{2,1,0:T(8,128)S(1)} %get-tuple-element.40.mine_ref, f32[2,1024,256]{2,1,0:T(8,128)S(1)} %get-tuple-element.42.got_ref, f32[2,2,8,128]{3,2,1,0:T(8,128)S(1)} %pad_maximum_fusion.p0_ref, f32[2,2,8,128]{3,2,1,0:T(8,128)S(1)} %collective-permute-done.2.p1_ref, ...), custom_call_target="tpu_custom_call" | custom-call | flops 8000000 | bytes 6291456 | tf_op jit(solution)/shard_map/scale/pallas_call | solution.py:280
  (2 shorter events, 0.1 us)
Async XLA Ops:
  3.9 4.1 %collective-permute-start = (f32[2,2,256]{2,1,0:T(2,128)S(1)}, f32[2,2,256]{2,1,0:T(2,128)S(1)}, u32[]{:S(2)}, u32[]{:S(2)}) collective-permute-start(f32[2,2,256]{2,1,0:T(2,128)S(1)} %get-tuple-element.26), channel_id=1, source_target_pairs={{0,4},{4,0},{1,5},{5,1},{2,6},{6,2},{3,7},{7,3},{8,12},{12,8},{9,1... | collective-permute-start | bytes 12296 | tf_op jit(solution)/shard_map/ppermute | solution.py:301
  7.2 21.8 %copy-start = (f32[256]{0:T(256)S(1)}, f32[256]{0:T(256)}, u32[]{:S(2)}) copy-start(f32[256]{0:T(256)} %param.7) | copy-start | bytes 3076
  26.8 3.0 %collective-permute-start.1 = (f32[2,256]{1,0:T(2,128)S(1)}, f32[2,256]{1,0:T(2,128)S(1)}, u32[]{:S(2)}, u32[]{:S(2)}) collective-permute-start(f32[2,256]{1,0:T(2,128)S(1)} %get-tuple-element.41), channel_id=1, source_target_pairs={{0,4},{4,0},{1,5},{5,1},{2,6},{6,2},{3,7},{7,3},{8,12},{12,8},{9,1... | collective-permute-start | bytes 6152 | tf_op jit(solution)/shard_map/ppermute | solution.py:308
  30.3 4.2 %collective-permute-start.4 = (f32[2,2,8,128]{3,2,1,0:T(8,128)S(1)}, f32[2,2,8,128]{3,2,1,0:T(8,128)S(1)}, u32[]{:S(2)}, u32[]{:S(2)}) collective-permute-start(f32[2,2,8,128]{3,2,1,0:T(8,128)S(1)} %pad_maximum_fusion.p0_ref), channel_id=1, source_target_pairs={{0,2},{1,3},{2,0},{3,1},{4,6},{5,7},{6,4},{7,5},{8,10},{9,11},{10,... | collective-permute-start | bytes 49160 | tf_op jit(solution)/shard_map/ppermute | solution.py:313
  33.1 3.8 %collective-permute-start.3 = (f32[2,2,8,128]{3,2,1,0:T(8,128)S(1)}, f32[2,2,8,128]{3,2,1,0:T(8,128)S(1)}, u32[]{:S(2)}, u32[]{:S(2)}) collective-permute-start(f32[2,2,8,128]{3,2,1,0:T(8,128)S(1)} %pad_maximum_fusion.p0_ref), channel_id=1, source_target_pairs={{0,3},{1,2},{2,1},{3,0},{4,7},{5,6},{6,5},{7,4},{8,11},{9,10},{10,... | collective-permute-start | bytes 49160 | tf_op jit(solution)/shard_map/ppermute | solution.py:313
  34.0 2.9 %collective-permute-start.2 = (f32[2,2,8,128]{3,2,1,0:T(8,128)S(1)}, f32[2,2,8,128]{3,2,1,0:T(8,128)S(1)}, u32[]{:S(2)}, u32[]{:S(2)}) collective-permute-start(f32[2,2,8,128]{3,2,1,0:T(8,128)S(1)} %pad_maximum_fusion.p0_ref), channel_id=1, source_target_pairs={{0,1},{1,0},{2,3},{3,2},{4,5},{5,4},{6,7},{7,6},{8,9},{9,8},{10,11... | collective-permute-start | bytes 49160 | tf_op jit(solution)/shard_map/ppermute | solution.py:313

commit v7 on v6

v7 whole, which is shorter than its diff:
```python
import functools
import math

import jax
import jax.numpy as jnp
from jax import lax
from jax.experimental import pallas as pl
from jax.experimental.pallas import tpu as pltpu
from jax.sharding import Mesh
from jax.sharding import PartitionSpec as P

SP = ("sp_0", "sp_1", "sp_2")
CHIPS = ("sp_0", "sp_1")
BLOCK = 128
LEAVING = 256
MIB = 1 << 20
VMEM = pl.BlockSpec(memory_space=pltpu.VMEM)
HBM = pl.BlockSpec(memory_space=pltpu.HBM)


def stacked_triangle():
    row = lax.broadcasted_iota(jnp.int32, (BLOCK, 2 * BLOCK), 0)
    col = lax.broadcasted_iota(jnp.int32, (BLOCK, 2 * BLOCK), 1)
    return (row >= col % BLOCK).astype(jnp.bfloat16)


def scan_sequence(total, b, rate, drive, tri_ref, kept_ref, sum_ref, lost_ref, carry_ref):
    length, channels = rate.shape[1:]
    to_log2 = math.log2(math.e) / total
    lost_in = jnp.zeros((1, channels), jnp.float32)
    carry = jnp.zeros((1, channels), jnp.float32)
    for k in range(length // BLOCK):
        at = pl.ds(k * BLOCK, BLOCK)
        rates = rate[b, at, :]
        lost = to_log2 * jnp.dot(tri_ref[:, :BLOCK], rates.astype(jnp.bfloat16), preferred_element_type=jnp.float32)
        kept_ref[b, at, :] = jnp.exp2(-lost)
        drives = drive[b, at, :]
        grown = (jnp.exp2(lost) - 1.0).astype(jnp.bfloat16) * drives
        sums = jnp.dot(tri_ref[...], jnp.concatenate([drives, grown], axis=0), preferred_element_type=jnp.float32)
        sum_ref[b, at, :] = sums
        lost_ref[b, k : k + 1, :] = lost_in
        carry_ref[b, k : k + 1, :] = carry
        carry = carry + jnp.exp2(lost_in) * sums[BLOCK - 1 :, :]
        whole = jnp.sum(rates.reshape(BLOCK // 8, 8, channels), axis=0)
        lost_in = lost_in + to_log2 * jnp.sum(whole, axis=0, keepdims=True)
    return lost_in, carry


def other_kernel(
    total, rate_hbm, drive_hbm, kept_ref, sum_ref, lost_ref, carry_ref, rate, drive, other_ref, tri_ref, rate_sem, drive_sem
):
    batch = rate.shape[0]
    half, core = batch // 2, lax.axis_index("sp_2")
    sets = ((rate_hbm, rate, rate_sem), (drive_hbm, drive, drive_sem))

    def copies(n):
        b = jnp.where(n < half, (1 - core) * half + n, core * half + n - half)
        return [pltpu.make_async_copy(hbm.at[b], vmem.at[b], sems.at[n]) for hbm, vmem, sems in sets]

    for n in range(batch):
        for copy in copies(n):
            copy.start()
    tri_ref[...] = stacked_triangle()

    def one_sequence(n, _):
        for copy in copies(n):
            copy.wait()
        b = (1 - core) * half + n
        lost, carry = scan_sequence(total, b, rate, drive, tri_ref, kept_ref, sum_ref, lost_ref, carry_ref)
        other_ref[n, 0:1, :] = lost
        other_ref[n, 1:2, :] = carry
        return 0

    lax.fori_loop(0, half, one_sequence, 0)
    for n in range(half, batch):
        for copy in copies(n):
            copy.wait()


def scan_other(decay_rate, drive_in, total):
    batch, length, channels = decay_rate.shape
    big = jax.ShapeDtypeStruct(decay_rate.shape, jnp.float32)
    blocks = jax.ShapeDtypeStruct((batch, length // BLOCK, channels), jnp.float32)
    pair = jax.ShapeDtypeStruct((batch // 2, 2, channels), jnp.float32)
    return pl.pallas_call(
        functools.partial(other_kernel, total),
        out_shape=(big, big, blocks, blocks, big, jax.ShapeDtypeStruct(drive_in.shape, drive_in.dtype), pair),
        in_specs=[HBM] * 2,
        out_specs=(VMEM,) * 7,
        scratch_shapes=[
            pltpu.VMEM((BLOCK, 2 * BLOCK), jnp.bfloat16),
            pltpu.SemaphoreType.DMA((batch,)),
            pltpu.SemaphoreType.DMA((batch,)),
        ],
        compiler_params=pltpu.CompilerParams(vmem_limit_bytes=20 * MIB),
        cost_estimate=pl.CostEstimate(flops=1_000_000_000, bytes_accessed=6 * MIB, transcendentals=MIB),
        name="scan_other",
    )(decay_rate, drive_in)


def mine_kernel(
    total,
    rate,
    drive,
    gate_hbm,
    kept_in,
    sum_in,
    lost_in,
    carry_in,
    kept_ref,
    sum_ref,
    lost_ref,
    carry_ref,
    gate_ref,
    mine_ref,
    tri_ref,
    gate_sem,
):
    batch = rate.shape[0]
    half, core = batch // 2, lax.axis_index("sp_2")
    gates = [pltpu.make_async_copy(gate_hbm.at[b], gate_ref.at[b], gate_sem.at[b]) for b in range(batch)]
    for copy in gates:
        copy.start()
    tri_ref[...] = stacked_triangle()

    def one_sequence(n, _):
        b = core * half + n
        lost, carry = scan_sequence(total, b, rate, drive, tri_ref, kept_ref, sum_ref, lost_ref, carry_ref)
        mine_ref[n, 0:1, :] = lost
        mine_ref[n, 1:2, :] = carry
        return 0

    lax.fori_loop(0, half, one_sequence, 0)
    for copy in gates:
        copy.wait()


def scan_mine(rate, drive, gate_in, local, total):
    batch, length, channels = rate.shape
    pair = jax.ShapeDtypeStruct((batch // 2, 2, channels), jnp.float32)
    return pl.pallas_call(
        functools.partial(mine_kernel, total),
        out_shape=(
            *(jax.ShapeDtypeStruct(array.shape, array.dtype) for array in local),
            jax.ShapeDtypeStruct(gate_in.shape, gate_in.dtype),
            pair,
        ),
        in_specs=[VMEM, VMEM, HBM] + [VMEM] * 4,
        out_specs=(VMEM,) * 6,
        scratch_shapes=[pltpu.VMEM((BLOCK, 2 * BLOCK), jnp.bfloat16), pltpu.SemaphoreType.DMA((batch,))],
        input_output_aliases={3: 0, 4: 1, 5: 2, 6: 3},
        compiler_params=pltpu.CompilerParams(vmem_limit_bytes=24 * MIB),
        cost_estimate=pl.CostEstimate(flops=1_000_000_000, bytes_accessed=2 * MIB, transcendentals=MIB),
        name="scan_mine",
    )(rate, drive, gate_in, *local)


def open_kernel(kept_ref, gate_ref, factor_ref):
    batch, length, channels = kept_ref.shape

    def one_piece(n, _):
        at = pl.ds(pl.multiple_of(n * BLOCK, BLOCK), BLOCK)
        for b in range(batch):
            opened = jnp.tanh((0.5 * gate_ref[b, at, :]).astype(jnp.float32)) + 1.0
            factor_ref[b, at, :] = kept_ref[b, at, :] * opened
        return 0

    lax.fori_loop(0, length // BLOCK, one_piece, 0)


def open_gate(kept, gate):
    return pl.pallas_call(
        open_kernel,
        out_shape=jax.ShapeDtypeStruct(kept.shape, jnp.float32),
        in_specs=[VMEM] * 2,
        out_specs=VMEM,
        input_output_aliases={0: 0},
        compiler_params=pltpu.CompilerParams(vmem_limit_bytes=12 * MIB),
        cost_estimate=pl.CostEstimate(flops=8_000_000, bytes_accessed=10 * MIB, transcendentals=MIB),
        name="open_gate",
    )(kept, gate)


def meet_kernel(mine_ref, got_ref, first_ref, every_ref):
    first_core = lax.axis_index("sp_2") == 0
    for p in range(mine_ref.shape[0]):
        mine, got = mine_ref[p], got_ref[p]
        first = jnp.where(first_core, mine, got)
        second = jnp.where(first_core, got, mine)
        first_ref[p] = first
        lost = first[0:1] + second[0:1]
        sums = first[1:2] + jnp.exp2(first[0:1]) * second[1:2]
        for j in range(every_ref.shape[0]):
            every_ref[j, p, 0:1, :] = lost
            every_ref[j, p, 1:2, :] = sums


def meet(mine, got, chips):
    return pl.pallas_call(
        meet_kernel,
        out_shape=(
            jax.ShapeDtypeStruct(mine.shape, jnp.float32),
            jax.ShapeDtypeStruct((chips,) + mine.shape, jnp.float32),
        ),
        in_specs=[VMEM] * 2,
        out_specs=(VMEM,) * 2,
        compiler_params=pltpu.CompilerParams(vmem_limit_bytes=2 * MIB),
        name="meet",
    )(mine, got)


def enter_kernel(every_ref, first_ref, mine_ref, other_ref):
    chips, pairs, _, channels = every_ref.shape
    place = lax.axis_index(CHIPS)
    first_core = lax.axis_index("sp_2") == 0
    for p in range(pairs):
        state = jnp.zeros((1, channels), jnp.float32)
        for j in range(chips):
            kept = jnp.exp2(-jnp.where(j < place, every_ref[j, p, 0:1, :], 0.0))
            state = kept * (state + jnp.where(j < place, every_ref[j, p, 1:2, :], 0.0))
        after = jnp.exp2(-first_ref[p, 0:1, :]) * (state + first_ref[p, 1:2, :])
        mine_ref[p : p + 1, :] = jnp.where(first_core, state, after)
        other_ref[p : p + 1, :] = jnp.where(first_core, after, state)


def entering(every, first):
    chips, pairs, _, channels = every.shape
    out = jax.ShapeDtypeStruct((pairs, channels), jnp.float32)
    return pl.pallas_call(
        enter_kernel,
        out_shape=(out, out),
        in_specs=[VMEM] * 2,
        out_specs=(VMEM,) * 2,
        compiler_params=pltpu.CompilerParams(vmem_limit_bytes=2 * MIB),
        name="entering",
    )(every, first)


def gate_kernel(mine, factor_ref, sum_ref, lost_ref, carry_ref, enter_ref, gated_ref, power_ref):
    half, length, channels = gated_ref.shape
    lane = lax.broadcasted_iota(jnp.int32, (8, length // 8), 1)
    core = lax.axis_index("sp_2")
    start = half * (core if mine else 1 - core)

    for p in range(half):
        b = start + p
        enter = jnp.exp2(-lost_ref[b]) * (enter_ref[pl.ds(p, 1), :] + carry_ref[b])
        power = jnp.zeros((8, length // 8), jnp.float32)
        for k in range(length // BLOCK):
            state = jnp.broadcast_to(enter[k : k + 1, :], (8, channels))
            for j in range(k * BLOCK // 8, (k + 1) * BLOCK // 8):
                at = pl.ds(8 * j, 8)
                gated = factor_ref[b, at, :] * (sum_ref[b, at, :] + state)
                gated_ref[p, at, :] = gated
                power = jnp.where(lane == j, jnp.sum(gated * gated, axis=-1, keepdims=True), power)
        power_ref[p] = power


def gate_and_square(mine, local, enter, name):
    batch, length, channels = local[0].shape
    half = batch // 2
    return pl.pallas_call(
        functools.partial(gate_kernel, mine),
        out_shape=(
            jax.ShapeDtypeStruct((half, length, channels), jnp.float32),
            jax.ShapeDtypeStruct((half, 8, length // 8), jnp.float32),
        ),
        in_specs=[VMEM] * 5,
        out_specs=(VMEM, VMEM),
        compiler_params=pltpu.CompilerParams(vmem_limit_bytes=14 * MIB),
        cost_estimate=pl.CostEstimate(flops=4_000_000, bytes_accessed=6 * MIB, transcendentals=0),
        name=name,
    )(*local, enter)


def scale_kernel(middle, width, mine_ref, got_ref, p0_ref, p1_ref, p2_ref, p3_ref, gain_ref, out_hbm, out, sem):
    half, length, channels = mine_ref.shape
    core = lax.axis_index("sp_2")
    which = [(h, p) for h in range(2) for p in range(half)]

    def copy(h, p, i):
        b = half * (core if h == 0 else 1 - core) + p
        at = pl.ds(i * LEAVING, LEAVING)
        return pltpu.make_async_copy(out.at[h, p, at, :], out_hbm.at[b, at, :], sem.at[(h * half + p) * (length // LEAVING) + i])

    lane = lax.broadcasted_iota(jnp.int32, (8, length // 8), 1)
    gain = jnp.broadcast_to(gain_ref[...], (8, channels))
    scales = []
    for h, p in which:
        power = (p0_ref[h, p] + p1_ref[h, p]) + (p2_ref[h, p] + p3_ref[h, p])
        scales.append(middle * lax.rsqrt(power * (middle * middle / width) + 1e-06))
    for i in range(length // LEAVING):
        for j in range(i * LEAVING // 16, (i + 1) * LEAVING // 16):
            columns = [lane == 2 * j + k for k in range(2)]
            for (h, p), scale in zip(which, scales):
                gated_ref = (mine_ref, got_ref)[h]
                parts = []
                for k, column in enumerate(columns):
                    rows = jnp.sum(jnp.where(column, scale, 0.0), axis=-1, keepdims=True)
                    parts.append(gated_ref[p, pl.ds(16 * j + 8 * k, 8), :] * rows * gain)
                out[h, p, pl.ds(16 * j, 16), :] = jnp.concatenate(parts, axis=0).astype(jnp.bfloat16)
        for h, p in which:
            copy(h, p, i).start()
    for i in range(length // LEAVING):
        for h, p in which:
            copy(h, p, i).wait()


def scale(mine, got, powers, gain, middle, width):
    half, length, channels = mine.shape
    return pl.pallas_call(
        functools.partial(scale_kernel, middle, width),
        out_shape=jax.ShapeDtypeStruct((2 * half, length, channels), jnp.bfloat16),
        in_specs=[VMEM] * 7,
        out_specs=HBM,
        scratch_shapes=[pltpu.VMEM((2,) + mine.shape, jnp.bfloat16), pltpu.SemaphoreType.DMA((2 * half * length // LEAVING,))],
        compiler_params=pltpu.CompilerParams(vmem_limit_bytes=8 * MIB),
        cost_estimate=pl.CostEstimate(flops=8_000_000, bytes_accessed=6 * MIB, transcendentals=0),
        name="scale",
    )(mine, got, *powers, gain.reshape(1, channels))


def shards(decay_rate, drive_in, gate_in, norm_gain):
    total = decay_rate.shape[1] * lax.axis_size(SP)
    parts = lax.axis_size("tp")
    width = decay_rate.shape[2] * parts
    swap = [(0, 1), (1, 0)]
    decay_rate, drive_in, gate_in = (
        pltpu.with_memory_space_constraint(array, pltpu.HBM) for array in (decay_rate, drive_in, gate_in)
    )
    *local, rate, drive, other = scan_other(decay_rate, drive_in, total)
    got = lax.ppermute(other, "sp_2", swap)
    kept, sums, lost, carry, gate, mine = scan_mine(rate, drive, gate_in, local, total)
    first, every = meet(mine, got, lax.axis_size(CHIPS))
    every = lax.all_to_all(every, CHIPS, 0, 0)
    every, kept, gate, norm_gain = lax.optimization_barrier((every, kept, gate, norm_gain))
    mine, other = entering(every, first)
    got = lax.ppermute(other, "sp_2", swap)
    factor = open_gate(kept, gate)
    local = (factor, sums, lost, carry)
    gated_mine, power_mine = gate_and_square(True, local, mine, "gate_mine")
    gated_got, power_got = gate_and_square(False, local, got, "gate_got")
    power = jnp.stack([power_mine, power_got])
    powers = [power] + [lax.ppermute(power, "tp", [(i, i ^ k) for i in range(parts)]) for k in (1, 3, 2)]
    return scale(gated_mine, gated_got, powers, norm_gain, 0.5 * total**-0.5, width)


def solution(mesh):
    torus = Mesh(mesh.devices.reshape(8, 4, 2, mesh.shape["tp"]), ("sp_0", "sp_1", "sp_2", "tp"))
    in_specs = (P(None, SP, "tp"), P(None, SP, "tp"), P(None, SP, "tp"), P("tp"))
    out_specs = P(None, SP, "tp")
    return jax.shard_map(shards, mesh=torus, in_specs=in_specs, out_specs=out_specs, check_vma=False)
```

time: 38.7 us -> 38.6 us (level)
  starting transfers between devices: 9.16 us -> 8.49 us
  blocking collectives: 18.6 us -> 19.2 us
  waiting for transfers between devices: 3.42 us -> 2.94 us
  Pallas kernels: 7.33 us -> 7.73 us
    ppermute x2, starting transfers between devices: 5.46 us -> 4.8 us  [shards(): got = lax.ppermute(other, 'sp_2', swap)]
    all_to_all x1, blocking collectives: 18.6 us -> 19.2 us  [shards(): every = lax.all_to_all(every, CHIPS, 0, 0)]
    pallas_call x1 -> x2, Pallas kernels: 3.91 us -> 4.4 us  [the longest x1 2.85 us: scan_other(): pl.pallas_call(functools.partial(other_kernel, total), out_shape=(big, bi...]
    ppermute x2, waiting for transfers between devices: 0.49 us -> 0.01 us  [shards(): got = lax.ppermute(other, 'sp_2', swap)]
  transfers between devices with their start and end apart: 5 -> 5, of which waited for: 4 -> 2; matrix products, arithmetic and copies ran while one was open for 0% -> 0% of each run, Pallas kernels for 3% -> 7%
where the time goes in v7:
time: 38.6 us; the launch traced here: 38.5 us
  blocking collectives  19.2 us (50%)
  starting transfers between devices  8.49 us (22%)
  Pallas kernels  7.73 us (20%)
  waiting for transfers between devices  2.94 us (8%)
    all_to_all x1, blocking collectives, shards(): every = lax.all_to_all(every, CHIPS, 0, 0)  19.2 us
    ppermute x2, starting transfers between devices, shards(): got = lax.ppermute(other, 'sp_2', swap)  4.8 us
    ppermute x3, starting transfers between devices, shards(): lax.ppermute(power, 'tp', [(i, i ^ k) for i in range(parts)])  3.69 us
    ppermute x3, waiting for transfers between devices, shards(): lax.ppermute(power, 'tp', [(i, i ^ k) for i in range(parts)])  2.94 us
    pallas_call x1, Pallas kernels, scan_other(): pl.pallas_call(functools.partial(other_kernel, total), out_shape=(big, bi...  2.85 us
    pallas_call x1, Pallas kernels, scale(): pl.pallas_call(functools.partial(scale_kernel, middle, width), out_shape=...  1.66 us
    pallas_call x1, Pallas kernels, scan_mine(): pl.pallas_call(functools.partial(mine_kernel, total), out_shape=(*(jax.Sh...  1.55 us
    pallas_call x2, Pallas kernels, gate_and_square(): pl.pallas_call(functools.partial(gate_kernel, mine), out_shape=(jax.Shape...  0.81 us
  transfers between devices with their start and end apart: 5, of which 2 were waited for; matrix products, arithmetic and copies ran while one was open for 0% of the time, Pallas kernels for 7%

profile of v7, /device:TPU:1, one launch (start us, length us, event | category | flops | bytes accessed | tf_op | source)
XLA Modules:
  0.0 38.5 jit_solution(16908107903643722442)
XLA Ops:
  0.0 2.8 %scan_other.1 = (f32[4,1024,256]{2,1,0:T(8,128)S(1)}, f32[4,1024,256]{2,1,0:T(8,128)S(1)}, f32[4,8,256]{2,1,0:T(8,128)S(1)}, f32[4,8,256]{2,1,0:T(8,128)S(1)}, f...) custom-call(f32[4,1024,256]{2,1,0:T(8,128)} %rate_hbm.1, ...), custom_call_target="tpu_custom_call" | custom-call | flops 1000000000 | bytes 6291456 | tf_op jit(solution)/shard_map/scan_other/pallas_call | solution.py:85
  2.9 3.3 %collective-permute-start = (f32[2,2,256]{2,1,0:T(2,128)S(1)}, f32[2,2,256]{2,1,0:T(2,128)S(1)}, u32[]{:S(2)}, u32[]{:S(2)}) collective-permute-start(f32[2,2,256]{2,1,0:T(2,128)S(1)} %get-tuple-element.37), channel_id=1, source_target_pairs={{0,4},{4,0},{1,5},{5,1},{2,6},{6,2},{3,7},{7,3},{8,12},{12,8},{9,1... | collective-permute-start | bytes 12296 | tf_op jit(solution)/shard_map/ppermute | solution.py:332
  6.1 1.6 %scan_mine.1 = (f32[4,1024,256]{2,1,0:T(8,128)S(1)}, f32[4,1024,256]{2,1,0:T(8,128)S(1)}, f32[4,8,256]{2,1,0:T(8,128)S(1)}, f32[4,8,256]{2,1,0:T(8,128)S(1)}, bf...) custom-call(f32[4,1024,256]{2,1,0:T(8,128)S(1)} %get-tuple-element.3, ...), custom_call_target="tpu_custom_call", output_to_operand_aliasing={{0}: (3, {}), {1}: (4, {}), {2}: (5, {}), {3}: (6, {})} | custom-call | flops 1000000000 | bytes 2097152 | tf_op jit(solution)/shard_map/scan_mine/pallas_call | solution.py:141
  7.7 0.0 collective-permute-done.got_ref
  7.7 0.1 meet.1
  7.8 19.2 %all_to_all.5.every_ref = f32[32,2,2,256]{3,2,1,0:T(2,128)S(1)} all-to-all(f32[32,2,2,256]{3,2,1,0:T(2,128)S(1)} %get-tuple-element.38), channel_id=1, replica_groups=mesh['sp_0'=8,'sp_1'=4,'sp_2'=2,'tp'=4] {'sp_0','sp_1'}, dimensions={0} | all-to-all | bytes 262144 | tf_op jit(solution)/shard_map/all_to_all | solution.py:335
  27.0 0.1 entering.1
  27.1 1.5 %collective-permute-start.1 = (f32[2,256]{1,0:T(2,128)S(1)}, f32[2,256]{1,0:T(2,128)S(1)}, u32[]{:S(2)}, u32[]{:S(2)}) collective-permute-start(f32[2,256]{1,0:T(2,128)S(1)} %get-tuple-element.50), channel_id=1, source_target_pairs={{0,4},{4,0},{1,5},{5,1},{2,6},{6,2},{3,7},{7,3},{8,12},{12,8},{9,1... | collective-permute-start | bytes 6152 | tf_op jit(solution)/shard_map/ppermute | solution.py:338
  28.6 0.7 %open_gate.1.factor_ref = f32[4,1024,256]{2,1,0:T(8,128)S(1)} custom-call(f32[4,1024,256]{2,1,0:T(8,128)S(1)} %get-tuple-element.41.kept_ref, bf16[4,1024,256]{2,1,0:T(8,128)(2,1)S(1)} %get-tuple-element.42.gate_ref), custom_call_target="tpu_custom_call", output_to_operand_aliasing={{}: (0, {})} | custom-call | flops 8000000 | bytes 10485760 | tf_op jit(solution)/shard_map/open_gate/pallas_call | solution.py:172
  29.3 0.4 %gate_mine.1 = (f32[2,1024,256]{2,1,0:T(8,128)S(1)}, f32[2,8,128]{2,1,0:T(8,128)S(1)}) custom-call(f32[4,1024,256]{2,1,0:T(8,128)S(1)} %open_gate.1.factor_ref, f32[4,1024,256]{2,1,0:T(8,128)S(1)} %get-tuple-element.43.sum_ref, f32[4,8,256]{2,1,0:T(8,128)S(1)} %get-tuple-element.44.lost_ref, f32[4,8,256]{2,1,0:T(8,128)S(1)} %get-tuple-element.45.carry_ref, ...), custom_call_target="tpu_custom_call" | custom-call | flops 4000000 | bytes 6291456 | tf_op jit(solution)/shard_map/gate_mine/pallas_call | solution.py:262
  29.7 0.0 copy-start
  29.7 0.0 collective-permute-done.1.enter_ref
  29.7 0.4 %gate_got.1 = (f32[2,1024,256]{2,1,0:T(8,128)S(1)}, f32[2,8,128]{2,1,0:T(8,128)S(1)}) custom-call(f32[4,1024,256]{2,1,0:T(8,128)S(1)} %open_gate.1.factor_ref, f32[4,1024,256]{2,1,0:T(8,128)S(1)} %get-tuple-element.43.sum_ref, f32[4,8,256]{2,1,0:T(8,128)S(1)} %get-tuple-element.44.lost_ref, f32[4,8,256]{2,1,0:T(8,128)S(1)} %get-tuple-element.45.carry_ref, ...), custom_call_target="tpu_custom_call" | custom-call | flops 4000000 | bytes 6291456 | tf_op jit(solution)/shard_map/gate_got/pallas_call | solution.py:262
  30.2 2.8 %collective-permute-start.4 = (f32[2,2,8,128]{3,2,1,0:T(8,128)S(1)}, f32[2,2,8,128]{3,2,1,0:T(8,128)S(1)}, u32[]{:S(2)}, u32[]{:S(2)}) collective-permute-start(f32[2,2,8,128]{3,2,1,0:T(8,128)S(1)} %pad_maximum_fusion.p0_ref), channel_id=1, source_target_pairs={{0,2},{1,3},{2,0},{3,1},{4,6},{5,7},{6,4},{7,5},{8,10},{9,11},{10,... | collective-permute-start | bytes 49160 | tf_op jit(solution)/shard_map/ppermute | solution.py:344
  33.0 0.9 %collective-permute-start.3 = (f32[2,2,8,128]{3,2,1,0:T(8,128)S(1)}, f32[2,2,8,128]{3,2,1,0:T(8,128)S(1)}, u32[]{:S(2)}, u32[]{:S(2)}) collective-permute-start(f32[2,2,8,128]{3,2,1,0:T(8,128)S(1)} %pad_maximum_fusion.p0_ref), channel_id=1, source_target_pairs={{0,3},{1,2},{2,1},{3,0},{4,7},{5,6},{6,5},{7,4},{8,11},{9,10},{10,... | collective-permute-start | bytes 49160 | tf_op jit(solution)/shard_map/ppermute | solution.py:344
  33.9 0.0 collective-permute-start.2
  33.9 0.5 %collective-permute-done.4.p3_ref = f32[2,2,8,128]{3,2,1,0:T(8,128)S(1)} collective-permute-done((f32[2,2,8,128]{3,2,1,0:T(8,128)S(1)}, f32[2,2,8,128]{3,2,1,0:T(8,128)S(1)}, u32[]{:S(2)}, u32[]{:S(2)}) %collective-permute-start.4) | collective-permute-done | bytes 16416 | tf_op jit(solution)/shard_map/ppermute | solution.py:344
  34.3 2.5 %collective-permute-done.3.p2_ref = f32[2,2,8,128]{3,2,1,0:T(8,128)S(1)} collective-permute-done((f32[2,2,8,128]{3,2,1,0:T(8,128)S(1)}, f32[2,2,8,128]{3,2,1,0:T(8,128)S(1)}, u32[]{:S(2)}, u32[]{:S(2)}) %collective-permute-start.3) | collective-permute-done | bytes 16416 | tf_op jit(solution)/shard_map/ppermute | solution.py:344
  36.8 0.0 collective-permute-done.2.p1_ref
  36.8 0.0 copy-done
  36.8 1.7 %scale.1 = bf16[4,1024,256]{2,1,0:T(8,128)(2,1)} custom-call(f32[2,1024,256]{2,1,0:T(8,128)S(1)} %get-tuple-element.49.mine_ref, f32[2,1024,256]{2,1,0:T(8,128)S(1)} %get-tuple-element.51.got_ref, f32[2,2,8,128]{3,2,1,0:T(8,128)S(1)} %pad_maximum_fusion.p0_ref, f32[2,2,8,128]{3,2,1,0:T(8,128)S(1)} %collective-permute-done.2.p1_ref, ...), custom_call_target="tpu_custom_call" | custom-call | flops 8000000 | bytes 6291456 | tf_op jit(solution)/shard_map/scale/pallas_call | solution.py:311
  (1 shorter events, 0.0 us)
Async XLA Ops:
  2.9 4.8 %collective-permute-start = (f32[2,2,256]{2,1,0:T(2,128)S(1)}, f32[2,2,256]{2,1,0:T(2,128)S(1)}, u32[]{:S(2)}, u32[]{:S(2)}) collective-permute-start(f32[2,2,256]{2,1,0:T(2,128)S(1)} %get-tuple-element.37), channel_id=1, source_target_pairs={{0,4},{4,0},{1,5},{5,1},{2,6},{6,2},{3,7},{7,3},{8,12},{12,8},{9,1... | collective-permute-start | bytes 12296 | tf_op jit(solution)/shard_map/ppermute | solution.py:332
  27.1 2.6 %collective-permute-start.1 = (f32[2,256]{1,0:T(2,128)S(1)}, f32[2,256]{1,0:T(2,128)S(1)}, u32[]{:S(2)}, u32[]{:S(2)}) collective-permute-start(f32[2,256]{1,0:T(2,128)S(1)} %get-tuple-element.50), channel_id=1, source_target_pairs={{0,4},{4,0},{1,5},{5,1},{2,6},{6,2},{3,7},{7,3},{8,12},{12,8},{9,1... | collective-permute-start | bytes 6152 | tf_op jit(solution)/shard_map/ppermute | solution.py:338
  29.7 7.1 %copy-start = (f32[256]{0:T(256)S(1)}, f32[256]{0:T(256)}, u32[]{:S(2)}) copy-start(f32[256]{0:T(256)} %param.7) | copy-start | bytes 3076
  30.2 4.2 %collective-permute-start.4 = (f32[2,2,8,128]{3,2,1,0:T(8,128)S(1)}, f32[2,2,8,128]{3,2,1,0:T(8,128)S(1)}, u32[]{:S(2)}, u32[]{:S(2)}) collective-permute-start(f32[2,2,8,128]{3,2,1,0:T(8,128)S(1)} %pad_maximum_fusion.p0_ref), channel_id=1, source_target_pairs={{0,2},{1,3},{2,0},{3,1},{4,6},{5,7},{6,4},{7,5},{8,10},{9,11},{10,... | collective-permute-start | bytes 49160 | tf_op jit(solution)/shard_map/ppermute | solution.py:344
  33.0 3.8 %collective-permute-start.3 = (f32[2,2,8,128]{3,2,1,0:T(8,128)S(1)}, f32[2,2,8,128]{3,2,1,0:T(8,128)S(1)}, u32[]{:S(2)}, u32[]{:S(2)}) collective-permute-start(f32[2,2,8,128]{3,2,1,0:T(8,128)S(1)} %pad_maximum_fusion.p0_ref), channel_id=1, source_target_pairs={{0,3},{1,2},{2,1},{3,0},{4,7},{5,6},{6,5},{7,4},{8,11},{9,10},{10,... | collective-permute-start | bytes 49160 | tf_op jit(solution)/shard_map/ppermute | solution.py:344
  33.9 2.9 %collective-permute-start.2 = (f32[2,2,8,128]{3,2,1,0:T(8,128)S(1)}, f32[2,2,8,128]{3,2,1,0:T(8,128)S(1)}, u32[]{:S(2)}, u32[]{:S(2)}) collective-permute-start(f32[2,2,8,128]{3,2,1,0:T(8,128)S(1)} %pad_maximum_fusion.p0_ref), channel_id=1, source_target_pairs={{0,1},{1,0},{2,3},{3,2},{4,5},{5,4},{6,7},{7,6},{8,9},{9,8},{10,11... | collective-permute-start | bytes 49160 | tf_op jit(solution)/shard_map/ppermute | solution.py:344

commit v8 on v7

--- a/solution.py
+++ b/solution.py
@@ -155,7 +155,7 @@
     )(rate, drive, gate_in, *local)
 
 
-def open_kernel(kept_ref, gate_ref, factor_ref):
+def open_kernel(core, kept_ref, gate_ref, factor_ref):
     batch, length, channels = kept_ref.shape
 
     def one_piece(n, _):
@@ -165,19 +165,21 @@
             factor_ref[b, at, :] = kept_ref[b, at, :] * opened
         return 0
 
-    lax.fori_loop(0, length // BLOCK, one_piece, 0)
-
-
-def open_gate(kept, gate):
-    return pl.pallas_call(
-        open_kernel,
+    @pl.when(lax.axis_index("sp_2") == core)
+    def _():
+        lax.fori_loop(0, length // BLOCK, one_piece, 0)
+
+
+def open_gate(core, kept, gate):
+    return pl.pallas_call(
+        functools.partial(open_kernel, core),
         out_shape=jax.ShapeDtypeStruct(kept.shape, jnp.float32),
         in_specs=[VMEM] * 2,
         out_specs=VMEM,
         input_output_aliases={0: 0},
         compiler_params=pltpu.CompilerParams(vmem_limit_bytes=12 * MIB),
         cost_estimate=pl.CostEstimate(flops=8_000_000, bytes_accessed=10 * MIB, transcendentals=MIB),
-        name="open_gate",
+        name=f"open_gate_{core}",
     )(kept, gate)
 
 
@@ -335,8 +337,10 @@
     every = lax.all_to_all(every, CHIPS, 0, 0)
     every, kept, gate, norm_gain = lax.optimization_barrier((every, kept, gate, norm_gain))
     mine, other = entering(every, first)
+    kept = open_gate(1, kept, gate)
+    other, kept = lax.optimization_barrier((other, kept))
     got = lax.ppermute(other, "sp_2", swap)
-    factor = open_gate(kept, gate)
+    factor = open_gate(0, kept, gate)
     local = (factor, sums, lost, carry)
     gated_mine, power_mine = gate_and_square(True, local, mine, "gate_mine")
     gated_got, power_got = gate_and_square(False, local, got, "gate_got")

time: 38.6 us -> 38.3 us (level)
  starting transfers between devices: 8.49 us -> 7.82 us
  waiting for transfers between devices: 2.94 us -> 3.36 us
    ppermute x2, starting transfers between devices: 4.8 us -> 4.12 us  [shards(): got = lax.ppermute(other, 'sp_2', swap)]
    ppermute x2, waiting for transfers between devices: 0.01 us -> 0.42 us  [shards(): got = lax.ppermute(other, 'sp_2', swap)]
  transfers between devices with their start and end apart: 5 -> 5, of which waited for: 2 -> 3; matrix products, arithmetic and copies ran while one was open for 0% -> 0% of each run, Pallas kernels for 7% -> 5%
where the time goes in v8:
time: 38.3 us; the launch traced here: 38.2 us
  blocking collectives  19.2 us (50%)
  starting transfers between devices  7.82 us (20%)
  Pallas kernels  7.71 us (20%)
  waiting for transfers between devices  3.36 us (9%)
    all_to_all x1, blocking collectives, shards(): every = lax.all_to_all(every, CHIPS, 0, 0)  19.2 us
    ppermute x2, starting transfers between devices, shards(): got = lax.ppermute(other, 'sp_2', swap)  4.12 us
    ppermute x3, starting transfers between devices, shards(): lax.ppermute(power, 'tp', [(i, i ^ k) for i in range(parts)])  3.69 us
    ppermute x3, waiting for transfers between devices, shards(): lax.ppermute(power, 'tp', [(i, i ^ k) for i in range(parts)])  2.94 us
    pallas_call x1, Pallas kernels, scan_other(): pl.pallas_call(functools.partial(other_kernel, total), out_shape=(big, bi...  2.85 us
    pallas_call x1, Pallas kernels, scale(): pl.pallas_call(functools.partial(scale_kernel, middle, width), out_shape=...  1.66 us
    pallas_call x1, Pallas kernels, scan_mine(): pl.pallas_call(functools.partial(mine_kernel, total), out_shape=(*(jax.Sh...  1.55 us
    pallas_call x2, Pallas kernels, gate_and_square(): pl.pallas_call(functools.partial(gate_kernel, mine), out_shape=(jax.Shape...  0.78 us
  transfers between devices with their start and end apart: 5, of which 3 were waited for; matrix products, arithmetic and copies ran while one was open for 0% of the time, Pallas kernels for 5%

profile of v8, /device:TPU:1, one launch (start us, length us, event | category | flops | bytes accessed | tf_op | source)
XLA Modules:
  0.0 38.2 jit_solution(8788311655381805382)
XLA Ops:
  0.0 2.8 %scan_other.1 = (f32[4,1024,256]{2,1,0:T(8,128)S(1)}, f32[4,1024,256]{2,1,0:T(8,128)S(1)}, f32[4,8,256]{2,1,0:T(8,128)S(1)}, f32[4,8,256]{2,1,0:T(8,128)S(1)}, f...) custom-call(f32[4,1024,256]{2,1,0:T(8,128)} %rate_hbm.1, ...), custom_call_target="tpu_custom_call" | custom-call | flops 1000000000 | bytes 6291456 | tf_op jit(solution)/shard_map/scan_other/pallas_call | solution.py:85
  2.9 3.3 %collective-permute-start = (f32[2,2,256]{2,1,0:T(2,128)S(1)}, f32[2,2,256]{2,1,0:T(2,128)S(1)}, u32[]{:S(2)}, u32[]{:S(2)}) collective-permute-start(f32[2,2,256]{2,1,0:T(2,128)S(1)} %get-tuple-element.39), channel_id=1, source_target_pairs={{0,4},{4,0},{1,5},{5,1},{2,6},{6,2},{3,7},{7,3},{8,12},{12,8},{9,1... | collective-permute-start | bytes 12296 | tf_op jit(solution)/shard_map/ppermute | solution.py:334
  6.1 1.6 %scan_mine.1 = (f32[4,1024,256]{2,1,0:T(8,128)S(1)}, f32[4,1024,256]{2,1,0:T(8,128)S(1)}, f32[4,8,256]{2,1,0:T(8,128)S(1)}, f32[4,8,256]{2,1,0:T(8,128)S(1)}, bf...) custom-call(f32[4,1024,256]{2,1,0:T(8,128)S(1)} %get-tuple-element.3, ...), custom_call_target="tpu_custom_call", output_to_operand_aliasing={{0}: (3, {}), {1}: (4, {}), {2}: (5, {}), {3}: (6, {})} | custom-call | flops 1000000000 | bytes 2097152 | tf_op jit(solution)/shard_map/scan_mine/pallas_call | solution.py:141
  7.7 0.0 collective-permute-done.got_ref
  7.7 0.1 meet.1
  7.8 19.2 %all_to_all.5.every_ref = f32[32,2,2,256]{3,2,1,0:T(2,128)S(1)} all-to-all(f32[32,2,2,256]{3,2,1,0:T(2,128)S(1)} %get-tuple-element.40), channel_id=1, replica_groups=mesh['sp_0'=8,'sp_1'=4,'sp_2'=2,'tp'=4] {'sp_0','sp_1'}, dimensions={0} | all-to-all | bytes 262144 | tf_op jit(solution)/shard_map/all_to_all | solution.py:337
  27.0 0.1 entering.1
  27.1 0.7 %open_gate_1.1.kept_ref = f32[4,1024,256]{2,1,0:T(8,128)S(1)} custom-call(f32[4,1024,256]{2,1,0:T(8,128)S(1)} %get-tuple-element.46.kept_ref, bf16[4,1024,256]{2,1,0:T(8,128)(2,1)S(1)} %get-tuple-element.47.gate_ref), custom_call_target="tpu_custom_call", output_to_operand_aliasing={{}: (0, {})} | custom-call | flops 8000000 | bytes 10485760 | tf_op jit(solution)/shard_map/open_gate_1/pallas_call | solution.py:174
  27.8 0.8 %collective-permute-start.1 = (f32[2,256]{1,0:T(2,128)S(1)}, f32[2,256]{1,0:T(2,128)S(1)}, u32[]{:S(2)}, u32[]{:S(2)}) collective-permute-start(f32[2,256]{1,0:T(2,128)S(1)} %get-tuple-element.54), channel_id=1, source_target_pairs={{0,4},{4,0},{1,5},{5,1},{2,6},{6,2},{3,7},{7,3},{8,12},{12,8},{9,1... | collective-permute-start | bytes 6152 | tf_op jit(solution)/shard_map/ppermute | solution.py:342
  28.7 0.4 %gate_mine.1 = (f32[2,1024,256]{2,1,0:T(8,128)S(1)}, f32[2,8,128]{2,1,0:T(8,128)S(1)}) custom-call(f32[4,1024,256]{2,1,0:T(8,128)S(1)} %open_gate_0.1.factor_ref, f32[4,1024,256]{2,1,0:T(8,128)S(1)} %get-tuple-element.49.sum_ref, f32[4,8,256]{2,1,0:T(8,128)S(1)} %get-tuple-element.50.lost_ref, f32[4,8,256]{2,1,0:T(8,128)S(1)} %get-tuple-element.51.carry_ref, ...), custom_call_target="tpu_custom_call" | custom-call | flops 4000000 | bytes 6291456 | tf_op jit(solution)/shard_map/gate_mine/pallas_call | solution.py:264
  29.0 0.0 copy-start
  29.1 0.4 %collective-permute-done.1.enter_ref = f32[2,256]{1,0:T(2,128)S(1)} collective-permute-done((f32[2,256]{1,0:T(2,128)S(1)}, f32[2,256]{1,0:T(2,128)S(1)}, u32[]{:S(2)}, u32[]{:S(2)}) %collective-permute-start.1) | collective-permute-done | bytes 2080 | tf_op jit(solution)/shard_map/ppermute | solution.py:342
  29.5 0.4 %gate_got.1 = (f32[2,1024,256]{2,1,0:T(8,128)S(1)}, f32[2,8,128]{2,1,0:T(8,128)S(1)}) custom-call(f32[4,1024,256]{2,1,0:T(8,128)S(1)} %open_gate_0.1.factor_ref, f32[4,1024,256]{2,1,0:T(8,128)S(1)} %get-tuple-element.49.sum_ref, f32[4,8,256]{2,1,0:T(8,128)S(1)} %get-tuple-element.50.lost_ref, f32[4,8,256]{2,1,0:T(8,128)S(1)} %get-tuple-element.51.carry_ref, ...), custom_call_target="tpu_custom_call" | custom-call | flops 4000000 | bytes 6291456 | tf_op jit(solution)/shard_map/gate_got/pallas_call | solution.py:264
  29.9 2.8 %collective-permute-start.4 = (f32[2,2,8,128]{3,2,1,0:T(8,128)S(1)}, f32[2,2,8,128]{3,2,1,0:T(8,128)S(1)}, u32[]{:S(2)}, u32[]{:S(2)}) collective-permute-start(f32[2,2,8,128]{3,2,1,0:T(8,128)S(1)} %pad_maximum_fusion.p0_ref), channel_id=1, source_target_pairs={{0,2},{1,3},{2,0},{3,1},{4,6},{5,7},{6,4},{7,5},{8,10},{9,11},{10,... | collective-permute-start | bytes 49160 | tf_op jit(solution)/shard_map/ppermute | solution.py:348
  32.7 0.9 %collective-permute-start.3 = (f32[2,2,8,128]{3,2,1,0:T(8,128)S(1)}, f32[2,2,8,128]{3,2,1,0:T(8,128)S(1)}, u32[]{:S(2)}, u32[]{:S(2)}) collective-permute-start(f32[2,2,8,128]{3,2,1,0:T(8,128)S(1)} %pad_maximum_fusion.p0_ref), channel_id=1, source_target_pairs={{0,3},{1,2},{2,1},{3,0},{4,7},{5,6},{6,5},{7,4},{8,11},{9,10},{10,... | collective-permute-start | bytes 49160 | tf_op jit(solution)/shard_map/ppermute | solution.py:348
  33.6 0.0 collective-permute-start.2
  33.6 0.5 %collective-permute-done.4.p3_ref = f32[2,2,8,128]{3,2,1,0:T(8,128)S(1)} collective-permute-done((f32[2,2,8,128]{3,2,1,0:T(8,128)S(1)}, f32[2,2,8,128]{3,2,1,0:T(8,128)S(1)}, u32[]{:S(2)}, u32[]{:S(2)}) %collective-permute-start.4) | collective-permute-done | bytes 16416 | tf_op jit(solution)/shard_map/ppermute | solution.py:348
  34.1 2.5 %collective-permute-done.3.p2_ref = f32[2,2,8,128]{3,2,1,0:T(8,128)S(1)} collective-permute-done((f32[2,2,8,128]{3,2,1,0:T(8,128)S(1)}, f32[2,2,8,128]{3,2,1,0:T(8,128)S(1)}, u32[]{:S(2)}, u32[]{:S(2)}) %collective-permute-start.3) | collective-permute-done | bytes 16416 | tf_op jit(solution)/shard_map/ppermute | solution.py:348
  36.5 0.0 collective-permute-done.2.p1_ref
  36.5 0.0 copy-done
  36.5 1.7 %scale.1 = bf16[4,1024,256]{2,1,0:T(8,128)(2,1)} custom-call(f32[2,1024,256]{2,1,0:T(8,128)S(1)} %get-tuple-element.53.mine_ref, f32[2,1024,256]{2,1,0:T(8,128)S(1)} %get-tuple-element.55.got_ref, f32[2,2,8,128]{3,2,1,0:T(8,128)S(1)} %pad_maximum_fusion.p0_ref, f32[2,2,8,128]{3,2,1,0:T(8,128)S(1)} %collective-permute-done.2.p1_ref, ...), custom_call_target="tpu_custom_call" | custom-call | flops 8000000 | bytes 6291456 | tf_op jit(solution)/shard_map/scale/pallas_call | solution.py:313
  (2 shorter events, 0.0 us)
Async XLA Ops:
  2.9 4.8 %collective-permute-start = (f32[2,2,256]{2,1,0:T(2,128)S(1)}, f32[2,2,256]{2,1,0:T(2,128)S(1)}, u32[]{:S(2)}, u32[]{:S(2)}) collective-permute-start(f32[2,2,256]{2,1,0:T(2,128)S(1)} %get-tuple-element.39), channel_id=1, source_target_pairs={{0,4},{4,0},{1,5},{5,1},{2,6},{6,2},{3,7},{7,3},{8,12},{12,8},{9,1... | collective-permute-start | bytes 12296 | tf_op jit(solution)/shard_map/ppermute | solution.py:334
  27.8 1.7 %collective-permute-start.1 = (f32[2,256]{1,0:T(2,128)S(1)}, f32[2,256]{1,0:T(2,128)S(1)}, u32[]{:S(2)}, u32[]{:S(2)}) collective-permute-start(f32[2,256]{1,0:T(2,128)S(1)} %get-tuple-element.54), channel_id=1, source_target_pairs={{0,4},{4,0},{1,5},{5,1},{2,6},{6,2},{3,7},{7,3},{8,12},{12,8},{9,1... | collective-permute-start | bytes 6152 | tf_op jit(solution)/shard_map/ppermute | solution.py:342
  29.0 7.5 %copy-start = (f32[256]{0:T(256)S(1)}, f32[256]{0:T(256)}, u32[]{:S(2)}) copy-start(f32[256]{0:T(256)} %param.7) | copy-start | bytes 3076
  29.9 4.2 %collective-permute-start.4 = (f32[2,2,8,128]{3,2,1,0:T(8,128)S(1)}, f32[2,2,8,128]{3,2,1,0:T(8,128)S(1)}, u32[]{:S(2)}, u32[]{:S(2)}) collective-permute-start(f32[2,2,8,128]{3,2,1,0:T(8,128)S(1)} %pad_maximum_fusion.p0_ref), channel_id=1, source_target_pairs={{0,2},{1,3},{2,0},{3,1},{4,6},{5,7},{6,4},{7,5},{8,10},{9,11},{10,... | collective-permute-start | bytes 49160 | tf_op jit(solution)/shard_map/ppermute | solution.py:348
  32.7 3.8 %collective-permute-start.3 = (f32[2,2,8,128]{3,2,1,0:T(8,128)S(1)}, f32[2,2,8,128]{3,2,1,0:T(8,128)S(1)}, u32[]{:S(2)}, u32[]{:S(2)}) collective-permute-start(f32[2,2,8,128]{3,2,1,0:T(8,128)S(1)} %pad_maximum_fusion.p0_ref), channel_id=1, source_target_pairs={{0,3},{1,2},{2,1},{3,0},{4,7},{5,6},{6,5},{7,4},{8,11},{9,10},{10,... | collective-permute-start | bytes 49160 | tf_op jit(solution)/shard_map/ppermute | solution.py:348
  33.6 2.9 %collective-permute-start.2 = (f32[2,2,8,128]{3,2,1,0:T(8,128)S(1)}, f32[2,2,8,128]{3,2,1,0:T(8,128)S(1)}, u32[]{:S(2)}, u32[]{:S(2)}) collective-permute-start(f32[2,2,8,128]{3,2,1,0:T(8,128)S(1)} %pad_maximum_fusion.p0_ref), channel_id=1, source_target_pairs={{0,1},{1,0},{2,3},{3,2},{4,5},{5,4},{6,7},{7,6},{8,9},{9,8},{10,11... | collective-permute-start | bytes 49160 | tf_op jit(solution)/shard_map/ppermute | solution.py:348
